TPU v7x, 32 devices: a 4x4x1 block of a 4x4x8 slice. The times are simulated.
32 devices in a mesh: dp: 1 (over z), cp: 32 (over y, x, core).
Axes of the slice: x: 4, y: 4, z: 1, core: 2. Of those that a mesh axis runs over, the one named last changes fastest.
The devices are a block of a 4x4x8 slice.
Arguments:
- x_in: bfloat16 [1, 8192, 8192], P('dp', 'cp')
- seg_ids: int32 [8192], P(('dp', 'cp'))
- positions: int32 [8192], P(('dp', 'cp'))
- attn_gain: bfloat16 [8192], replicated
- w_q: bfloat16 [8192, 1024], replicated
- w_k: bfloat16 [8192, 128], replicated
- w_v: bfloat16 [8192, 128], replicated
- w_o: bfloat16 [1024, 8192], replicated
- mlp_gain: bfloat16 [8192], replicated
- w_gate: bfloat16 [8192, 3584], replicated
- w_up: bfloat16 [8192, 3584], replicated
- w_down: bfloat16 [3584, 8192], replicated
Outputs:
- output 1: bfloat16 [1, 8192, 8192], P('dp', 'cp')
- output 2: bfloat16 [8192, 1, 128], P(('dp', 'cp'))
- output 3: bfloat16 [8192, 1, 128], P(('dp', 'cp'))
All inputs are finite; a program needn't handle non-finite values.
Results may differ from a plain program's by a relative error of at most 0.0112256.
Values are sent between devices in bfloat16 or wider.
A program may use at most 768 MiB of HBM per device.

v0:
```python
import jax
import jax.numpy as jnp
from jax import lax
from jax.sharding import PartitionSpec as P

HEAD_DIM = 128
ROPE_THETA = 500000.0
ROPE_FACTOR = 8.0
LOW_FREQ = 1.0
HIGH_FREQ = 4.0
ORIG_CTX = 8192.0
NORM_EPS = 1e-5
NEG_BIG = -1e30


def rope_freqs():
    exponent = jnp.arange(0, HEAD_DIM, 2).astype(jnp.float32) / HEAD_DIM
    inv_freq = 1.0 / (ROPE_THETA ** exponent)
    wavelen = 2.0 * jnp.pi / inv_freq
    smooth = jnp.clip((ORIG_CTX / wavelen - LOW_FREQ) / (HIGH_FREQ - LOW_FREQ), 0.0, 1.0)
    return (1.0 - smooth) * inv_freq / ROPE_FACTOR + smooth * inv_freq


def apply_rope(tensor, cos_t, sin_t):
    half = tensor.shape[-1] // 2
    first = tensor[..., :half]
    second = tensor[..., half:]
    return jnp.concatenate([first * cos_t - second * sin_t, second * cos_t + first * sin_t], axis=-1)


def rms_norm(tensor, gain):
    vec_f32 = tensor.astype(jnp.float32)
    inv_rms = lax.rsqrt(jnp.mean(vec_f32 * vec_f32, axis=-1, keepdims=True) + NORM_EPS)
    return (vec_f32 * inv_rms * gain.astype(jnp.float32)).astype(jnp.bfloat16)


def project_rows(rows, pos_rows, attn_gain, w_q, w_k, w_v):
    count = rows.shape[0]
    kv_heads = w_k.shape[1] // HEAD_DIM
    group_rep = w_q.shape[1] // w_k.shape[1]
    normed = rms_norm(rows, attn_gain)
    angles = pos_rows.astype(jnp.float32)[:, None] * rope_freqs()[None, :]
    cos_t = jnp.cos(angles)[:, None, :]
    sin_t = jnp.sin(angles)[:, None, :]
    q_raw = jnp.dot(normed, w_q, preferred_element_type=jnp.float32).reshape(count, kv_heads * group_rep, HEAD_DIM)
    k_raw = jnp.dot(normed, w_k, preferred_element_type=jnp.float32).reshape(count, kv_heads, HEAD_DIM)
    v_raw = jnp.dot(normed, w_v, preferred_element_type=jnp.float32).reshape(count, kv_heads, HEAD_DIM)
    q_heads = apply_rope(q_raw, cos_t, sin_t).astype(jnp.bfloat16).reshape(count, kv_heads, group_rep, HEAD_DIM)
    k_heads = apply_rope(k_raw, cos_t, sin_t).astype(jnp.bfloat16)
    return q_heads, k_heads, v_raw.astype(jnp.bfloat16)


def attend_block(state, q_heads, seg_rows, pos_rows, k_block, v_block, seg_keys, pos_keys):
    m_run, l_run, acc_run = state
    scores = jnp.einsum('tgrd,ugd->grtu', q_heads, k_block, preferred_element_type=jnp.float32) * (HEAD_DIM ** -0.5)
    visible = (seg_keys[None, :] == seg_rows[:, None]) & (pos_keys[None, :] <= pos_rows[:, None])
    scores = jnp.where(visible, scores, NEG_BIG)
    m_new = jnp.maximum(m_run, jnp.max(scores, axis=-1))
    prob_w = jnp.where(visible, jnp.exp(scores - m_new[..., None]), 0.0)
    rescale = jnp.exp(m_run - m_new)
    l_new = l_run * rescale + jnp.sum(prob_w, axis=-1)
    acc_new = acc_run * rescale[..., None] + jnp.einsum('grtu,ugd->grtd', prob_w.astype(jnp.bfloat16), v_block, preferred_element_type=jnp.float32)
    return m_new, l_new, acc_new


def close_attention(state):
    l_run = state[1]
    kv_heads, group_rep, count = l_run.shape
    out_rows = state[2] / l_run[..., None]
    return out_rows.transpose(2, 0, 1, 3).reshape(count, kv_heads * group_rep * HEAD_DIM).astype(jnp.bfloat16)


def finish_rows(rows, attn_rows, w_o, mlp_gain, w_gate, w_up, w_down):
    resid_mid = (rows.astype(jnp.float32) + jnp.dot(attn_rows, w_o, preferred_element_type=jnp.float32)).astype(jnp.bfloat16)
    normed = rms_norm(resid_mid, mlp_gain)
    gate = jnp.dot(normed, w_gate, preferred_element_type=jnp.float32)
    up_val = jnp.dot(normed, w_up, preferred_element_type=jnp.float32)
    hidden = (jax.nn.silu(gate) * up_val).astype(jnp.bfloat16)
    return (resid_mid.astype(jnp.float32) + jnp.dot(hidden, w_down, preferred_element_type=jnp.float32)).astype(jnp.bfloat16)


def solution(mesh):
    cp_size = mesh.shape['cp']
    shift = [(src, (src + 1) % cp_size) for src in range(cp_size)]

    def device_fn(x_loc, seg_loc, pos_loc, attn_gain, w_q, w_k, w_v, w_o, mlp_gain, w_gate, w_up, w_down):
        rows = x_loc[0]
        q_heads, k_heads, v_heads = project_rows(rows, pos_loc, attn_gain, w_q, w_k, w_v)
        count = q_heads.shape[0]
        kv_heads = q_heads.shape[1]
        group_rep = q_heads.shape[2]
        state = (jnp.full((kv_heads, group_rep, count), NEG_BIG, jnp.float32), jnp.zeros((kv_heads, group_rep, count), jnp.float32), jnp.zeros((kv_heads, group_rep, count, HEAD_DIM), jnp.float32))
        state = attend_block(state, q_heads, seg_loc, pos_loc, k_heads, v_heads, seg_loc, pos_loc)

        def remote_step(step, carry):
            run_state, held = carry
            held = lax.ppermute(held, 'cp', shift)
            run_state = attend_block(run_state, q_heads, seg_loc, pos_loc, held[0], held[1], held[2], held[3])
            return run_state, held

        state = lax.fori_loop(0, cp_size - 1, remote_step, (state, (k_heads, v_heads, seg_loc, pos_loc)))[0]
        attn_rows = close_attention(state)
        z_rows = finish_rows(rows, attn_rows, w_o, mlp_gain, w_gate, w_up, w_down)
        return z_rows[None], k_heads, v_heads

    seq_spec = P(('dp', 'cp'))
    return jax.shard_map(device_fn, mesh=mesh, in_specs=(P('dp', 'cp', None), seq_spec, seq_spec, P(), P(), P(), P(), P(), P(), P(), P(), P()), out_specs=(P('dp', 'cp', None), P(('dp', 'cp'), None, None), P(('dp', 'cp'), None, None)), check_vma=False)
```

profile of v0, /device:TPU:97, one launch (start us, length us, event | category | flops | bytes accessed | tf_op | source)
XLA Modules:
  0.0 429.9 jit_solution(3294017206788666886)
XLA Ops:
  1.5 3.1 fusion.24
  4.6 21.3 %copy.37 = bf16[1024,8192]{1,0:T(8,128)(2,1)} copy(bf16[1024,8192]{0,1:T(8,128)(2,1)} %bitcast.150) | data formatting | bytes 33554432 | tf_op jit(solution)/shard_map/dot_general | solution.py:45
  25.9 11.6 %fusion.34 = f32[256,8,128]{0,2,1:T(8,128)S(1)} fusion(bf16[8,128,8192]{2,1,0:T(8,128)(2,1)} %bitcast.151, bf16[1,256,8192]{2,1,0:T(8,128)(2,1)} %param.14, f32[8192]{0:T(1024)S(1)} %convert_element_type.94, f32[256]{0:T(256)S(1)} %add_rsqrt_fusion.1), kind=kOutput, calls=%fused_computation.47 | convolution fusion | flops 4303355904 | bytes 22053888 | tf_op jit(solution)/shard_map/dot_general | solution.py:45
  38.2 1.7 fusion.49
  40.9 1.5 fusion.52
  42.5 1.0 fusion.41
  45.1 288.6 %while.22 = (s32[]{:T(128)}, f32[1,8,256]{2,1,0:T(8,128)S(1)}, f32[1,8,256]{2,1,0:T(8,128)S(1)}, f32[1,8,256,128]{3,2,1,0:T(8,128)S(1)}, bf16[256,1,128]{2,0,1:T...) while((s32[]{:T(128)}, f32[1,8,256]{2,1,0:T(8,128)S(1)}, ...), condition=%wide.region_6.7_spmd, body=%wide.region_3.6_spmd.sunk | while | flops 275978240 | bytes 10240277 | solution.py:101
  45.1 2.7 collective-permute-start
  47.8 1.7 collective-permute-start.2
  49.7 1.1 collective-permute-done.2
  51.9 1.0 fusion.102
  52.9 2.5 collective-permute-start
  55.5 1.3 collective-permute-start.2
  57.0 1.2 collective-permute-done
  59.5 1.0 fusion.102
  60.6 2.1 collective-permute-start
  62.8 2.0 collective-permute-start.2
  64.8 1.1 collective-permute-start.3
  65.9 1.6 collective-permute-done
  70.7 1.1 collective-permute-start.1
  71.8 2.4 collective-permute-start.2
  74.3 2.7 collective-permute-done
  80.2 2.2 collective-permute-start.2
  82.5 3.9 collective-permute-done
  87.8 1.0 fusion.102
  89.1 1.5 collective-permute-start.2
  90.7 5.1 %collective-permute-done = s32[256]{0:T(256)S(1)} collective-permute-done((s32[256]{0:T(256)S(1)}, s32[256]{0:T(256)S(1)}, u32[]{:S(2)}, u32[]{:S(2)}) %collective-permute-start) | collective-permute-done | bytes 1056 | tf_op jit(solution)/shard_map/while/body/eval_jaxpr/ppermute | solution.py:97
  97.2 1.0 fusion.102
  98.9 6.3 %collective-permute-done = s32[256]{0:T(256)S(1)} collective-permute-done((s32[256]{0:T(256)S(1)}, s32[256]{0:T(256)S(1)}, u32[]{:S(2)}, u32[]{:S(2)}) %collective-permute-start) | collective-permute-done | bytes 1056 | tf_op jit(solution)/shard_map/while/body/eval_jaxpr/ppermute | solution.py:97
  106.6 1.0 fusion.102
  108.1 6.5 %collective-permute-done = s32[256]{0:T(256)S(1)} collective-permute-done((s32[256]{0:T(256)S(1)}, s32[256]{0:T(256)S(1)}, u32[]{:S(2)}, u32[]{:S(2)}) %collective-permute-start) | collective-permute-done | bytes 1056 | tf_op jit(solution)/shard_map/while/body/eval_jaxpr/ppermute | solution.py:97
  116.1 1.0 fusion.102
  117.5 6.5 %collective-permute-done = s32[256]{0:T(256)S(1)} collective-permute-done((s32[256]{0:T(256)S(1)}, s32[256]{0:T(256)S(1)}, u32[]{:S(2)}, u32[]{:S(2)}) %collective-permute-start) | collective-permute-done | bytes 1056 | tf_op jit(solution)/shard_map/while/body/eval_jaxpr/ppermute | solution.py:97
  125.5 1.0 fusion.102
  127.0 6.6 %collective-permute-done = s32[256]{0:T(256)S(1)} collective-permute-done((s32[256]{0:T(256)S(1)}, s32[256]{0:T(256)S(1)}, u32[]{:S(2)}, u32[]{:S(2)}) %collective-permute-start) | collective-permute-done | bytes 1056 | tf_op jit(solution)/shard_map/while/body/eval_jaxpr/ppermute | solution.py:97
  134.9 1.0 fusion.102
  136.4 6.5 %collective-permute-done = s32[256]{0:T(256)S(1)} collective-permute-done((s32[256]{0:T(256)S(1)}, s32[256]{0:T(256)S(1)}, u32[]{:S(2)}, u32[]{:S(2)}) %collective-permute-start) | collective-permute-done | bytes 1056 | tf_op jit(solution)/shard_map/while/body/eval_jaxpr/ppermute | solution.py:97
  145.8 6.5 %collective-permute-done = s32[256]{0:T(256)S(1)} collective-permute-done((s32[256]{0:T(256)S(1)}, s32[256]{0:T(256)S(1)}, u32[]{:S(2)}, u32[]{:S(2)}) %collective-permute-start) | collective-permute-done | bytes 1056 | tf_op jit(solution)/shard_map/while/body/eval_jaxpr/ppermute | solution.py:97
  155.2 6.6 %collective-permute-done = s32[256]{0:T(256)S(1)} collective-permute-done((s32[256]{0:T(256)S(1)}, s32[256]{0:T(256)S(1)}, u32[]{:S(2)}, u32[]{:S(2)}) %collective-permute-start) | collective-permute-done | bytes 1056 | tf_op jit(solution)/shard_map/while/body/eval_jaxpr/ppermute | solution.py:97
  163.2 1.0 fusion.102
  164.6 6.5 %collective-permute-done = s32[256]{0:T(256)S(1)} collective-permute-done((s32[256]{0:T(256)S(1)}, s32[256]{0:T(256)S(1)}, u32[]{:S(2)}, u32[]{:S(2)}) %collective-permute-start) | collective-permute-done | bytes 1056 | tf_op jit(solution)/shard_map/while/body/eval_jaxpr/ppermute | solution.py:97
  172.6 1.0 fusion.102
  174.1 6.5 %collective-permute-done = s32[256]{0:T(256)S(1)} collective-permute-done((s32[256]{0:T(256)S(1)}, s32[256]{0:T(256)S(1)}, u32[]{:S(2)}, u32[]{:S(2)}) %collective-permute-start) | collective-permute-done | bytes 1056 | tf_op jit(solution)/shard_map/while/body/eval_jaxpr/ppermute | solution.py:97
  182.0 1.0 fusion.102
  183.5 6.6 %collective-permute-done = s32[256]{0:T(256)S(1)} collective-permute-done((s32[256]{0:T(256)S(1)}, s32[256]{0:T(256)S(1)}, u32[]{:S(2)}, u32[]{:S(2)}) %collective-permute-start) | collective-permute-done | bytes 1056 | tf_op jit(solution)/shard_map/while/body/eval_jaxpr/ppermute | solution.py:97
  192.9 6.5 %collective-permute-done = s32[256]{0:T(256)S(1)} collective-permute-done((s32[256]{0:T(256)S(1)}, s32[256]{0:T(256)S(1)}, u32[]{:S(2)}, u32[]{:S(2)}) %collective-permute-start) | collective-permute-done | bytes 1056 | tf_op jit(solution)/shard_map/while/body/eval_jaxpr/ppermute | solution.py:97
  202.3 6.5 %collective-permute-done = s32[256]{0:T(256)S(1)} collective-permute-done((s32[256]{0:T(256)S(1)}, s32[256]{0:T(256)S(1)}, u32[]{:S(2)}, u32[]{:S(2)}) %collective-permute-start) | collective-permute-done | bytes 1056 | tf_op jit(solution)/shard_map/while/body/eval_jaxpr/ppermute | solution.py:97
  211.7 6.6 %collective-permute-done = s32[256]{0:T(256)S(1)} collective-permute-done((s32[256]{0:T(256)S(1)}, s32[256]{0:T(256)S(1)}, u32[]{:S(2)}, u32[]{:S(2)}) %collective-permute-start) | collective-permute-done | bytes 1056 | tf_op jit(solution)/shard_map/while/body/eval_jaxpr/ppermute | solution.py:97
  221.2 6.5 %collective-permute-done = s32[256]{0:T(256)S(1)} collective-permute-done((s32[256]{0:T(256)S(1)}, s32[256]{0:T(256)S(1)}, u32[]{:S(2)}, u32[]{:S(2)}) %collective-permute-start) | collective-permute-done | bytes 1056 | tf_op jit(solution)/shard_map/while/body/eval_jaxpr/ppermute | solution.py:97
  230.6 6.5 %collective-permute-done = s32[256]{0:T(256)S(1)} collective-permute-done((s32[256]{0:T(256)S(1)}, s32[256]{0:T(256)S(1)}, u32[]{:S(2)}, u32[]{:S(2)}) %collective-permute-start) | collective-permute-done | bytes 1056 | tf_op jit(solution)/shard_map/while/body/eval_jaxpr/ppermute | solution.py:97
  240.0 6.6 %collective-permute-done = s32[256]{0:T(256)S(1)} collective-permute-done((s32[256]{0:T(256)S(1)}, s32[256]{0:T(256)S(1)}, u32[]{:S(2)}, u32[]{:S(2)}) %collective-permute-start) | collective-permute-done | bytes 1056 | tf_op jit(solution)/shard_map/while/body/eval_jaxpr/ppermute | solution.py:97
  249.4 6.5 %collective-permute-done = s32[256]{0:T(256)S(1)} collective-permute-done((s32[256]{0:T(256)S(1)}, s32[256]{0:T(256)S(1)}, u32[]{:S(2)}, u32[]{:S(2)}) %collective-permute-start) | collective-permute-done | bytes 1056 | tf_op jit(solution)/shard_map/while/body/eval_jaxpr/ppermute | solution.py:97
  258.8 6.5 %collective-permute-done = s32[256]{0:T(256)S(1)} collective-permute-done((s32[256]{0:T(256)S(1)}, s32[256]{0:T(256)S(1)}, u32[]{:S(2)}, u32[]{:S(2)}) %collective-permute-start) | collective-permute-done | bytes 1056 | tf_op jit(solution)/shard_map/while/body/eval_jaxpr/ppermute | solution.py:97
  268.3 6.6 %collective-permute-done = s32[256]{0:T(256)S(1)} collective-permute-done((s32[256]{0:T(256)S(1)}, s32[256]{0:T(256)S(1)}, u32[]{:S(2)}, u32[]{:S(2)}) %collective-permute-start) | collective-permute-done | bytes 1056 | tf_op jit(solution)/shard_map/while/body/eval_jaxpr/ppermute | solution.py:97
  277.7 6.5 %collective-permute-done = s32[256]{0:T(256)S(1)} collective-permute-done((s32[256]{0:T(256)S(1)}, s32[256]{0:T(256)S(1)}, u32[]{:S(2)}, u32[]{:S(2)}) %collective-permute-start) | collective-permute-done | bytes 1056 | tf_op jit(solution)/shard_map/while/body/eval_jaxpr/ppermute | solution.py:97
  287.1 6.5 %collective-permute-done = s32[256]{0:T(256)S(1)} collective-permute-done((s32[256]{0:T(256)S(1)}, s32[256]{0:T(256)S(1)}, u32[]{:S(2)}, u32[]{:S(2)}) %collective-permute-start) | collective-permute-done | bytes 1056 | tf_op jit(solution)/shard_map/while/body/eval_jaxpr/ppermute | solution.py:97
  296.5 6.6 %collective-permute-done = s32[256]{0:T(256)S(1)} collective-permute-done((s32[256]{0:T(256)S(1)}, s32[256]{0:T(256)S(1)}, u32[]{:S(2)}, u32[]{:S(2)}) %collective-permute-start) | collective-permute-done | bytes 1056 | tf_op jit(solution)/shard_map/while/body/eval_jaxpr/ppermute | solution.py:97
  306.0 6.5 %collective-permute-done = s32[256]{0:T(256)S(1)} collective-permute-done((s32[256]{0:T(256)S(1)}, s32[256]{0:T(256)S(1)}, u32[]{:S(2)}, u32[]{:S(2)}) %collective-permute-start) | collective-permute-done | bytes 1056 | tf_op jit(solution)/shard_map/while/body/eval_jaxpr/ppermute | solution.py:97
  315.4 6.5 %collective-permute-done = s32[256]{0:T(256)S(1)} collective-permute-done((s32[256]{0:T(256)S(1)}, s32[256]{0:T(256)S(1)}, u32[]{:S(2)}, u32[]{:S(2)}) %collective-permute-start) | collective-permute-done | bytes 1056 | tf_op jit(solution)/shard_map/while/body/eval_jaxpr/ppermute | solution.py:97
  324.8 6.6 %collective-permute-done = s32[256]{0:T(256)S(1)} collective-permute-done((s32[256]{0:T(256)S(1)}, s32[256]{0:T(256)S(1)}, u32[]{:S(2)}, u32[]{:S(2)}) %collective-permute-start) | collective-permute-done | bytes 1056 | tf_op jit(solution)/shard_map/while/body/eval_jaxpr/ppermute | solution.py:97
  334.2 14.2 %fusion.29 = (f32[256]{0:T(256)S(1)}, bf16[256,8192]{1,0:T(8,128)(2,1)}) fusion(bf16[256,1024]{0,1:T(8,128)(2,1)S(1)} %bitcast.154, bf16[1024,8192]{1,0:T(8,128)(2,1)} %param.21, bf16[1,256,8192]{2,1,0:T(8,128)(2,1)} %param.14), kind=kOutput, calls=%fused_computation.41 | convolution fusion | flops 4307550208 | bytes 25691136 | tf_op jit(solution)/shard_map/dot_general | solution.py:74
  348.4 26.9 %fusion.43 = f32[256,3584]{1,0:T(8,128)} fusion(bf16[8192,3584]{1,0:T(8,128)(2,1)} %param.23, bf16[256,8192]{1,0:T(8,128)(2,1)} %get-tuple-element.129, f32[8192]{0:T(1024)S(1)} %convert_element_type.109, f32[256]{0:T(256)S(1)} %add_rsqrt_fusion), kind=kOutput, calls=%fused_computation.57 | convolution fusion | flops 15040774144 | bytes 66618368 | tf_op jit(solution)/shard_map/dot_general | solution.py:76
  375.3 27.3 %fusion.32 = bf16[256,3584]{1,0:T(8,128)(2,1)} fusion(bf16[8192,3584]{1,0:T(8,128)(2,1)} %param.24, f32[256,3584]{1,0:T(8,128)} %fusion.43, bf16[256,8192]{1,0:T(8,128)(2,1)} %get-tuple-element.129, f32[8192]{0:T(1024)S(1)} %convert_element_type.109, f32[256]{0:T(256)S(1)} %add_rsqrt_fusion), kind=kOutput, calls=%fused_computation.45 | convolution fusion | flops 15046279168 | bytes 68453376 | tf_op jit(solution)/shard_map/dot_general | solution.py:77
  402.7 27.2 %fusion.23 = bf16[1,256,8192]{2,1,0:T(8,128)(2,1)} fusion(bf16[256,3584]{1,0:T(8,128)(2,1)} %fusion.32, bf16[3584,8192]{1,0:T(8,128)(2,1)} %param.25, bf16[256,8192]{1,0:T(8,128)(2,1)} %get-tuple-element.129), kind=kOutput, calls=%fused_computation.35 | convolution fusion | flops 15038676992 | bytes 68943872 | tf_op jit(solution)/shard_map/dot_general | solution.py:79
  (578 shorter events, 78.1 us)
Async XLA Ops:
  60.6 7.0 %collective-permute-start = (s32[256]{0:T(256)S(1)}, s32[256]{0:T(256)S(1)}, u32[]{:S(2)}, u32[]{:S(2)}) collective-permute-start(s32[256]{0:T(256)S(1)} %get-tuple-element.224), channel_id=1, source_target_pairs={{0,1},{1,2},{2,3},{3,4},{4,5},{5,6},{6,7},{7,8},{8,9},{9,10},{10,1... | collective-permute-start | bytes 3080 | tf_op jit(solution)/shard_map/while/body/eval_jaxpr/ppermute | solution.py:97
  70.0 7.0 %collective-permute-start = (s32[256]{0:T(256)S(1)}, s32[256]{0:T(256)S(1)}, u32[]{:S(2)}, u32[]{:S(2)}) collective-permute-start(s32[256]{0:T(256)S(1)} %get-tuple-element.224), channel_id=1, source_target_pairs={{0,1},{1,2},{2,3},{3,4},{4,5},{5,6},{6,7},{7,8},{8,9},{9,10},{10,1... | collective-permute-start | bytes 3080 | tf_op jit(solution)/shard_map/while/body/eval_jaxpr/ppermute | solution.py:97
  89.1 7.1 %collective-permute-start.2 = (bf16[256,1,128]{2,0,1:T(8,128)(2,1)S(1)}, bf16[256,1,128]{2,0,1:T(8,128)(2,1)S(1)}, u32[]{:S(2)}, u32[]{:S(2)}) collective-permute-start(bf16[256,1,128]{2,0,1:T(8,128)(2,1)S(1)} %get-tuple-element.221), channel_id=1, source_target_pairs={{0,1},{1,2},{2,3},{3,4},{4,5},{5,6},{6,7},{7,8},{8,9},{9,10},{10,1... | collective-permute-start | bytes 196616 | tf_op jit(solution)/shard_map/while/body/eval_jaxpr/ppermute | solution.py:97
  98.2 7.0 %collective-permute-start = (s32[256]{0:T(256)S(1)}, s32[256]{0:T(256)S(1)}, u32[]{:S(2)}, u32[]{:S(2)}) collective-permute-start(s32[256]{0:T(256)S(1)} %get-tuple-element.224), channel_id=1, source_target_pairs={{0,1},{1,2},{2,3},{3,4},{4,5},{5,6},{6,7},{7,8},{8,9},{9,10},{10,1... | collective-permute-start | bytes 3080 | tf_op jit(solution)/shard_map/while/body/eval_jaxpr/ppermute | solution.py:97
  98.4 7.0 %collective-permute-start.1 = (s32[256]{0:T(256)S(1)}, s32[256]{0:T(256)S(1)}, u32[]{:S(2)}, u32[]{:S(2)}) collective-permute-start(s32[256]{0:T(256)S(1)} %get-tuple-element.223), channel_id=1, source_target_pairs={{0,1},{1,2},{2,3},{3,4},{4,5},{5,6},{6,7},{7,8},{8,9},{9,10},{10,1... | collective-permute-start | bytes 3080 | tf_op jit(solution)/shard_map/while/body/eval_jaxpr/ppermute | solution.py:97
  98.5 7.1 %collective-permute-start.2 = (bf16[256,1,128]{2,0,1:T(8,128)(2,1)S(1)}, bf16[256,1,128]{2,0,1:T(8,128)(2,1)S(1)}, u32[]{:S(2)}, u32[]{:S(2)}) collective-permute-start(bf16[256,1,128]{2,0,1:T(8,128)(2,1)S(1)} %get-tuple-element.221), channel_id=1, source_target_pairs={{0,1},{1,2},{2,3},{3,4},{4,5},{5,6},{6,7},{7,8},{8,9},{9,10},{10,1... | collective-permute-start | bytes 196616 | tf_op jit(solution)/shard_map/while/body/eval_jaxpr/ppermute | solution.py:97
  98.8 7.8 %collective-permute-start.3 = (bf16[256,1,128]{2,0,1:T(8,128)(2,1)S(1)}, bf16[256,1,128]{2,0,1:T(8,128)(2,1)S(1)}, u32[]{:S(2)}, u32[]{:S(2)}) collective-permute-start(bf16[256,1,128]{2,0,1:T(8,128)(2,1)S(1)} %get-tuple-element.222), channel_id=1, source_target_pairs={{0,1},{1,2},{2,3},{3,4},{4,5},{5,6},{6,7},{7,8},{8,9},{9,10},{10,1... | collective-permute-start | bytes 196616 | tf_op jit(solution)/shard_map/while/body/eval_jaxpr/ppermute | solution.py:97
  107.9 7.1 %collective-permute-start.2 = (bf16[256,1,128]{2,0,1:T(8,128)(2,1)S(1)}, bf16[256,1,128]{2,0,1:T(8,128)(2,1)S(1)}, u32[]{:S(2)}, u32[]{:S(2)}) collective-permute-start(bf16[256,1,128]{2,0,1:T(8,128)(2,1)S(1)} %get-tuple-element.221), channel_id=1, source_target_pairs={{0,1},{1,2},{2,3},{3,4},{4,5},{5,6},{6,7},{7,8},{8,9},{9,10},{10,1... | collective-permute-start | bytes 196616 | tf_op jit(solution)/shard_map/while/body/eval_jaxpr/ppermute | solution.py:97
  108.0 8.0 %collective-permute-start.3 = (bf16[256,1,128]{2,0,1:T(8,128)(2,1)S(1)}, bf16[256,1,128]{2,0,1:T(8,128)(2,1)S(1)}, u32[]{:S(2)}, u32[]{:S(2)}) collective-permute-start(bf16[256,1,128]{2,0,1:T(8,128)(2,1)S(1)} %get-tuple-element.222), channel_id=1, source_target_pairs={{0,1},{1,2},{2,3},{3,4},{4,5},{5,6},{6,7},{7,8},{8,9},{9,10},{10,1... | collective-permute-start | bytes 196616 | tf_op jit(solution)/shard_map/while/body/eval_jaxpr/ppermute | solution.py:97
  117.3 7.1 %collective-permute-start.2 = (bf16[256,1,128]{2,0,1:T(8,128)(2,1)S(1)}, bf16[256,1,128]{2,0,1:T(8,128)(2,1)S(1)}, u32[]{:S(2)}, u32[]{:S(2)}) collective-permute-start(bf16[256,1,128]{2,0,1:T(8,128)(2,1)S(1)} %get-tuple-element.221), channel_id=1, source_target_pairs={{0,1},{1,2},{2,3},{3,4},{4,5},{5,6},{6,7},{7,8},{8,9},{9,10},{10,1... | collective-permute-start | bytes 196616 | tf_op jit(solution)/shard_map/while/body/eval_jaxpr/ppermute | solution.py:97
  117.4 8.0 %collective-permute-start.3 = (bf16[256,1,128]{2,0,1:T(8,128)(2,1)S(1)}, bf16[256,1,128]{2,0,1:T(8,128)(2,1)S(1)}, u32[]{:S(2)}, u32[]{:S(2)}) collective-permute-start(bf16[256,1,128]{2,0,1:T(8,128)(2,1)S(1)} %get-tuple-element.222), channel_id=1, source_target_pairs={{0,1},{1,2},{2,3},{3,4},{4,5},{5,6},{6,7},{7,8},{8,9},{9,10},{10,1... | collective-permute-start | bytes 196616 | tf_op jit(solution)/shard_map/while/body/eval_jaxpr/ppermute | solution.py:97
  126.5 7.0 %collective-permute-start = (s32[256]{0:T(256)S(1)}, s32[256]{0:T(256)S(1)}, u32[]{:S(2)}, u32[]{:S(2)}) collective-permute-start(s32[256]{0:T(256)S(1)} %get-tuple-element.224), channel_id=1, source_target_pairs={{0,1},{1,2},{2,3},{3,4},{4,5},{5,6},{6,7},{7,8},{8,9},{9,10},{10,1... | collective-permute-start | bytes 3080 | tf_op jit(solution)/shard_map/while/body/eval_jaxpr/ppermute | solution.py:97
  126.6 7.0 %collective-permute-start.1 = (s32[256]{0:T(256)S(1)}, s32[256]{0:T(256)S(1)}, u32[]{:S(2)}, u32[]{:S(2)}) collective-permute-start(s32[256]{0:T(256)S(1)} %get-tuple-element.223), channel_id=1, source_target_pairs={{0,1},{1,2},{2,3},{3,4},{4,5},{5,6},{6,7},{7,8},{8,9},{9,10},{10,1... | collective-permute-start | bytes 3080 | tf_op jit(solution)/shard_map/while/body/eval_jaxpr/ppermute | solution.py:97
  126.7 7.1 %collective-permute-start.2 = (bf16[256,1,128]{2,0,1:T(8,128)(2,1)S(1)}, bf16[256,1,128]{2,0,1:T(8,128)(2,1)S(1)}, u32[]{:S(2)}, u32[]{:S(2)}) collective-permute-start(bf16[256,1,128]{2,0,1:T(8,128)(2,1)S(1)} %get-tuple-element.221), channel_id=1, source_target_pairs={{0,1},{1,2},{2,3},{3,4},{4,5},{5,6},{6,7},{7,8},{8,9},{9,10},{10,1... | collective-permute-start | bytes 196616 | tf_op jit(solution)/shard_map/while/body/eval_jaxpr/ppermute | solution.py:97
  126.8 8.0 %collective-permute-start.3 = (bf16[256,1,128]{2,0,1:T(8,128)(2,1)S(1)}, bf16[256,1,128]{2,0,1:T(8,128)(2,1)S(1)}, u32[]{:S(2)}, u32[]{:S(2)}) collective-permute-start(bf16[256,1,128]{2,0,1:T(8,128)(2,1)S(1)} %get-tuple-element.222), channel_id=1, source_target_pairs={{0,1},{1,2},{2,3},{3,4},{4,5},{5,6},{6,7},{7,8},{8,9},{9,10},{10,1... | collective-permute-start | bytes 196616 | tf_op jit(solution)/shard_map/while/body/eval_jaxpr/ppermute | solution.py:97
  136.2 7.1 %collective-permute-start.2 = (bf16[256,1,128]{2,0,1:T(8,128)(2,1)S(1)}, bf16[256,1,128]{2,0,1:T(8,128)(2,1)S(1)}, u32[]{:S(2)}, u32[]{:S(2)}) collective-permute-start(bf16[256,1,128]{2,0,1:T(8,128)(2,1)S(1)} %get-tuple-element.221), channel_id=1, source_target_pairs={{0,1},{1,2},{2,3},{3,4},{4,5},{5,6},{6,7},{7,8},{8,9},{9,10},{10,1... | collective-permute-start | bytes 196616 | tf_op jit(solution)/shard_map/while/body/eval_jaxpr/ppermute | solution.py:97
  136.3 8.0 %collective-permute-start.3 = (bf16[256,1,128]{2,0,1:T(8,128)(2,1)S(1)}, bf16[256,1,128]{2,0,1:T(8,128)(2,1)S(1)}, u32[]{:S(2)}, u32[]{:S(2)}) collective-permute-start(bf16[256,1,128]{2,0,1:T(8,128)(2,1)S(1)} %get-tuple-element.222), channel_id=1, source_target_pairs={{0,1},{1,2},{2,3},{3,4},{4,5},{5,6},{6,7},{7,8},{8,9},{9,10},{10,1... | collective-permute-start | bytes 196616 | tf_op jit(solution)/shard_map/while/body/eval_jaxpr/ppermute | solution.py:97
  145.6 7.1 %collective-permute-start.2 = (bf16[256,1,128]{2,0,1:T(8,128)(2,1)S(1)}, bf16[256,1,128]{2,0,1:T(8,128)(2,1)S(1)}, u32[]{:S(2)}, u32[]{:S(2)}) collective-permute-start(bf16[256,1,128]{2,0,1:T(8,128)(2,1)S(1)} %get-tuple-element.221), channel_id=1, source_target_pairs={{0,1},{1,2},{2,3},{3,4},{4,5},{5,6},{6,7},{7,8},{8,9},{9,10},{10,1... | collective-permute-start | bytes 196616 | tf_op jit(solution)/shard_map/while/body/eval_jaxpr/ppermute | solution.py:97
  145.7 8.0 %collective-permute-start.3 = (bf16[256,1,128]{2,0,1:T(8,128)(2,1)S(1)}, bf16[256,1,128]{2,0,1:T(8,128)(2,1)S(1)}, u32[]{:S(2)}, u32[]{:S(2)}) collective-permute-start(bf16[256,1,128]{2,0,1:T(8,128)(2,1)S(1)} %get-tuple-element.222), channel_id=1, source_target_pairs={{0,1},{1,2},{2,3},{3,4},{4,5},{5,6},{6,7},{7,8},{8,9},{9,10},{10,1... | collective-permute-start | bytes 196616 | tf_op jit(solution)/shard_map/while/body/eval_jaxpr/ppermute | solution.py:97
  154.9 7.0 %collective-permute-start.1 = (s32[256]{0:T(256)S(1)}, s32[256]{0:T(256)S(1)}, u32[]{:S(2)}, u32[]{:S(2)}) collective-permute-start(s32[256]{0:T(256)S(1)} %get-tuple-element.223), channel_id=1, source_target_pairs={{0,1},{1,2},{2,3},{3,4},{4,5},{5,6},{6,7},{7,8},{8,9},{9,10},{10,1... | collective-permute-start | bytes 3080 | tf_op jit(solution)/shard_map/while/body/eval_jaxpr/ppermute | solution.py:97
  155.0 7.1 %collective-permute-start.2 = (bf16[256,1,128]{2,0,1:T(8,128)(2,1)S(1)}, bf16[256,1,128]{2,0,1:T(8,128)(2,1)S(1)}, u32[]{:S(2)}, u32[]{:S(2)}) collective-permute-start(bf16[256,1,128]{2,0,1:T(8,128)(2,1)S(1)} %get-tuple-element.221), channel_id=1, source_target_pairs={{0,1},{1,2},{2,3},{3,4},{4,5},{5,6},{6,7},{7,8},{8,9},{9,10},{10,1... | collective-permute-start | bytes 196616 | tf_op jit(solution)/shard_map/while/body/eval_jaxpr/ppermute | solution.py:97
  155.1 8.0 %collective-permute-start.3 = (bf16[256,1,128]{2,0,1:T(8,128)(2,1)S(1)}, bf16[256,1,128]{2,0,1:T(8,128)(2,1)S(1)}, u32[]{:S(2)}, u32[]{:S(2)}) collective-permute-start(bf16[256,1,128]{2,0,1:T(8,128)(2,1)S(1)} %get-tuple-element.222), channel_id=1, source_target_pairs={{0,1},{1,2},{2,3},{3,4},{4,5},{5,6},{6,7},{7,8},{8,9},{9,10},{10,1... | collective-permute-start | bytes 196616 | tf_op jit(solution)/shard_map/while/body/eval_jaxpr/ppermute | solution.py:97
  164.4 7.1 %collective-permute-start.2 = (bf16[256,1,128]{2,0,1:T(8,128)(2,1)S(1)}, bf16[256,1,128]{2,0,1:T(8,128)(2,1)S(1)}, u32[]{:S(2)}, u32[]{:S(2)}) collective-permute-start(bf16[256,1,128]{2,0,1:T(8,128)(2,1)S(1)} %get-tuple-element.221), channel_id=1, source_target_pairs={{0,1},{1,2},{2,3},{3,4},{4,5},{5,6},{6,7},{7,8},{8,9},{9,10},{10,1... | collective-permute-start | bytes 196616 | tf_op jit(solution)/shard_map/while/body/eval_jaxpr/ppermute | solution.py:97
  164.5 8.0 %collective-permute-start.3 = (bf16[256,1,128]{2,0,1:T(8,128)(2,1)S(1)}, bf16[256,1,128]{2,0,1:T(8,128)(2,1)S(1)}, u32[]{:S(2)}, u32[]{:S(2)}) collective-permute-start(bf16[256,1,128]{2,0,1:T(8,128)(2,1)S(1)} %get-tuple-element.222), channel_id=1, source_target_pairs={{0,1},{1,2},{2,3},{3,4},{4,5},{5,6},{6,7},{7,8},{8,9},{9,10},{10,1... | collective-permute-start | bytes 196616 | tf_op jit(solution)/shard_map/while/body/eval_jaxpr/ppermute | solution.py:97
  173.8 7.1 %collective-permute-start.2 = (bf16[256,1,128]{2,0,1:T(8,128)(2,1)S(1)}, bf16[256,1,128]{2,0,1:T(8,128)(2,1)S(1)}, u32[]{:S(2)}, u32[]{:S(2)}) collective-permute-start(bf16[256,1,128]{2,0,1:T(8,128)(2,1)S(1)} %get-tuple-element.221), channel_id=1, source_target_pairs={{0,1},{1,2},{2,3},{3,4},{4,5},{5,6},{6,7},{7,8},{8,9},{9,10},{10,1... | collective-permute-start | bytes 196616 | tf_op jit(solution)/shard_map/while/body/eval_jaxpr/ppermute | solution.py:97
  173.9 8.0 %collective-permute-start.3 = (bf16[256,1,128]{2,0,1:T(8,128)(2,1)S(1)}, bf16[256,1,128]{2,0,1:T(8,128)(2,1)S(1)}, u32[]{:S(2)}, u32[]{:S(2)}) collective-permute-start(bf16[256,1,128]{2,0,1:T(8,128)(2,1)S(1)} %get-tuple-element.222), channel_id=1, source_target_pairs={{0,1},{1,2},{2,3},{3,4},{4,5},{5,6},{6,7},{7,8},{8,9},{9,10},{10,1... | collective-permute-start | bytes 196616 | tf_op jit(solution)/shard_map/while/body/eval_jaxpr/ppermute | solution.py:97
  183.1 7.0 %collective-permute-start.1 = (s32[256]{0:T(256)S(1)}, s32[256]{0:T(256)S(1)}, u32[]{:S(2)}, u32[]{:S(2)}) collective-permute-start(s32[256]{0:T(256)S(1)} %get-tuple-element.223), channel_id=1, source_target_pairs={{0,1},{1,2},{2,3},{3,4},{4,5},{5,6},{6,7},{7,8},{8,9},{9,10},{10,1... | collective-permute-start | bytes 3080 | tf_op jit(solution)/shard_map/while/body/eval_jaxpr/ppermute | solution.py:97
  183.3 7.1 %collective-permute-start.2 = (bf16[256,1,128]{2,0,1:T(8,128)(2,1)S(1)}, bf16[256,1,128]{2,0,1:T(8,128)(2,1)S(1)}, u32[]{:S(2)}, u32[]{:S(2)}) collective-permute-start(bf16[256,1,128]{2,0,1:T(8,128)(2,1)S(1)} %get-tuple-element.221), channel_id=1, source_target_pairs={{0,1},{1,2},{2,3},{3,4},{4,5},{5,6},{6,7},{7,8},{8,9},{9,10},{10,1... | collective-permute-start | bytes 196616 | tf_op jit(solution)/shard_map/while/body/eval_jaxpr/ppermute | solution.py:97
  183.4 8.0 %collective-permute-start.3 = (bf16[256,1,128]{2,0,1:T(8,128)(2,1)S(1)}, bf16[256,1,128]{2,0,1:T(8,128)(2,1)S(1)}, u32[]{:S(2)}, u32[]{:S(2)}) collective-permute-start(bf16[256,1,128]{2,0,1:T(8,128)(2,1)S(1)} %get-tuple-element.222), channel_id=1, source_target_pairs={{0,1},{1,2},{2,3},{3,4},{4,5},{5,6},{6,7},{7,8},{8,9},{9,10},{10,1... | collective-permute-start | bytes 196616 | tf_op jit(solution)/shard_map/while/body/eval_jaxpr/ppermute | solution.py:97
  192.7 7.1 %collective-permute-start.2 = (bf16[256,1,128]{2,0,1:T(8,128)(2,1)S(1)}, bf16[256,1,128]{2,0,1:T(8,128)(2,1)S(1)}, u32[]{:S(2)}, u32[]{:S(2)}) collective-permute-start(bf16[256,1,128]{2,0,1:T(8,128)(2,1)S(1)} %get-tuple-element.221), channel_id=1, source_target_pairs={{0,1},{1,2},{2,3},{3,4},{4,5},{5,6},{6,7},{7,8},{8,9},{9,10},{10,1... | collective-permute-start | bytes 196616 | tf_op jit(solution)/shard_map/while/body/eval_jaxpr/ppermute | solution.py:97
  192.8 8.0 %collective-permute-start.3 = (bf16[256,1,128]{2,0,1:T(8,128)(2,1)S(1)}, bf16[256,1,128]{2,0,1:T(8,128)(2,1)S(1)}, u32[]{:S(2)}, u32[]{:S(2)}) collective-permute-start(bf16[256,1,128]{2,0,1:T(8,128)(2,1)S(1)} %get-tuple-element.222), channel_id=1, source_target_pairs={{0,1},{1,2},{2,3},{3,4},{4,5},{5,6},{6,7},{7,8},{8,9},{9,10},{10,1... | collective-permute-start | bytes 196616 | tf_op jit(solution)/shard_map/while/body/eval_jaxpr/ppermute | solution.py:97
  202.1 7.1 %collective-permute-start.2 = (bf16[256,1,128]{2,0,1:T(8,128)(2,1)S(1)}, bf16[256,1,128]{2,0,1:T(8,128)(2,1)S(1)}, u32[]{:S(2)}, u32[]{:S(2)}) collective-permute-start(bf16[256,1,128]{2,0,1:T(8,128)(2,1)S(1)} %get-tuple-element.221), channel_id=1, source_target_pairs={{0,1},{1,2},{2,3},{3,4},{4,5},{5,6},{6,7},{7,8},{8,9},{9,10},{10,1... | collective-permute-start | bytes 196616 | tf_op jit(solution)/shard_map/while/body/eval_jaxpr/ppermute | solution.py:97
  202.2 8.0 %collective-permute-start.3 = (bf16[256,1,128]{2,0,1:T(8,128)(2,1)S(1)}, bf16[256,1,128]{2,0,1:T(8,128)(2,1)S(1)}, u32[]{:S(2)}, u32[]{:S(2)}) collective-permute-start(bf16[256,1,128]{2,0,1:T(8,128)(2,1)S(1)} %get-tuple-element.222), channel_id=1, source_target_pairs={{0,1},{1,2},{2,3},{3,4},{4,5},{5,6},{6,7},{7,8},{8,9},{9,10},{10,1... | collective-permute-start | bytes 196616 | tf_op jit(solution)/shard_map/while/body/eval_jaxpr/ppermute | solution.py:97
  211.3 7.0 %collective-permute-start = (s32[256]{0:T(256)S(1)}, s32[256]{0:T(256)S(1)}, u32[]{:S(2)}, u32[]{:S(2)}) collective-permute-start(s32[256]{0:T(256)S(1)} %get-tuple-element.224), channel_id=1, source_target_pairs={{0,1},{1,2},{2,3},{3,4},{4,5},{5,6},{6,7},{7,8},{8,9},{9,10},{10,1... | collective-permute-start | bytes 3080 | tf_op jit(solution)/shard_map/while/body/eval_jaxpr/ppermute | solution.py:97
  211.5 7.1 %collective-permute-start.2 = (bf16[256,1,128]{2,0,1:T(8,128)(2,1)S(1)}, bf16[256,1,128]{2,0,1:T(8,128)(2,1)S(1)}, u32[]{:S(2)}, u32[]{:S(2)}) collective-permute-start(bf16[256,1,128]{2,0,1:T(8,128)(2,1)S(1)} %get-tuple-element.221), channel_id=1, source_target_pairs={{0,1},{1,2},{2,3},{3,4},{4,5},{5,6},{6,7},{7,8},{8,9},{9,10},{10,1... | collective-permute-start | bytes 196616 | tf_op jit(solution)/shard_map/while/body/eval_jaxpr/ppermute | solution.py:97
  211.6 8.0 %collective-permute-start.3 = (bf16[256,1,128]{2,0,1:T(8,128)(2,1)S(1)}, bf16[256,1,128]{2,0,1:T(8,128)(2,1)S(1)}, u32[]{:S(2)}, u32[]{:S(2)}) collective-permute-start(bf16[256,1,128]{2,0,1:T(8,128)(2,1)S(1)} %get-tuple-element.222), channel_id=1, source_target_pairs={{0,1},{1,2},{2,3},{3,4},{4,5},{5,6},{6,7},{7,8},{8,9},{9,10},{10,1... | collective-permute-start | bytes 196616 | tf_op jit(solution)/shard_map/while/body/eval_jaxpr/ppermute | solution.py:97
  220.9 7.1 %collective-permute-start.2 = (bf16[256,1,128]{2,0,1:T(8,128)(2,1)S(1)}, bf16[256,1,128]{2,0,1:T(8,128)(2,1)S(1)}, u32[]{:S(2)}, u32[]{:S(2)}) collective-permute-start(bf16[256,1,128]{2,0,1:T(8,128)(2,1)S(1)} %get-tuple-element.221), channel_id=1, source_target_pairs={{0,1},{1,2},{2,3},{3,4},{4,5},{5,6},{6,7},{7,8},{8,9},{9,10},{10,1... | collective-permute-start | bytes 196616 | tf_op jit(solution)/shard_map/while/body/eval_jaxpr/ppermute | solution.py:97
  221.1 8.0 %collective-permute-start.3 = (bf16[256,1,128]{2,0,1:T(8,128)(2,1)S(1)}, bf16[256,1,128]{2,0,1:T(8,128)(2,1)S(1)}, u32[]{:S(2)}, u32[]{:S(2)}) collective-permute-start(bf16[256,1,128]{2,0,1:T(8,128)(2,1)S(1)} %get-tuple-element.222), channel_id=1, source_target_pairs={{0,1},{1,2},{2,3},{3,4},{4,5},{5,6},{6,7},{7,8},{8,9},{9,10},{10,1... | collective-permute-start | bytes 196616 | tf_op jit(solution)/shard_map/while/body/eval_jaxpr/ppermute | solution.py:97
  230.4 7.1 %collective-permute-start.2 = (bf16[256,1,128]{2,0,1:T(8,128)(2,1)S(1)}, bf16[256,1,128]{2,0,1:T(8,128)(2,1)S(1)}, u32[]{:S(2)}, u32[]{:S(2)}) collective-permute-start(bf16[256,1,128]{2,0,1:T(8,128)(2,1)S(1)} %get-tuple-element.221), channel_id=1, source_target_pairs={{0,1},{1,2},{2,3},{3,4},{4,5},{5,6},{6,7},{7,8},{8,9},{9,10},{10,1... | collective-permute-start | bytes 196616 | tf_op jit(solution)/shard_map/while/body/eval_jaxpr/ppermute | solution.py:97
  230.5 8.0 %collective-permute-start.3 = (bf16[256,1,128]{2,0,1:T(8,128)(2,1)S(1)}, bf16[256,1,128]{2,0,1:T(8,128)(2,1)S(1)}, u32[]{:S(2)}, u32[]{:S(2)}) collective-permute-start(bf16[256,1,128]{2,0,1:T(8,128)(2,1)S(1)} %get-tuple-element.222), channel_id=1, source_target_pairs={{0,1},{1,2},{2,3},{3,4},{4,5},{5,6},{6,7},{7,8},{8,9},{9,10},{10,1... | collective-permute-start | bytes 196616 | tf_op jit(solution)/shard_map/while/body/eval_jaxpr/ppermute | solution.py:97
  239.7 7.0 %collective-permute-start.1 = (s32[256]{0:T(256)S(1)}, s32[256]{0:T(256)S(1)}, u32[]{:S(2)}, u32[]{:S(2)}) collective-permute-start(s32[256]{0:T(256)S(1)} %get-tuple-element.223), channel_id=1, source_target_pairs={{0,1},{1,2},{2,3},{3,4},{4,5},{5,6},{6,7},{7,8},{8,9},{9,10},{10,1... | collective-permute-start | bytes 3080 | tf_op jit(solution)/shard_map/while/body/eval_jaxpr/ppermute | solution.py:97
  239.8 7.1 %collective-permute-start.2 = (bf16[256,1,128]{2,0,1:T(8,128)(2,1)S(1)}, bf16[256,1,128]{2,0,1:T(8,128)(2,1)S(1)}, u32[]{:S(2)}, u32[]{:S(2)}) collective-permute-start(bf16[256,1,128]{2,0,1:T(8,128)(2,1)S(1)} %get-tuple-element.221), channel_id=1, source_target_pairs={{0,1},{1,2},{2,3},{3,4},{4,5},{5,6},{6,7},{7,8},{8,9},{9,10},{10,1... | collective-permute-start | bytes 196616 | tf_op jit(solution)/shard_map/while/body/eval_jaxpr/ppermute | solution.py:97
  239.9 8.0 %collective-permute-start.3 = (bf16[256,1,128]{2,0,1:T(8,128)(2,1)S(1)}, bf16[256,1,128]{2,0,1:T(8,128)(2,1)S(1)}, u32[]{:S(2)}, u32[]{:S(2)}) collective-permute-start(bf16[256,1,128]{2,0,1:T(8,128)(2,1)S(1)} %get-tuple-element.222), channel_id=1, source_target_pairs={{0,1},{1,2},{2,3},{3,4},{4,5},{5,6},{6,7},{7,8},{8,9},{9,10},{10,1... | collective-permute-start | bytes 196616 | tf_op jit(solution)/shard_map/while/body/eval_jaxpr/ppermute | solution.py:97
  249.2 7.1 %collective-permute-start.2 = (bf16[256,1,128]{2,0,1:T(8,128)(2,1)S(1)}, bf16[256,1,128]{2,0,1:T(8,128)(2,1)S(1)}, u32[]{:S(2)}, u32[]{:S(2)}) collective-permute-start(bf16[256,1,128]{2,0,1:T(8,128)(2,1)S(1)} %get-tuple-element.221), channel_id=1, source_target_pairs={{0,1},{1,2},{2,3},{3,4},{4,5},{5,6},{6,7},{7,8},{8,9},{9,10},{10,1... | collective-permute-start | bytes 196616 | tf_op jit(solution)/shard_map/while/body/eval_jaxpr/ppermute | solution.py:97
  249.3 8.0 %collective-permute-start.3 = (bf16[256,1,128]{2,0,1:T(8,128)(2,1)S(1)}, bf16[256,1,128]{2,0,1:T(8,128)(2,1)S(1)}, u32[]{:S(2)}, u32[]{:S(2)}) collective-permute-start(bf16[256,1,128]{2,0,1:T(8,128)(2,1)S(1)} %get-tuple-element.222), channel_id=1, source_target_pairs={{0,1},{1,2},{2,3},{3,4},{4,5},{5,6},{6,7},{7,8},{8,9},{9,10},{10,1... | collective-permute-start | bytes 196616 | tf_op jit(solution)/shard_map/while/body/eval_jaxpr/ppermute | solution.py:97
  258.6 7.1 %collective-permute-start.2 = (bf16[256,1,128]{2,0,1:T(8,128)(2,1)S(1)}, bf16[256,1,128]{2,0,1:T(8,128)(2,1)S(1)}, u32[]{:S(2)}, u32[]{:S(2)}) collective-permute-start(bf16[256,1,128]{2,0,1:T(8,128)(2,1)S(1)} %get-tuple-element.221), channel_id=1, source_target_pairs={{0,1},{1,2},{2,3},{3,4},{4,5},{5,6},{6,7},{7,8},{8,9},{9,10},{10,1... | collective-permute-start | bytes 196616 | tf_op jit(solution)/shard_map/while/body/eval_jaxpr/ppermute | solution.py:97
  258.7 8.0 %collective-permute-start.3 = (bf16[256,1,128]{2,0,1:T(8,128)(2,1)S(1)}, bf16[256,1,128]{2,0,1:T(8,128)(2,1)S(1)}, u32[]{:S(2)}, u32[]{:S(2)}) collective-permute-start(bf16[256,1,128]{2,0,1:T(8,128)(2,1)S(1)} %get-tuple-element.222), channel_id=1, source_target_pairs={{0,1},{1,2},{2,3},{3,4},{4,5},{5,6},{6,7},{7,8},{8,9},{9,10},{10,1... | collective-permute-start | bytes 196616 | tf_op jit(solution)/shard_map/while/body/eval_jaxpr/ppermute | solution.py:97
  267.8 7.0 %collective-permute-start = (s32[256]{0:T(256)S(1)}, s32[256]{0:T(256)S(1)}, u32[]{:S(2)}, u32[]{:S(2)}) collective-permute-start(s32[256]{0:T(256)S(1)} %get-tuple-element.224), channel_id=1, source_target_pairs={{0,1},{1,2},{2,3},{3,4},{4,5},{5,6},{6,7},{7,8},{8,9},{9,10},{10,1... | collective-permute-start | bytes 3080 | tf_op jit(solution)/shard_map/while/body/eval_jaxpr/ppermute | solution.py:97
  268.0 7.1 %collective-permute-start.2 = (bf16[256,1,128]{2,0,1:T(8,128)(2,1)S(1)}, bf16[256,1,128]{2,0,1:T(8,128)(2,1)S(1)}, u32[]{:S(2)}, u32[]{:S(2)}) collective-permute-start(bf16[256,1,128]{2,0,1:T(8,128)(2,1)S(1)} %get-tuple-element.221), channel_id=1, source_target_pairs={{0,1},{1,2},{2,3},{3,4},{4,5},{5,6},{6,7},{7,8},{8,9},{9,10},{10,1... | collective-permute-start | bytes 196616 | tf_op jit(solution)/shard_map/while/body/eval_jaxpr/ppermute | solution.py:97
  268.2 8.0 %collective-permute-start.3 = (bf16[256,1,128]{2,0,1:T(8,128)(2,1)S(1)}, bf16[256,1,128]{2,0,1:T(8,128)(2,1)S(1)}, u32[]{:S(2)}, u32[]{:S(2)}) collective-permute-start(bf16[256,1,128]{2,0,1:T(8,128)(2,1)S(1)} %get-tuple-element.222), channel_id=1, source_target_pairs={{0,1},{1,2},{2,3},{3,4},{4,5},{5,6},{6,7},{7,8},{8,9},{9,10},{10,1... | collective-permute-start | bytes 196616 | tf_op jit(solution)/shard_map/while/body/eval_jaxpr/ppermute | solution.py:97
  277.5 7.1 %collective-permute-start.2 = (bf16[256,1,128]{2,0,1:T(8,128)(2,1)S(1)}, bf16[256,1,128]{2,0,1:T(8,128)(2,1)S(1)}, u32[]{:S(2)}, u32[]{:S(2)}) collective-permute-start(bf16[256,1,128]{2,0,1:T(8,128)(2,1)S(1)} %get-tuple-element.221), channel_id=1, source_target_pairs={{0,1},{1,2},{2,3},{3,4},{4,5},{5,6},{6,7},{7,8},{8,9},{9,10},{10,1... | collective-permute-start | bytes 196616 | tf_op jit(solution)/shard_map/while/body/eval_jaxpr/ppermute | solution.py:97
  277.6 8.0 %collective-permute-start.3 = (bf16[256,1,128]{2,0,1:T(8,128)(2,1)S(1)}, bf16[256,1,128]{2,0,1:T(8,128)(2,1)S(1)}, u32[]{:S(2)}, u32[]{:S(2)}) collective-permute-start(bf16[256,1,128]{2,0,1:T(8,128)(2,1)S(1)} %get-tuple-element.222), channel_id=1, source_target_pairs={{0,1},{1,2},{2,3},{3,4},{4,5},{5,6},{6,7},{7,8},{8,9},{9,10},{10,1... | collective-permute-start | bytes 196616 | tf_op jit(solution)/shard_map/while/body/eval_jaxpr/ppermute | solution.py:97
  286.9 7.1 %collective-permute-start.2 = (bf16[256,1,128]{2,0,1:T(8,128)(2,1)S(1)}, bf16[256,1,128]{2,0,1:T(8,128)(2,1)S(1)}, u32[]{:S(2)}, u32[]{:S(2)}) collective-permute-start(bf16[256,1,128]{2,0,1:T(8,128)(2,1)S(1)} %get-tuple-element.221), channel_id=1, source_target_pairs={{0,1},{1,2},{2,3},{3,4},{4,5},{5,6},{6,7},{7,8},{8,9},{9,10},{10,1... | collective-permute-start | bytes 196616 | tf_op jit(solution)/shard_map/while/body/eval_jaxpr/ppermute | solution.py:97
  287.0 8.0 %collective-permute-start.3 = (bf16[256,1,128]{2,0,1:T(8,128)(2,1)S(1)}, bf16[256,1,128]{2,0,1:T(8,128)(2,1)S(1)}, u32[]{:S(2)}, u32[]{:S(2)}) collective-permute-start(bf16[256,1,128]{2,0,1:T(8,128)(2,1)S(1)} %get-tuple-element.222), channel_id=1, source_target_pairs={{0,1},{1,2},{2,3},{3,4},{4,5},{5,6},{6,7},{7,8},{8,9},{9,10},{10,1... | collective-permute-start | bytes 196616 | tf_op jit(solution)/shard_map/while/body/eval_jaxpr/ppermute | solution.py:97
  296.1 7.0 %collective-permute-start = (s32[256]{0:T(256)S(1)}, s32[256]{0:T(256)S(1)}, u32[]{:S(2)}, u32[]{:S(2)}) collective-permute-start(s32[256]{0:T(256)S(1)} %get-tuple-element.224), channel_id=1, source_target_pairs={{0,1},{1,2},{2,3},{3,4},{4,5},{5,6},{6,7},{7,8},{8,9},{9,10},{10,1... | collective-permute-start | bytes 3080 | tf_op jit(solution)/shard_map/while/body/eval_jaxpr/ppermute | solution.py:97
  296.3 7.1 %collective-permute-start.2 = (bf16[256,1,128]{2,0,1:T(8,128)(2,1)S(1)}, bf16[256,1,128]{2,0,1:T(8,128)(2,1)S(1)}, u32[]{:S(2)}, u32[]{:S(2)}) collective-permute-start(bf16[256,1,128]{2,0,1:T(8,128)(2,1)S(1)} %get-tuple-element.221), channel_id=1, source_target_pairs={{0,1},{1,2},{2,3},{3,4},{4,5},{5,6},{6,7},{7,8},{8,9},{9,10},{10,1... | collective-permute-start | bytes 196616 | tf_op jit(solution)/shard_map/while/body/eval_jaxpr/ppermute | solution.py:97
  296.4 8.0 %collective-permute-start.3 = (bf16[256,1,128]{2,0,1:T(8,128)(2,1)S(1)}, bf16[256,1,128]{2,0,1:T(8,128)(2,1)S(1)}, u32[]{:S(2)}, u32[]{:S(2)}) collective-permute-start(bf16[256,1,128]{2,0,1:T(8,128)(2,1)S(1)} %get-tuple-element.222), channel_id=1, source_target_pairs={{0,1},{1,2},{2,3},{3,4},{4,5},{5,6},{6,7},{7,8},{8,9},{9,10},{10,1... | collective-permute-start | bytes 196616 | tf_op jit(solution)/shard_map/while/body/eval_jaxpr/ppermute | solution.py:97
  305.7 7.1 %collective-permute-start.2 = (bf16[256,1,128]{2,0,1:T(8,128)(2,1)S(1)}, bf16[256,1,128]{2,0,1:T(8,128)(2,1)S(1)}, u32[]{:S(2)}, u32[]{:S(2)}) collective-permute-start(bf16[256,1,128]{2,0,1:T(8,128)(2,1)S(1)} %get-tuple-element.221), channel_id=1, source_target_pairs={{0,1},{1,2},{2,3},{3,4},{4,5},{5,6},{6,7},{7,8},{8,9},{9,10},{10,1... | collective-permute-start | bytes 196616 | tf_op jit(solution)/shard_map/while/body/eval_jaxpr/ppermute | solution.py:97
  305.8 8.0 %collective-permute-start.3 = (bf16[256,1,128]{2,0,1:T(8,128)(2,1)S(1)}, bf16[256,1,128]{2,0,1:T(8,128)(2,1)S(1)}, u32[]{:S(2)}, u32[]{:S(2)}) collective-permute-start(bf16[256,1,128]{2,0,1:T(8,128)(2,1)S(1)} %get-tuple-element.222), channel_id=1, source_target_pairs={{0,1},{1,2},{2,3},{3,4},{4,5},{5,6},{6,7},{7,8},{8,9},{9,10},{10,1... | collective-permute-start | bytes 196616 | tf_op jit(solution)/shard_map/while/body/eval_jaxpr/ppermute | solution.py:97
  315.1 7.1 %collective-permute-start.2 = (bf16[256,1,128]{2,0,1:T(8,128)(2,1)S(1)}, bf16[256,1,128]{2,0,1:T(8,128)(2,1)S(1)}, u32[]{:S(2)}, u32[]{:S(2)}) collective-permute-start(bf16[256,1,128]{2,0,1:T(8,128)(2,1)S(1)} %get-tuple-element.221), channel_id=1, source_target_pairs={{0,1},{1,2},{2,3},{3,4},{4,5},{5,6},{6,7},{7,8},{8,9},{9,10},{10,1... | collective-permute-start | bytes 196616 | tf_op jit(solution)/shard_map/while/body/eval_jaxpr/ppermute | solution.py:97
  315.3 8.0 %collective-permute-start.3 = (bf16[256,1,128]{2,0,1:T(8,128)(2,1)S(1)}, bf16[256,1,128]{2,0,1:T(8,128)(2,1)S(1)}, u32[]{:S(2)}, u32[]{:S(2)}) collective-permute-start(bf16[256,1,128]{2,0,1:T(8,128)(2,1)S(1)} %get-tuple-element.222), channel_id=1, source_target_pairs={{0,1},{1,2},{2,3},{3,4},{4,5},{5,6},{6,7},{7,8},{8,9},{9,10},{10,1... | collective-permute-start | bytes 196616 | tf_op jit(solution)/shard_map/while/body/eval_jaxpr/ppermute | solution.py:97
  324.4 7.0 %collective-permute-start.1 = (s32[256]{0:T(256)S(1)}, s32[256]{0:T(256)S(1)}, u32[]{:S(2)}, u32[]{:S(2)}) collective-permute-start(s32[256]{0:T(256)S(1)} %get-tuple-element.223), channel_id=1, source_target_pairs={{0,1},{1,2},{2,3},{3,4},{4,5},{5,6},{6,7},{7,8},{8,9},{9,10},{10,1... | collective-permute-start | bytes 3080 | tf_op jit(solution)/shard_map/while/body/eval_jaxpr/ppermute | solution.py:97
  324.6 7.1 %collective-permute-start.2 = (bf16[256,1,128]{2,0,1:T(8,128)(2,1)S(1)}, bf16[256,1,128]{2,0,1:T(8,128)(2,1)S(1)}, u32[]{:S(2)}, u32[]{:S(2)}) collective-permute-start(bf16[256,1,128]{2,0,1:T(8,128)(2,1)S(1)} %get-tuple-element.221), channel_id=1, source_target_pairs={{0,1},{1,2},{2,3},{3,4},{4,5},{5,6},{6,7},{7,8},{8,9},{9,10},{10,1... | collective-permute-start | bytes 196616 | tf_op jit(solution)/shard_map/while/body/eval_jaxpr/ppermute | solution.py:97
  324.7 8.0 %collective-permute-start.3 = (bf16[256,1,128]{2,0,1:T(8,128)(2,1)S(1)}, bf16[256,1,128]{2,0,1:T(8,128)(2,1)S(1)}, u32[]{:S(2)}, u32[]{:S(2)}) collective-permute-start(bf16[256,1,128]{2,0,1:T(8,128)(2,1)S(1)} %get-tuple-element.222), channel_id=1, source_target_pairs={{0,1},{1,2},{2,3},{3,4},{4,5},{5,6},{6,7},{7,8},{8,9},{9,10},{10,1... | collective-permute-start | bytes 196616 | tf_op jit(solution)/shard_map/while/body/eval_jaxpr/ppermute | solution.py:97
  (69 other events, 485.3 us)
where the time goes:
time: 435 us; the launch traced here: 430 us
  waiting for transfers between devices  184 us (42%)
  matrix products  157 us (36%)
  starting transfers between devices  33.9 us (8%)
  other arithmetic  26.4 us (6%)
  local copies, waits for them, and re-layouts  23.3 us (5%)
    ppermute x124, waiting for transfers between devices, remote_step(): held = lax.ppermute(held, 'cp', shift)  184 us
    ppermute x124, starting transfers between devices, remote_step(): held = lax.ppermute(held, 'cp', shift)  33.9 us
    dot_general x32, matrix products, attend_block(): jnp.einsum('grtu,ugd->grtd', prob_w.astype(jnp.bfloat16), v_block, prefer...  31.9 us
    dot_general x1, matrix products, finish_rows(): up_val = jnp.dot(normed, w_up, preferred_element_type=jnp.float32)  27.3 us
    dot_general x1, matrix products, finish_rows(): jnp.dot(hidden, w_down, preferred_element_type=jnp.float32)  27.2 us
    dot_general x1, matrix products, finish_rows(): gate = jnp.dot(normed, w_gate, preferred_element_type=jnp.float32)  26.9 us
    dot_general x1, local copies, waits for them, and re-layouts, project_rows(): jnp.dot(normed, w_q, preferred_element_type=jnp.float32)  21.3 us
    reduce_sum x32, other arithmetic, attend_block(): l_new = l_run * rescale + jnp.sum(prob_w, axis=-1)  16.5 us
  transfers between devices with their start and end apart: 124, of which 61 were waited for; matrix products, arithmetic and copies ran while one was open for 8% of the time, Pallas kernels for 0%

commit v1 on v0

v1 whole, which is shorter than its diff:
```python
import functools
import math

import jax
import jax.numpy as jnp
from jax import lax
from jax.experimental import pallas as pl
from jax.experimental.pallas import tpu as pltpu
from jax.sharding import PartitionSpec as P

HEAD_DIM = 128
ROPE_THETA = 500000.0
ROPE_FACTOR = 8.0
LOW_FREQ = 1.0
HIGH_FREQ = 4.0
ORIG_CTX = 8192.0
NORM_EPS = 1e-5
NEG_BIG = -1e30
SCORE_LOG2 = HEAD_DIM ** -0.5 * math.log2(math.e)
MESH = pl.DeviceIdType.MESH
COLS = 512
SLOTS = 10
OWNERS = 4
LANES = 256
F32 = jnp.float32
BF16 = jnp.bfloat16


def rope_freqs():
    exponent = jnp.arange(0, HEAD_DIM, 2).astype(F32) / HEAD_DIM
    inv_freq = 1.0 / (ROPE_THETA ** exponent)
    wavelen = 2.0 * jnp.pi / inv_freq
    smooth = jnp.clip((ORIG_CTX / wavelen - LOW_FREQ) / (HIGH_FREQ - LOW_FREQ), 0.0, 1.0)
    return (1.0 - smooth) * inv_freq / ROPE_FACTOR + smooth * inv_freq


def fdot(lhs, rhs):
    return jnp.dot(lhs, rhs, preferred_element_type=F32)


def norm_rows(src_ref, dst_ref, gain_ref, row, count):
    depth = src_ref.shape[1]
    rows = pl.ds(row, count)
    total = jnp.zeros((count, 128), F32)
    for col in range(0, depth, 128):
        part = src_ref[rows, col:col + 128].astype(F32)
        total = total + part * part
    inv_rms = lax.rsqrt(jnp.sum(total, axis=1, keepdims=True) / depth + NORM_EPS)
    for col in range(0, depth, 512):
        part = src_ref[rows, col:col + 512].astype(F32)
        gain = gain_ref[:, col:col + 512].astype(F32)
        dst_ref[rows, col:col + 512] = (part * inv_rms * gain).astype(BF16)


def project_kernel(x_hbm, gain_ref, cos_ref, sin_ref, wq_hbm, wk_hbm, wv_hbm, qt_ref, kv_ref, kc_ref, vc_ref, x_buf, a_buf, wkv_buf, wq_buf, x_sem, wkv_sem, wq_sem):
    count, depth = x_buf.shape
    piece = count // 2
    heads = wq_hbm.shape[1] // HEAD_DIM
    half_depth = depth // 2
    blocks = x_sem.shape[0]
    rows_blk = count // blocks

    def x_copy(idx):
        rows = pl.ds(idx * rows_blk, rows_blk)
        return pltpu.make_async_copy(x_hbm.at[rows], x_buf.at[rows], x_sem.at[idx])

    for idx in range(blocks):
        x_copy(idx).start()
    wkv = [pltpu.make_async_copy(src, wkv_buf.at[:, idx * HEAD_DIM:(idx + 1) * HEAD_DIM], wkv_sem.at[idx]) for idx, src in enumerate((wk_hbm, wv_hbm))]
    for copy in wkv:
        copy.start()
    wq_copies = []
    for col in range(wq_hbm.shape[1] // COLS):
        for part in range(2):
            slot = 2 * col + part
            copy = pltpu.make_async_copy(wq_hbm.at[pl.ds(part * half_depth, half_depth), pl.ds(col * COLS, COLS)], wq_buf.at[slot], wq_sem.at[slot])
            copy.start()
            wq_copies.append(copy)

    @pl.loop(0, blocks)
    def _(idx):
        x_copy(idx).wait()
        norm_rows(x_buf, a_buf, gain_ref, pl.multiple_of(idx * rows_blk, rows_blk), rows_blk)

    for copy in wkv:
        copy.wait()
    kv_raw = fdot(a_buf[...], wkv_buf[...])
    cos_t = cos_ref[...]
    sin_t = sin_ref[...]

    def rope(raw):
        return raw * cos_t + pltpu.roll(raw, HEAD_DIM // 2, 1) * sin_t

    k_rot = rope(kv_raw[:, :HEAD_DIM])
    v_raw = kv_raw[:, HEAD_DIM:]
    kc_ref[...] = k_rot.astype(BF16)
    vc_ref[...] = v_raw.astype(BF16)
    for half in range(2):
        rows = slice(half * piece, (half + 1) * piece)
        kv_ref[half] = k_rot[rows].astype(BF16)
        kv_ref[2 + half] = v_raw[rows].T.astype(BF16)

    for col in range(wq_hbm.shape[1] // COLS):
        wq_copies[2 * col].wait()
        wq_copies[2 * col + 1].wait()
        q_raw = fdot(a_buf[:, :half_depth], wq_buf[2 * col]) + fdot(a_buf[:, half_depth:], wq_buf[2 * col + 1])
        for sub in range(COLS // HEAD_DIM):
            head = col * (COLS // HEAD_DIM) + sub
            q_rot = rope(q_raw[:, sub * HEAD_DIM:(sub + 1) * HEAD_DIM])
            for half in range(2):
                qt_ref[half, :, head * piece:(head + 1) * piece] = q_rot[half * piece:(half + 1) * piece].T.astype(BF16)


def gather_shards(side, kv_ref, all_ref, send_sem, recv_sem):
    me = lax.axis_index('cp')
    core = lax.rem(me, 2)
    chip = me // 2
    chip_x = lax.rem(chip, side)
    chip_y = chip // side

    def owner(first, second):
        pos_x = lax.rem(chip_x + first * (1 - core) + second * core + 2 * side, side)
        pos_y = lax.rem(chip_y + first * core + second * (1 - core) + 2 * side, side)
        return (pos_y * side + pos_x) * 2 + core

    sibling = me + 1 - 2 * core
    targets = {'a+': owner(1, 0), 'a-': owner(-1, 0), 'b+': owner(0, 1), 'b-': owner(0, -1), 's': sibling}
    barrier = pltpu.get_barrier_semaphore()
    for target in targets.values():
        pl.semaphore_signal(barrier, inc=1, device_id={'cp': target}, device_id_type=MESH)
    pl.semaphore_wait(barrier, len(targets))

    copies = []

    def send(shard, where, half=None):
        num = len(copies)
        dst = all_ref.at[shard]
        src = kv_ref if num < 5 else dst
        if half is not None:
            dst = dst.at[pl.ds(2 * half, 2)]
            src = dst
        copy = pltpu.make_async_remote_copy(src_ref=src, dst_ref=dst, send_sem=send_sem.at[num], recv_sem=recv_sem.at[num], device_id={'cp': targets[where]}, device_id_type=MESH)
        copy.start()
        copies.append(copy)
        return copy

    from_sibling = []

    def spread(shard):
        plus = send(shard, 'b+')
        minus = send(shard, 'b-')
        from_sibling.append(send(shard, 's'))
        return plus, minus

    own_right = send(me, 'a+')
    own_left = send(me, 'a-')
    row_own = spread(me)
    all_ref[me] = kv_ref[...]
    own_right.wait_recv()
    shard = owner(-1, 0)
    far_k = send(shard, 'a+', 0)
    row_left = spread(shard)
    own_left.wait_recv()
    shard = owner(1, 0)
    far_v = send(shard, 'a-', 1)
    row_right = spread(shard)

    def relay(first, row):
        row[0].wait_recv()
        shard = owner(first, -1)
        half_k = send(shard, 'b+', 0)
        from_sibling.append(send(shard, 's'))
        row[1].wait_recv()
        shard = owner(first, 1)
        half_v = send(shard, 'b-', 1)
        from_sibling.append(send(shard, 's'))
        return half_k, half_v

    def close(first, halves):
        halves[0].wait_recv()
        halves[1].wait_recv()
        from_sibling.append(send(owner(first, 2), 's'))

    far_own = relay(0, row_own)
    far_k.wait_recv()
    far_v.wait_recv()
    row_far = spread(owner(2, 0))
    far_left = relay(-1, row_left)
    far_right = relay(1, row_right)
    close(0, far_own)
    far_far = relay(2, row_far)
    close(-1, far_left)
    close(1, far_right)
    close(2, far_far)
    for copy in from_sibling:
        copy.wait_recv()
    for copy in copies:
        copy.wait_send()


NUM_COPIES = 36


def attend_kernel(cp_size, side, kv_ref, qt_ref, pos_ref, out_ref, all_ref, max_ref, sum_ref, acc_ref, send_sem, recv_sem):
    gather_shards(side, kv_ref, all_ref, send_sem, recv_sem)
    me = lax.axis_index('cp')
    piece = kv_ref.shape[1]
    width = qt_ref.shape[2]
    tiles = width // LANES
    bases = (me * piece, (2 * cp_size - 1 - me) * piece)
    lane_tok = lax.broadcasted_iota(jnp.int32, (1, piece), 1)

    def starts(half):
        first = bases[half] + lane_tok - pos_ref[half]
        return jnp.concatenate([first] * (LANES // piece), axis=1)

    first_key = (starts(0), starts(1))
    tok = jnp.concatenate([lane_tok] * (LANES // piece), axis=1)
    key_row = lax.broadcasted_iota(jnp.int32, (piece, LANES), 0)

    for half in range(2):
        visible = (key_row <= tok) & (key_row + bases[half] >= first_key[half])
        for tile in range(tiles):
            cols = slice(tile * LANES, (tile + 1) * LANES)
            scores = fdot(kv_ref[half], qt_ref[half, :, cols])
            scores = jnp.where(visible, scores, NEG_BIG)
            top = jnp.max(scores, axis=0, keepdims=True)
            prob = jnp.exp2((scores - top) * SCORE_LOG2)
            max_ref[half, :, cols] = top
            sum_ref[half, :, cols] = jnp.sum(prob, axis=0, keepdims=True)
            acc_ref[half, :, cols] = fdot(kv_ref[2 + half], prob.astype(BF16))

    def chunk(half, part, idx):
        first = idx * OWNERS
        key_base = []
        for sub in range(OWNERS):
            own = first + sub
            if part == 0:
                base = own * piece
                base = base if half == 1 else jnp.where(own < me, base, -2 * piece)
            else:
                base = jnp.where(own > me, (2 * cp_size - 1 - own) * piece, -2 * piece)
            key_base.append(base)
        keys = all_ref[pl.ds(first, OWNERS), part].reshape(OWNERS * piece, HEAD_DIM)
        vals = jnp.concatenate([all_ref[first + sub, 2 + part] for sub in range(OWNERS)], axis=1)
        for tile in range(tiles):
            cols = slice(tile * LANES, (tile + 1) * LANES)
            raw = fdot(keys, qt_ref[half, :, cols])
            scores = [jnp.where(key_row >= first_key[half] - key_base[sub], raw[sub * piece:(sub + 1) * piece], NEG_BIG) for sub in range(OWNERS)]
            old_top = max_ref[half, :, cols]
            peak = functools.reduce(jnp.maximum, scores)
            top = jnp.maximum(old_top, jnp.max(peak, axis=0, keepdims=True))
            probs = [jnp.exp2((score - top) * SCORE_LOG2) for score in scores]
            scale = jnp.exp2((old_top - top) * SCORE_LOG2)
            max_ref[half, :, cols] = top
            sum_ref[half, :, cols] = sum_ref[half, :, cols] * scale + jnp.sum(functools.reduce(jnp.add, probs), axis=0, keepdims=True)
            prob = jnp.concatenate([part_p.astype(BF16) for part_p in probs], axis=0)
            acc_ref[half, :, cols] = acc_ref[half, :, cols] * scale + fdot(vals, prob)

    @pl.loop(0, cp_size // OWNERS)
    def _(idx):
        chunk(1, 0, idx)

    @pl.loop(0, (me + OWNERS - 1) // OWNERS)
    def _(idx):
        chunk(0, 0, idx)

    @pl.loop((me + 1) // OWNERS, cp_size // OWNERS)
    def _(idx):
        chunk(1, 1, idx)

    for half in range(2):
        for head in range(width // piece):
            cols = slice(head * piece, (head + 1) * piece)
            done = acc_ref[half, :, cols] / sum_ref[half, :, cols]
            out_ref[half * piece:(half + 1) * piece, head * HEAD_DIM:(head + 1) * HEAD_DIM] = done.T.astype(BF16)


def finish_kernel(x_hbm, attn_ref, gain_ref, wo_hbm, wg_hbm, wu_hbm, wd_hbm, z_hbm, h_buf, b_buf, m_buf, z_buf, slots, x_sem, slot_sem, z_sem):
    count, depth = h_buf.shape
    slot_rows = slots.shape[1]
    attn_w = attn_ref.shape[1]
    stack = slot_rows // attn_w
    ff = wg_hbm.shape[1]
    n_wo = depth // COLS // stack
    n_ff = ff // COLS
    n_dn = depth // COLS
    up_from = n_wo
    dn_from = n_wo + 4 * n_ff
    total = dn_from + n_dn

    def col(idx):
        return pl.ds(pl.multiple_of(idx * COLS, COLS), COLS)

    def issue(num):
        slot = lax.rem(num, SLOTS)
        sem = slot_sem.at[slot]

        @pl.when(num < up_from)
        def _():
            for sub in range(stack):
                pltpu.make_async_copy(wo_hbm.at[:, col(num * stack + sub)], slots.at[slot, pl.ds(sub * attn_w, attn_w)], sem).start()

        rel = num - up_from
        blk = rel // 4
        kind = lax.rem(rel, 4)
        rows = pl.ds(pl.multiple_of(lax.rem(kind, 2) * slot_rows, slot_rows), slot_rows)

        @pl.when((num >= up_from) & (num < dn_from) & (kind < 2))
        def _():
            pltpu.make_async_copy(wg_hbm.at[rows, col(blk)], slots.at[slot], sem).start()

        @pl.when((num >= up_from) & (num < dn_from) & (kind >= 2))
        def _():
            pltpu.make_async_copy(wu_hbm.at[rows, col(blk)], slots.at[slot], sem).start()

        @pl.when((num >= dn_from) & (num < total))
        def _():
            pltpu.make_async_copy(wd_hbm.at[:, col(num - dn_from)], slots.at[slot, pl.ds(0, ff)], sem).start()

    def take(num, rows):
        slot = lax.rem(num, SLOTS)
        part = slots.at[slot, pl.ds(0, rows)]
        pltpu.make_async_copy(part, part, slot_sem.at[slot]).wait()
        return slots.at[slot]

    x_copy = pltpu.make_async_copy(x_hbm, h_buf, x_sem)
    x_copy.start()
    for num in range(SLOTS):
        issue(jnp.int32(num))
    x_copy.wait()

    @pl.loop(0, n_wo)
    def _(num):
        slot = take(num, slot_rows)
        for sub in range(stack):
            cols = col(num * stack + sub)
            out = fdot(attn_ref[...], slot[sub * attn_w:(sub + 1) * attn_w])
            h_buf[:, cols] = (h_buf[:, cols].astype(F32) + out).astype(BF16)
        issue(num + SLOTS)

    @pl.loop(0, count // 32)
    def _(idx):
        norm_rows(h_buf, b_buf, gain_ref, pl.multiple_of(idx * 32, 32), 32)

    @pl.loop(0, n_ff)
    def _(blk):
        first = up_from + 4 * blk

        def product(num):
            low = take(num, slot_rows)
            res = fdot(b_buf[:, :slot_rows], low[...])
            high = take(num + 1, slot_rows)
            return res + fdot(b_buf[:, slot_rows:], high[...])

        gate = product(first)
        issue(first + SLOTS)
        issue(first + 1 + SLOTS)
        up_val = product(first + 2)
        issue(first + 2 + SLOTS)
        issue(first + 3 + SLOTS)
        m_buf[:, col(blk)] = (gate * jax.nn.sigmoid(gate) * up_val).astype(BF16)

    def z_copy(blk):
        slot = lax.rem(blk, 2)
        return pltpu.make_async_copy(z_buf.at[slot], z_hbm.at[:, col(blk)], z_sem.at[slot])

    @pl.loop(0, n_dn)
    def _(blk):
        num = dn_from + blk
        slot = take(num, ff)
        out = fdot(m_buf[...], slot[:ff])

        @pl.when(blk >= 2)
        def _():
            z_copy(blk - 2).wait()

        z_buf[lax.rem(blk, 2)] = (h_buf[:, col(blk)].astype(F32) + out).astype(BF16)
        z_copy(blk).start()
        issue(num + SLOTS)

    z_copy(n_dn - 2).wait()
    z_copy(n_dn - 1).wait()


def solution(mesh):
    cp_size = mesh.shape['cp']
    side = math.isqrt(cp_size // 2)
    vmem = pl.BlockSpec(memory_space=pltpu.VMEM)
    hbm = pl.BlockSpec(memory_space=pl.ANY)
    dma = pltpu.SemaphoreType.DMA
    limit = 60 * 1024 * 1024

    def device_fn(x_loc, seg_loc, pos_loc, attn_gain, w_q, w_k, w_v, w_o, mlp_gain, w_gate, w_up, w_down):
        rows = x_loc[0]
        count, depth = rows.shape
        piece = count // 2
        width = w_q.shape[1] // HEAD_DIM * piece
        ff = w_gate.shape[1]
        angles = pos_loc.astype(F32)[:, None] * rope_freqs()[None, :]
        cos_t = jnp.cos(angles)
        sin_t = jnp.sin(angles)
        cos_t = jnp.concatenate([cos_t, cos_t], axis=1)
        sin_t = jnp.concatenate([-sin_t, sin_t], axis=1)
        q_t, kv, k_rows, v_rows = pl.pallas_call(
            project_kernel,
            out_shape=(jax.ShapeDtypeStruct((2, HEAD_DIM, width), BF16), jax.ShapeDtypeStruct((4, piece, HEAD_DIM), BF16), jax.ShapeDtypeStruct((count, HEAD_DIM), BF16), jax.ShapeDtypeStruct((count, HEAD_DIM), BF16)),
            in_specs=[hbm, vmem, vmem, vmem, hbm, hbm, hbm],
            out_specs=(vmem, vmem, vmem, vmem),
            scratch_shapes=[pltpu.VMEM((count, depth), BF16), pltpu.VMEM((count, depth), BF16), pltpu.VMEM((depth, 2 * HEAD_DIM), BF16), pltpu.VMEM((2 * w_q.shape[1] // COLS, depth // 2, COLS), BF16), dma((count // 32,)), dma((2,)), dma((2 * w_q.shape[1] // COLS,))],
            compiler_params=pltpu.CompilerParams(vmem_limit_bytes=limit),
            name='project',
        )(rows, attn_gain.reshape(1, depth), cos_t, sin_t, w_q, w_k, w_v)
        attn_rows = pl.pallas_call(
            functools.partial(attend_kernel, cp_size, side),
            out_shape=jax.ShapeDtypeStruct((count, w_q.shape[1]), BF16),
            in_specs=[vmem, vmem, vmem],
            out_specs=vmem,
            scratch_shapes=[pltpu.VMEM((cp_size, 4, piece, HEAD_DIM), BF16), pltpu.VMEM((2, 1, width), F32), pltpu.VMEM((2, 1, width), F32), pltpu.VMEM((2, HEAD_DIM, width), F32), dma((NUM_COPIES,)), dma((NUM_COPIES,))],
            compiler_params=pltpu.CompilerParams(vmem_limit_bytes=limit, collective_id=0, has_side_effects=True),
            name='attend',
        )(kv, q_t, pos_loc.reshape(2, 1, piece))
        z_rows = pl.pallas_call(
            finish_kernel,
            out_shape=jax.ShapeDtypeStruct((count, depth), BF16),
            in_specs=[hbm, vmem, vmem, hbm, hbm, hbm, hbm],
            out_specs=hbm,
            scratch_shapes=[pltpu.VMEM((count, depth), BF16), pltpu.VMEM((count, depth), BF16), pltpu.VMEM((count, ff), BF16), pltpu.VMEM((2, count, COLS), BF16), pltpu.VMEM((SLOTS, depth // 2, COLS), BF16), dma(()), dma((SLOTS,)), dma((2,))],
            compiler_params=pltpu.CompilerParams(vmem_limit_bytes=limit),
            name='finish',
        )(rows, attn_rows, mlp_gain.reshape(1, depth), w_o, w_gate, w_up, w_down)
        return z_rows[None], k_rows[:, None, :], v_rows[:, None, :]

    seq_spec = P(('dp', 'cp'))
    return jax.shard_map(device_fn, mesh=mesh, in_specs=(P('dp', 'cp', None), seq_spec, seq_spec, P(), P(), P(), P(), P(), P(), P(), P(), P()), out_specs=(P('dp', 'cp', None), P(('dp', 'cp'), None, None), P(('dp', 'cp'), None, None)), check_vma=False)
```

time: 435 us -> 165 us (0.38); the launches traced: 430 us -> 164 us
  waiting for transfers between devices: 184 us -> 0 us
  Pallas kernels: 0 us -> 159 us
  matrix products: 157 us -> 0 us
  starting transfers between devices: 33.9 us -> 0 us
  other arithmetic: 26.4 us -> 2.06 us
  local copies, waits for them, and re-layouts: 23.3 us -> 2.69 us
    ppermute x124 -> x0, waiting for transfers between devices: 184 us -> none  [remote_step(): held = lax.ppermute(held, 'cp', shift)]
    pallas_call x0 -> x3, Pallas kernels: none -> 159 us  [the longest x1 80.1 us: device_fn(): pl.pallas_call(finish_kernel, out_shape=jax.ShapeDtypeStruct((count, dept...]
    dot_general x71 -> x0, matrix products: 157 us -> none  [the longest x32 31.9 us: attend_block(): jnp.einsum('grtu,ugd->grtd', prob_w.astype(jnp.bfloat16), v_block, prefer...]
    ppermute x124 -> x0, starting transfers between devices: 33.9 us -> none  [remote_step(): held = lax.ppermute(held, 'cp', shift)]
    dot_general x1 -> x0, local copies, waits for them, and re-layouts: 21.3 us -> none  [project_rows(): jnp.dot(normed, w_q, preferred_element_type=jnp.float32)]
    reduce_sum x33 -> x0, other arithmetic: 19.6 us -> none  [the longest x32 16.5 us: attend_block(): l_new = l_run * rescale + jnp.sum(prob_w, axis=-1)]
  transfers between devices with their start and end apart: 124 -> 0, of which waited for: 61 -> 0; matrix products, arithmetic and copies ran while one was open for 8% -> 0% of each run, Pallas kernels for 0% -> 0%
where the time goes in v1:
time: 165 us; the launch traced here: 164 us
  Pallas kernels  159 us (96%)
  local copies, waits for them, and re-layouts  2.69 us (2%)
  other arithmetic  2.06 us (1%)
    pallas_call x1, Pallas kernels, device_fn(): pl.pallas_call(finish_kernel, out_shape=jax.ShapeDtypeStruct((count, dept...  80.1 us
    pallas_call x1, Pallas kernels, device_fn(): pl.pallas_call(functools.partial(attend_kernel, cp_size, side), out_shape...  58.9 us
    pallas_call x1, Pallas kernels, device_fn(): pl.pallas_call(project_kernel, out_shape=(jax.ShapeDtypeStruct((2, HEAD_D...  19.8 us

profile of v1, /device:TPU:97, one launch (start us, length us, event | category | flops | bytes accessed | tf_op | source)
XLA Modules:
  0.0 164.3 jit_solution(2417401717625160735)
XLA Ops:
  0.6 0.7 convert_element_type.10
  1.3 1.4 reshape.34.gain_ref
  2.7 1.3 reshape.36.gain_ref
  4.0 0.5 fusion
  4.6 0.8 pad_maximum_fusion
  5.4 19.8 %project.1 = (bf16[2,128,1024]{2,1,0:T(8,128)(2,1)}, bf16[4,128,128]{2,1,0:T(8,128)(2,1)}, bf16[256,128]{1,0:T(8,128)(2,1)}, bf16[256,128]{1,0:T(8,128)(2,1)}) custom-call(bf16[256,8192]{1,0:T(8,128)(2,1)} %bitcast.5, bf16[1,8192]{1,0:T(2,128)(2,1)} %reshape.34.gain_ref, f32[256,128]{1,0:T(8,128)} %get-tuple-element.14.cos_ref, ...), custom_call_target="tpu_custom_call" | custom-call | tf_op jit(solution)/shard_map/project/pallas_call | solution.py:405
  25.2 58.9 %attend.1.attn_ref = bf16[256,1024]{1,0:T(8,128)(2,1)} custom-call(bf16[4,128,128]{2,1,0:T(8,128)(2,1)} %get-tuple-element.7.kv_ref, bf16[2,128,1024]{2,1,0:T(8,128)(2,1)} %get-tuple-element.8.qt_ref, s32[2,1,128]{2,1,0:T(1,128)} %bitcast.8), custom_call_target="tpu_custom_call" | custom-call | tf_op jit(solution)/shard_map/attend/pallas_call | solution.py:414
  84.1 80.1 %finish.1 = bf16[256,8192]{1,0:T(8,128)(2,1)} custom-call(bf16[256,8192]{1,0:T(8,128)(2,1)} %bitcast.6, bf16[256,1024]{1,0:T(8,128)(2,1)} %attend.1.attn_ref, bf16[1,8192]{1,0:T(2,128)(2,1)} %reshape.36.gain_ref, bf16[1024,8192]{1,0:T(8,128)(2,1)} %wo_hbm.1, bf16[8192,3584]{1,0:T(8,128)(2,1)} %wg_hbm.1, bf16[8192,3584]{1,0:T(8,128)(2,1)} %wu_hbm.1, ...), custom_call_target="tpu_custom_call" | custom-call | tf_op jit(solution)/shard_map/finish/pallas_call | solution.py:423
  (1 shorter events, 0.0 us)

commit v2 on v1

v2 whole, which is shorter than its diff:
```python
import functools
import math

import jax
import jax.numpy as jnp
import numpy as np
from jax import lax
from jax.experimental import pallas as pl
from jax.experimental.pallas import tpu as pltpu
from jax.sharding import PartitionSpec as P

HEAD_DIM = 128
ROPE_THETA = 500000.0
ROPE_FACTOR = 8.0
LOW_FREQ = 1.0
HIGH_FREQ = 4.0
ORIG_CTX = 8192.0
NORM_EPS = 1e-5
NEG_BIG = -1e30
SCORE_LOG2 = HEAD_DIM ** -0.5 * math.log2(math.e)
MESH = pl.DeviceIdType.MESH
COLS = 512
SLOTS = 8
SLOT_ROWS = 1024
SLOT_COLS = 2048
OWNERS = 4
LANES = 256
F32 = jnp.float32
BF16 = jnp.bfloat16


def rope_freqs():
    exponent = np.arange(0, HEAD_DIM, 2) / HEAD_DIM
    inv_freq = 1.0 / (ROPE_THETA ** exponent)
    wavelen = 2.0 * np.pi / inv_freq
    smooth = np.clip((ORIG_CTX / wavelen - LOW_FREQ) / (HIGH_FREQ - LOW_FREQ), 0.0, 1.0)
    return ((1.0 - smooth) * inv_freq / ROPE_FACTOR + smooth * inv_freq).astype(np.float32)


def fdot(lhs, rhs):
    return jnp.dot(lhs, rhs, preferred_element_type=F32)


def norm_rows(src_ref, dst_ref, gain_ref, row, count):
    depth = src_ref.shape[1]
    rows = pl.ds(row, count)
    total = jnp.zeros((count, 128), F32)
    for col in range(0, depth, 128):
        part = src_ref[rows, col:col + 128].astype(F32)
        total = total + part * part
    inv_rms = lax.rsqrt(jnp.sum(total, axis=1, keepdims=True) / depth + NORM_EPS)
    for col in range(0, depth, 512):
        part = src_ref[rows, col:col + 512].astype(F32)
        gain = gain_ref[col:col + 512].astype(F32).reshape(1, 512)
        dst_ref[rows, col:col + 512] = (part * inv_rms * gain).astype(BF16)


def project_kernel(x_hbm, gain_ref, pos_ref, freq_ref, wq_hbm, wk_hbm, wv_hbm, qt_ref, kv_ref, kc_ref, vc_ref, x_buf, a_buf, wk_buf, wv_buf, wq_buf, x_sem, wkv_sem, wq_sem):
    count, depth = x_buf.shape
    piece = count // 2
    blocks = x_sem.shape[0]
    rows_blk = count // blocks
    chunks = wq_buf.shape[0]
    chunk_rows = wq_buf.shape[1]

    def x_copy(idx):
        rows = pl.ds(idx * rows_blk, rows_blk)
        return pltpu.make_async_copy(x_hbm.at[rows], x_buf.at[rows], x_sem.at[idx])

    for idx in range(blocks):
        x_copy(idx).start()
    wkv = [pltpu.make_async_copy(wk_hbm, wk_buf, wkv_sem.at[0]), pltpu.make_async_copy(wv_hbm, wv_buf, wkv_sem.at[1])]
    for copy in wkv:
        copy.start()
    wq_copies = [pltpu.make_async_copy(wq_hbm.at[pl.ds(idx * chunk_rows, chunk_rows)], wq_buf.at[idx], wq_sem.at[idx]) for idx in range(chunks)]
    for copy in wq_copies:
        copy.start()

    cos_t, sin_t = rope_tables(pos_ref, freq_ref)

    @pl.loop(0, blocks)
    def _(idx):
        x_copy(idx).wait()
        norm_rows(x_buf, a_buf, gain_ref, pl.multiple_of(idx * rows_blk, rows_blk), rows_blk)

    for copy in wkv:
        copy.wait()
    kv_raw = fdot(a_buf[...], jnp.concatenate([wk_buf[...], wv_buf[...]], axis=1))

    def rope(raw):
        return raw * cos_t + pltpu.roll(raw, HEAD_DIM // 2, 1) * sin_t

    k_rot = rope(kv_raw[:, :HEAD_DIM])
    v_raw = kv_raw[:, HEAD_DIM:]
    kc_ref[...] = k_rot.astype(BF16)
    vc_ref[...] = v_raw.astype(BF16)
    for half in range(2):
        rows = slice(half * piece, (half + 1) * piece)
        kv_ref[half] = k_rot[rows].astype(BF16)
        kv_ref[2 + half] = v_raw[rows].T.astype(BF16)

    for copy in wq_copies:
        copy.wait()
    for col in range(wq_hbm.shape[1] // COLS):
        q_raw = fdot(a_buf[...], jnp.concatenate([wq_buf[idx, :, col * COLS:(col + 1) * COLS] for idx in range(chunks)], axis=0))
        for sub in range(COLS // HEAD_DIM):
            head = col * (COLS // HEAD_DIM) + sub
            q_rot = rope(q_raw[:, sub * HEAD_DIM:(sub + 1) * HEAD_DIM])
            for half in range(2):
                qt_ref[half, :, head * piece:(head + 1) * piece] = q_rot[half * piece:(half + 1) * piece].T.astype(BF16)


def rope_tables(pos_ref, freq_ref):
    cos_parts, sin_parts = [], []
    for half in range(2):
        angles = freq_ref[...] * pos_ref[half].astype(F32)
        cos_parts.append(jnp.cos(angles).T)
        sin_parts.append(jnp.sin(angles).T)
    cos_h = jnp.concatenate(cos_parts, axis=0)
    sin_h = jnp.concatenate(sin_parts, axis=0)
    return jnp.concatenate([cos_h, cos_h], axis=1), jnp.concatenate([-sin_h, sin_h], axis=1)


def gather_shards(side, kv_ref, all_ref, send_sem, recv_sem, on_start, on_group):
    me = lax.axis_index('cp')
    core = lax.rem(me, 2)
    chip = me // 2
    chip_x = lax.rem(chip, side)
    chip_y = chip // side

    def owner(first, second, core=core):
        pos_x = lax.rem(chip_x + first * (1 - core) + second * core + 2 * side, side)
        pos_y = lax.rem(chip_y + first * core + second * (1 - core) + 2 * side, side)
        return (pos_y * side + pos_x) * 2 + core

    def other(first, second):
        return owner(first, second, 1 - core)

    sibling = me + 1 - 2 * core
    targets = {'a+': owner(1, 0), 'a-': owner(-1, 0), 'b+': owner(0, 1), 'b-': owner(0, -1), 's': sibling}
    barrier = pltpu.get_barrier_semaphore()
    for target in targets.values():
        pl.semaphore_signal(barrier, inc=1, device_id={'cp': target}, device_id_type=MESH)
    pl.semaphore_wait(barrier, len(targets))

    copies = []

    def send(shard, where, half=None):
        num = len(copies)
        dst = all_ref.at[shard]
        src = kv_ref if num < 5 else dst
        if half is not None:
            dst = dst.at[pl.ds(2 * half, 2)]
            src = dst
        copy = pltpu.make_async_remote_copy(src_ref=src, dst_ref=dst, send_sem=send_sem.at[num], recv_sem=recv_sem.at[num], device_id={'cp': targets[where]}, device_id_type=MESH)
        copy.start()
        copies.append(copy)
        return copy

    from_sibling = []

    def spread(shard):
        plus = send(shard, 'b+')
        minus = send(shard, 'b-')
        from_sibling.append(send(shard, 's'))
        return plus, minus

    own_right = send(me, 'a+')
    own_left = send(me, 'a-')
    row_own = spread(me)
    all_ref[me] = kv_ref[...]
    on_start()
    own_right.wait_recv()
    shard = owner(-1, 0)
    far_k = send(shard, 'a+', 0)
    row_left = spread(shard)
    own_left.wait_recv()
    shard = owner(1, 0)
    far_v = send(shard, 'a-', 1)
    row_right = spread(shard)

    def relay(first, row):
        row[0].wait_recv()
        shard = owner(first, -1)
        half_k = send(shard, 'b+', 0)
        from_sibling.append(send(shard, 's'))
        row[1].wait_recv()
        shard = owner(first, 1)
        half_v = send(shard, 'b-', 1)
        from_sibling.append(send(shard, 's'))
        return half_k, half_v

    def close(first, halves):
        halves[0].wait_recv()
        halves[1].wait_recv()
        from_sibling.append(send(owner(first, 2), 's'))

    def arrived(*nums):
        for num in nums:
            from_sibling[num].wait_recv()

    arrived(0)
    on_group(me, sibling, owner(-1, 0), owner(1, 0))
    far_own = relay(0, row_own)
    far_k.wait_recv()
    far_v.wait_recv()
    row_far = spread(owner(2, 0))
    arrived(1, 2)
    on_group(owner(0, -1), owner(0, 1), other(-1, 0), other(1, 0))
    far_left = relay(-1, row_left)
    far_right = relay(1, row_right)
    arrived(3, 4)
    on_group(owner(2, 0), owner(-1, -1), other(0, -1), other(0, 1))
    close(0, far_own)
    far_far = relay(2, row_far)
    arrived(5)
    on_group(owner(-1, 1), owner(1, -1), owner(1, 1), other(2, 0))
    close(-1, far_left)
    close(1, far_right)
    arrived(6, 7)
    on_group(owner(0, 2), owner(2, -1), other(-1, -1), other(-1, 1))
    close(2, far_far)
    arrived(8, 9)
    on_group(owner(2, 1), owner(-1, 2), other(1, -1), other(1, 1))
    arrived(10, 11)
    on_group(owner(1, 2), owner(2, 2), other(0, 2), other(2, -1))
    arrived(12, 13, 14, 15)
    on_group(other(2, 1), other(-1, 2), other(1, 2), other(2, 2))
    for copy in copies:
        copy.wait_send()


NUM_COPIES = 36


def attend_kernel(cp_size, side, kv_ref, qt_ref, pos_ref, out_ref, all_ref, max_ref, sum_ref, acc_ref, score_ref, send_sem, recv_sem):
    me = lax.axis_index('cp')
    piece = kv_ref.shape[1]
    width = qt_ref.shape[2]
    tiles = width // LANES
    bases = (me * piece, (2 * cp_size - 1 - me) * piece)
    lane_tok = lax.broadcasted_iota(jnp.int32, (1, piece), 1)

    def starts(half):
        first = bases[half] + lane_tok - pos_ref[half]
        return jnp.concatenate([first] * (LANES // piece), axis=1)

    first_key = (starts(0), starts(1))
    tok = jnp.concatenate([lane_tok] * (LANES // piece), axis=1)
    key_row = lax.broadcasted_iota(jnp.int32, (piece, LANES), 0)

    def diagonal():
        for half in range(2):
            visible = (key_row <= tok) & (key_row + bases[half] >= first_key[half])
            for tile in range(tiles):
                cols = slice(tile * LANES, (tile + 1) * LANES)
                scores = fdot(kv_ref[half], qt_ref[half, :, cols])
                scores = jnp.where(visible, scores, NEG_BIG)
                top = jnp.max(scores, axis=0, keepdims=True)
                prob = jnp.exp2((scores - top) * SCORE_LOG2)
                max_ref[half, :, cols] = top
                sum_ref[half, :, cols] = jnp.sum(prob, axis=0, keepdims=True)
                acc_ref[half, :, cols] = fdot(kv_ref[2 + half], prob.astype(BF16))

    def block(half, part, owners, key_base):
        keys = jnp.concatenate([all_ref[own, part] for own in owners], axis=0)
        vals = jnp.concatenate([all_ref[own, 2 + part] for own in owners], axis=1)
        hidden = [key_row < first_key[half] - base for base in key_base]
        tops, scales = [], []
        for tile in range(tiles):
            cols = slice(tile * LANES, (tile + 1) * LANES)
            raw = fdot(keys, qt_ref[half, :, cols])
            peak = None
            for sub in range(OWNERS):
                rows = slice(sub * piece, (sub + 1) * piece)
                score = jnp.where(hidden[sub], NEG_BIG, raw[rows])
                score_ref[rows, cols] = score
                best = jnp.max(score, axis=0, keepdims=True)
                peak = best if peak is None else jnp.maximum(peak, best)
            old_top = max_ref[half, :, cols]
            top = jnp.maximum(old_top, peak)
            max_ref[half, :, cols] = top
            tops.append(top)
            scales.append(jnp.exp2((old_top - top) * SCORE_LOG2))
        for tile in range(tiles):
            cols = slice(tile * LANES, (tile + 1) * LANES)
            prob = jnp.exp2((score_ref[:, cols] - tops[tile]) * SCORE_LOG2)
            sum_ref[half, :, cols] = sum_ref[half, :, cols] * scales[tile] + jnp.sum(prob, axis=0, keepdims=True)
            acc_ref[half, :, cols] = acc_ref[half, :, cols] * scales[tile] + fdot(vals, prob.astype(BF16))

    def low_group(*owners):
        block(1, 0, owners, [own * piece for own in owners])

    gather_shards(side, kv_ref, all_ref, send_sem, recv_sem, diagonal, low_group)

    @pl.loop(0, (me + OWNERS - 1) // OWNERS)
    def _(idx):
        owners = [idx * OWNERS + sub for sub in range(OWNERS)]
        block(0, 0, owners, [jnp.where(own < me, own * piece, -2 * piece) for own in owners])

    @pl.loop((me + 1) // OWNERS, cp_size // OWNERS)
    def _(idx):
        owners = [idx * OWNERS + sub for sub in range(OWNERS)]
        block(1, 1, owners, [jnp.where(own > me, (2 * cp_size - 1 - own) * piece, -2 * piece) for own in owners])

    for half in range(2):
        for head in range(width // piece):
            cols = slice(head * piece, (head + 1) * piece)
            done = acc_ref[half, :, cols] / sum_ref[half, :, cols]
            out_ref[half * piece:(half + 1) * piece, head * HEAD_DIM:(head + 1) * HEAD_DIM] = done.T.astype(BF16)


def finish_kernel(x_hbm, attn_ref, gain_ref, wo_hbm, wg_hbm, wu_hbm, wd_hbm, z_hbm, h_buf, b_buf, m_buf, acc_ref, z_buf, slots, x_sem, slot_sem, z_sem):
    count, depth = h_buf.shape
    ff = wg_hbm.shape[1]
    ff_half = ff // 2
    group = 4
    n_wo = depth // SLOT_COLS
    k_steps = depth // (SLOT_ROWS * group)
    n_ff = 4 * k_steps
    dn_rows = [min(SLOT_ROWS, ff - row) for row in range(0, ff, SLOT_ROWS)]
    n_dn = depth // SLOT_COLS
    ff_from = n_wo
    dn_from = ff_from + n_ff * group
    total = dn_from + n_dn * len(dn_rows)

    def cols_of(idx, size):
        return pl.ds(pl.multiple_of(idx * size, size), size)

    def issue(num):
        slot = lax.rem(num, SLOTS)
        sem = slot_sem.at[slot]
        dst = slots.at[slot]

        @pl.when(num < ff_from)
        def _():
            pltpu.make_async_copy(wo_hbm.at[:, cols_of(num, SLOT_COLS)], dst, sem).start()

        rel = num - ff_from
        step = rel // group
        half = step // (2 * k_steps)
        kind = lax.rem(step // k_steps, 2)
        row = cols_of(lax.rem(step, k_steps) * group + lax.rem(rel, group), SLOT_ROWS)
        in_ff = (num >= ff_from) & (num < dn_from)

        @pl.when(in_ff & (kind == 0))
        def _():
            pltpu.make_async_copy(wg_hbm.at[row, cols_of(half, ff_half)], dst.at[:, pl.ds(0, ff_half)], sem).start()

        @pl.when(in_ff & (kind == 1))
        def _():
            pltpu.make_async_copy(wu_hbm.at[row, cols_of(half, ff_half)], dst.at[:, pl.ds(0, ff_half)], sem).start()

        rel = num - dn_from
        for idx, rows in enumerate(dn_rows):
            @pl.when((num >= dn_from) & (num < total) & (lax.rem(rel, len(dn_rows)) == idx))
            def _():
                src = wd_hbm.at[pl.ds(idx * SLOT_ROWS, rows), cols_of(rel // len(dn_rows), SLOT_COLS)]
                pltpu.make_async_copy(src, dst.at[pl.ds(0, rows)], sem).start()

    def take(num, rows, cols):
        slot = lax.rem(num, SLOTS)
        part = slots.at[slot, pl.ds(0, rows), pl.ds(0, cols)]
        pltpu.make_async_copy(part, part, slot_sem.at[slot]).wait()
        return slots.at[slot]

    x_copy = pltpu.make_async_copy(x_hbm, h_buf, x_sem)
    x_copy.start()
    for num in range(SLOTS):
        issue(jnp.int32(num))
    x_copy.wait()

    @pl.loop(0, n_wo)
    def _(num):
        slot = take(num, SLOT_ROWS, SLOT_COLS)
        for sub in range(0, SLOT_COLS, COLS):
            cols = pl.ds(pl.multiple_of(num * SLOT_COLS + sub, COLS), COLS)
            out = fdot(attn_ref[...], slot[:, sub:sub + COLS])
            h_buf[:, cols] = (h_buf[:, cols].astype(F32) + out).astype(BF16)
        issue(num + SLOTS)

    @pl.loop(0, count // 32)
    def _(idx):
        norm_rows(h_buf, b_buf, gain_ref, pl.multiple_of(idx * 32, 32), 32)

    @pl.loop(0, n_ff)
    def _(step):
        num = ff_from + step * group
        half = step // (2 * k_steps)
        kind = lax.rem(step // k_steps, 2)
        k_idx = lax.rem(step, k_steps)
        parts = [take(num + sub, SLOT_ROWS, ff_half) for sub in range(group)]
        lhs = b_buf[:, cols_of(k_idx, SLOT_ROWS * group)]
        for col in range(0, ff_half, COLS):
            size = min(COLS, ff_half - col)
            cols = slice(col, col + size)
            out = fdot(lhs, jnp.concatenate([part[:, cols] for part in parts], axis=0))
            acc_ref[kind, :, cols] = jnp.where(k_idx == 0, 0.0, acc_ref[kind, :, cols]) + out
        for sub in range(group):
            issue(num + sub + SLOTS)

        @pl.when((kind == 1) & (k_idx == k_steps - 1))
        def _():
            for col in range(0, ff_half, 256):
                gate = acc_ref[0, :, col:col + 256]
                dst = pl.ds(pl.multiple_of(half * ff_half + col, 256), 256)
                m_buf[:, dst] = (gate * jax.nn.sigmoid(gate) * acc_ref[1, :, col:col + 256]).astype(BF16)

    def z_copy(blk):
        slot = lax.rem(blk, 2)
        return pltpu.make_async_copy(z_buf.at[slot], z_hbm.at[:, cols_of(blk, SLOT_COLS)], z_sem.at[slot])

    @pl.loop(0, n_dn)
    def _(blk):
        num = dn_from + blk * len(dn_rows)
        parts = [take(num + idx, rows, SLOT_COLS) for idx, rows in enumerate(dn_rows)]

        @pl.when(blk >= 2)
        def _():
            z_copy(blk - 2).wait()

        for sub in range(0, SLOT_COLS, COLS):
            cols = pl.ds(pl.multiple_of(blk * SLOT_COLS + sub, COLS), COLS)
            out = fdot(m_buf[...], jnp.concatenate([part[:rows, sub:sub + COLS] for part, rows in zip(parts, dn_rows)], axis=0))
            z_buf[lax.rem(blk, 2), :, sub:sub + COLS] = (h_buf[:, cols].astype(F32) + out).astype(BF16)
        z_copy(blk).start()
        for idx in range(len(dn_rows)):
            issue(num + idx + SLOTS)

    for blk in range(max(0, n_dn - 2), n_dn):
        z_copy(blk).wait()


def solution(mesh):
    cp_size = mesh.shape['cp']
    side = math.isqrt(cp_size // 2)
    vmem = pl.BlockSpec(memory_space=pltpu.VMEM)
    hbm = pl.BlockSpec(memory_space=pl.ANY)
    dma = pltpu.SemaphoreType.DMA
    limit = 60 * 1024 * 1024

    def device_fn(x_loc, seg_loc, pos_loc, attn_gain, w_q, w_k, w_v, w_o, mlp_gain, w_gate, w_up, w_down):
        rows = x_loc[0]
        count, depth = rows.shape
        piece = count // 2
        width = w_q.shape[1] // HEAD_DIM * piece
        ff = w_gate.shape[1]
        pos3 = pos_loc.reshape(2, 1, piece)
        freqs = jnp.asarray(rope_freqs()).reshape(HEAD_DIM // 2, 1)
        q_t, kv, k_rows, v_rows = pl.pallas_call(
            project_kernel,
            out_shape=(jax.ShapeDtypeStruct((2, HEAD_DIM, width), BF16), jax.ShapeDtypeStruct((4, piece, HEAD_DIM), BF16), jax.ShapeDtypeStruct((count, HEAD_DIM), BF16), jax.ShapeDtypeStruct((count, HEAD_DIM), BF16)),
            in_specs=[hbm, vmem, vmem, vmem, hbm, hbm, hbm],
            out_specs=(vmem, vmem, vmem, vmem),
            scratch_shapes=[pltpu.VMEM((count, depth), BF16), pltpu.VMEM((count, depth), BF16), pltpu.VMEM((depth, HEAD_DIM), BF16), pltpu.VMEM((depth, HEAD_DIM), BF16), pltpu.VMEM((depth // SLOT_ROWS, SLOT_ROWS, w_q.shape[1]), BF16), dma((count // 32,)), dma((2,)), dma((depth // SLOT_ROWS,))],
            compiler_params=pltpu.CompilerParams(vmem_limit_bytes=limit),
            name='project',
        )(rows, attn_gain, pos3, freqs, w_q, w_k, w_v)
        attn_rows = pl.pallas_call(
            functools.partial(attend_kernel, cp_size, side),
            out_shape=jax.ShapeDtypeStruct((count, w_q.shape[1]), BF16),
            in_specs=[vmem, vmem, vmem],
            out_specs=vmem,
            scratch_shapes=[pltpu.VMEM((cp_size, 4, piece, HEAD_DIM), BF16), pltpu.VMEM((2, 1, width), F32), pltpu.VMEM((2, 1, width), F32), pltpu.VMEM((2, HEAD_DIM, width), F32), pltpu.VMEM((OWNERS * piece, width), F32), dma((NUM_COPIES,)), dma((NUM_COPIES,))],
            compiler_params=pltpu.CompilerParams(vmem_limit_bytes=limit, collective_id=0, has_side_effects=True),
            name='attend',
        )(kv, q_t, pos3)
        z_rows = pl.pallas_call(
            finish_kernel,
            out_shape=jax.ShapeDtypeStruct((count, depth), BF16),
            in_specs=[hbm, vmem, vmem, hbm, hbm, hbm, hbm],
            out_specs=hbm,
            scratch_shapes=[pltpu.VMEM((count, depth), BF16), pltpu.VMEM((count, depth), BF16), pltpu.VMEM((count, ff), BF16), pltpu.VMEM((2, count, ff // 2), F32), pltpu.VMEM((2, count, SLOT_COLS), BF16), pltpu.VMEM((SLOTS, SLOT_ROWS, SLOT_COLS), BF16), dma(()), dma((SLOTS,)), dma((2,))],
            compiler_params=pltpu.CompilerParams(vmem_limit_bytes=limit),
            name='finish',
        )(rows, attn_rows, mlp_gain, w_o, w_gate, w_up, w_down)
        return z_rows[None], k_rows[:, None, :], v_rows[:, None, :]

    seq_spec = P(('dp', 'cp'))
    return jax.shard_map(device_fn, mesh=mesh, in_specs=(P('dp', 'cp', None), seq_spec, seq_spec, P(), P(), P(), P(), P(), P(), P(), P(), P()), out_specs=(P('dp', 'cp', None), P(('dp', 'cp'), None, None), P(('dp', 'cp'), None, None)), check_vma=False)
```

time: 165 us -> 127 us (0.77)
  Pallas kernels: 159 us -> 126 us
  local copies, waits for them, and re-layouts: 2.69 us -> 0 us
  other arithmetic: 2.06 us -> 0 us
    pallas_call x1, Pallas kernels: 58.9 us -> 36.6 us  [device_fn(): pl.pallas_call(functools.partial(attend_kernel, cp_size, side), out_shape...]
    pallas_call x1, Pallas kernels: 80.1 us -> 74.2 us  [device_fn(): pl.pallas_call(finish_kernel, out_shape=jax.ShapeDtypeStruct((count, dept...]
    pallas_call x1, Pallas kernels: 19.8 us -> 15.6 us  [device_fn(): pl.pallas_call(project_kernel, out_shape=(jax.ShapeDtypeStruct((2, HEAD_D...]
    reshape x2 -> x0, local copies, waits for them, and re-layouts: 2.69 us -> none  [the longest x1 1.35 us: device_fn(): attn_gain.reshape(1, depth)]
where the time goes in v2:
time: 127 us
  Pallas kernels  126 us (99%)
    pallas_call x1, Pallas kernels, device_fn(): pl.pallas_call(finish_kernel, out_shape=jax.ShapeDtypeStruct((count, dept...  74.2 us
    pallas_call x1, Pallas kernels, device_fn(): pl.pallas_call(functools.partial(attend_kernel, cp_size, side), out_shape...  36.6 us
    pallas_call x1, Pallas kernels, device_fn(): pl.pallas_call(project_kernel, out_shape=(jax.ShapeDtypeStruct((2, HEAD_D...  15.6 us

profile of v2, /device:TPU:97, one launch (start us, length us, event | category | flops | bytes accessed | tf_op | source)
XLA Modules:
  0.0 127.2 jit_solution(6166698572124960641)
XLA Ops:
  0.6 15.6 %project.1 = (bf16[2,128,1024]{2,1,0:T(8,128)(2,1)}, bf16[4,128,128]{2,1,0:T(8,128)(2,1)}, bf16[256,128]{1,0:T(8,128)(2,1)}, bf16[256,128]{1,0:T(8,128)(2,1)}) custom-call(bf16[256,8192]{1,0:T(8,128)(2,1)} %bitcast.5, bf16[8192]{0:T(1024)(128)(2,1)} %gain_ref.2, s32[2,1,128]{2,1,0:T(1,128)} %bitcast.8, f32[64,1]{1,0:T(8,128)} %constant.3.freq_ref, ...), custom_call_target="tpu_custom_call" | custom-call | tf_op jit(solution)/shard_map/project/pallas_call | solution.py:450
  16.3 36.6 %attend.1.attn_ref = bf16[256,1024]{1,0:T(8,128)(2,1)} custom-call(bf16[4,128,128]{2,1,0:T(8,128)(2,1)} %get-tuple-element.7.kv_ref, bf16[2,128,1024]{2,1,0:T(8,128)(2,1)} %get-tuple-element.8.qt_ref, s32[2,1,128]{2,1,0:T(1,128)} %bitcast.9), custom_call_target="tpu_custom_call" | custom-call | tf_op jit(solution)/shard_map/attend/pallas_call | solution.py:459
  52.9 74.2 %finish.1 = bf16[256,8192]{1,0:T(8,128)(2,1)} custom-call(bf16[256,8192]{1,0:T(8,128)(2,1)} %bitcast.6, bf16[256,1024]{1,0:T(8,128)(2,1)} %attend.1.attn_ref, bf16[8192]{0:T(1024)(128)(2,1)} %gain_ref.3, bf16[1024,8192]{1,0:T(8,128)(2,1)} %wo_hbm.1, bf16[8192,3584]{1,0:T(8,128)(2,1)} %wg_hbm.1, bf16[8192,3584]{1,0:T(8,128)(2,1)} %wu_hbm.1, ...), custom_call_target="tpu_custom_call" | custom-call | tf_op jit(solution)/shard_map/finish/pallas_call | solution.py:468

commit v3 on v2

--- a/solution.py
+++ b/solution.py
@@ -73,8 +73,8 @@
     for copy in wkv:
         copy.start()
     wq_copies = [pltpu.make_async_copy(wq_hbm.at[pl.ds(idx * chunk_rows, chunk_rows)], wq_buf.at[idx], wq_sem.at[idx]) for idx in range(chunks)]
-    for copy in wq_copies:
-        copy.start()
+    for idx, copy in enumerate(wq_copies):
+        copy.start(priority=idx % 2)
 
     cos_t, sin_t = rope_tables(pos_ref, freq_ref)
 
@@ -327,6 +327,11 @@
     def cols_of(idx, size):
         return pl.ds(pl.multiple_of(idx * size, size), size)
 
+    def halves(src, dst, rows, sem):
+        for part in range(2):
+            sel = pl.ds(part * rows // 2, rows // 2)
+            pltpu.make_async_copy(src.at[sel], dst.at[sel], sem).start(priority=part)
+
     def issue(num):
         slot = lax.rem(num, SLOTS)
         sem = slot_sem.at[slot]
@@ -334,7 +339,7 @@
 
         @pl.when(num < ff_from)
         def _():
-            pltpu.make_async_copy(wo_hbm.at[:, cols_of(num, SLOT_COLS)], dst, sem).start()
+            halves(wo_hbm.at[:, cols_of(num, SLOT_COLS)], dst, SLOT_ROWS, sem)
 
         rel = num - ff_from
         step = rel // group
@@ -345,18 +350,18 @@
 
         @pl.when(in_ff & (kind == 0))
         def _():
-            pltpu.make_async_copy(wg_hbm.at[row, cols_of(half, ff_half)], dst.at[:, pl.ds(0, ff_half)], sem).start()
+            halves(wg_hbm.at[row, cols_of(half, ff_half)], dst.at[:, pl.ds(0, ff_half)], SLOT_ROWS, sem)
 
         @pl.when(in_ff & (kind == 1))
         def _():
-            pltpu.make_async_copy(wu_hbm.at[row, cols_of(half, ff_half)], dst.at[:, pl.ds(0, ff_half)], sem).start()
+            halves(wu_hbm.at[row, cols_of(half, ff_half)], dst.at[:, pl.ds(0, ff_half)], SLOT_ROWS, sem)
 
         rel = num - dn_from
         for idx, rows in enumerate(dn_rows):
             @pl.when((num >= dn_from) & (num < total) & (lax.rem(rel, len(dn_rows)) == idx))
             def _():
                 src = wd_hbm.at[pl.ds(idx * SLOT_ROWS, rows), cols_of(rel // len(dn_rows), SLOT_COLS)]
-                pltpu.make_async_copy(src, dst.at[pl.ds(0, rows)], sem).start()
+                halves(src, dst.at[pl.ds(0, rows)], rows, sem)
 
     def take(num, rows, cols):
         slot = lax.rem(num, SLOTS)

time: 127 us -> 124 us (0.976)
  Pallas kernels: 126 us -> 123 us
    pallas_call x1, Pallas kernels: 74.2 us -> 71.7 us  [device_fn(): pl.pallas_call(finish_kernel, out_shape=jax.ShapeDtypeStruct((count, dept...]
where the time goes in v3:
time: 124 us
  Pallas kernels  123 us (99%)
    pallas_call x1, Pallas kernels, device_fn(): pl.pallas_call(finish_kernel, out_shape=jax.ShapeDtypeStruct((count, dept...  71.7 us
    pallas_call x1, Pallas kernels, device_fn(): pl.pallas_call(functools.partial(attend_kernel, cp_size, side), out_shape...  36.6 us
    pallas_call x1, Pallas kernels, device_fn(): pl.pallas_call(project_kernel, out_shape=(jax.ShapeDtypeStruct((2, HEAD_D...  14.9 us

profile of v3, /device:TPU:97, one launch (start us, length us, event | category | flops | bytes accessed | tf_op | source)
XLA Modules:
  0.0 124.0 jit_solution(14874744545334796187)
XLA Ops:
  0.6 14.9 %project.1 = (bf16[2,128,1024]{2,1,0:T(8,128)(2,1)}, bf16[4,128,128]{2,1,0:T(8,128)(2,1)}, bf16[256,128]{1,0:T(8,128)(2,1)}, bf16[256,128]{1,0:T(8,128)(2,1)}) custom-call(bf16[256,8192]{1,0:T(8,128)(2,1)} %bitcast.5, bf16[8192]{0:T(1024)(128)(2,1)} %gain_ref.2, s32[2,1,128]{2,1,0:T(1,128)} %bitcast.8, f32[64,1]{1,0:T(8,128)} %constant.3.freq_ref, ...), custom_call_target="tpu_custom_call" | custom-call | tf_op jit(solution)/shard_map/project/pallas_call | solution.py:455
  15.5 36.6 %attend.1.attn_ref = bf16[256,1024]{1,0:T(8,128)(2,1)} custom-call(bf16[4,128,128]{2,1,0:T(8,128)(2,1)} %get-tuple-element.7.kv_ref, bf16[2,128,1024]{2,1,0:T(8,128)(2,1)} %get-tuple-element.8.qt_ref, s32[2,1,128]{2,1,0:T(1,128)} %bitcast.9), custom_call_target="tpu_custom_call" | custom-call | tf_op jit(solution)/shard_map/attend/pallas_call | solution.py:464
  52.1 71.7 %finish.1 = bf16[256,8192]{1,0:T(8,128)(2,1)} custom-call(bf16[256,8192]{1,0:T(8,128)(2,1)} %bitcast.6, bf16[256,1024]{1,0:T(8,128)(2,1)} %attend.1.attn_ref, bf16[8192]{0:T(1024)(128)(2,1)} %gain_ref.3, bf16[1024,8192]{1,0:T(8,128)(2,1)} %wo_hbm.1, bf16[8192,3584]{1,0:T(8,128)(2,1)} %wg_hbm.1, bf16[8192,3584]{1,0:T(8,128)(2,1)} %wu_hbm.1, ...), custom_call_target="tpu_custom_call" | custom-call | tf_op jit(solution)/shard_map/finish/pallas_call | solution.py:473

commit v4 on v3

--- a/solution.py
+++ b/solution.py
@@ -24,7 +24,7 @@
 SLOT_ROWS = 1024
 SLOT_COLS = 2048
 OWNERS = 4
-LANES = 256
+LANES = 512
 F32 = jnp.float32
 BF16 = jnp.bfloat16
 
@@ -55,42 +55,43 @@
         dst_ref[rows, col:col + 512] = (part * inv_rms * gain).astype(BF16)
 
 
-def project_kernel(x_hbm, gain_ref, pos_ref, freq_ref, wq_hbm, wk_hbm, wv_hbm, qt_ref, kv_ref, kc_ref, vc_ref, x_buf, a_buf, wk_buf, wv_buf, wq_buf, x_sem, wkv_sem, wq_sem):
-    count, depth = x_buf.shape
+def project_kernel(x_hbm, gain_ref, pos_ref, freq_ref, wk_hbm, wv_hbm, a_hbm, cos_ref, sin_ref, kv_ref, kc_ref, vc_ref, x_buf, a_buf, wk_buf, wv_buf, x_sem, wkv_sem, a_sem):
+    count = x_buf.shape[0]
     piece = count // 2
     blocks = x_sem.shape[0]
     rows_blk = count // blocks
-    chunks = wq_buf.shape[0]
-    chunk_rows = wq_buf.shape[1]
 
     def x_copy(idx):
         rows = pl.ds(idx * rows_blk, rows_blk)
         return pltpu.make_async_copy(x_hbm.at[rows], x_buf.at[rows], x_sem.at[idx])
+
+    def a_copy(idx):
+        rows = pl.ds(idx * rows_blk, rows_blk)
+        return pltpu.make_async_copy(a_buf.at[rows], a_hbm.at[rows], a_sem.at[idx])
 
     for idx in range(blocks):
         x_copy(idx).start()
     wkv = [pltpu.make_async_copy(wk_hbm, wk_buf, wkv_sem.at[0]), pltpu.make_async_copy(wv_hbm, wv_buf, wkv_sem.at[1])]
     for copy in wkv:
-        copy.start()
-    wq_copies = [pltpu.make_async_copy(wq_hbm.at[pl.ds(idx * chunk_rows, chunk_rows)], wq_buf.at[idx], wq_sem.at[idx]) for idx in range(chunks)]
-    for idx, copy in enumerate(wq_copies):
-        copy.start(priority=idx % 2)
-
-    cos_t, sin_t = rope_tables(pos_ref, freq_ref)
+        copy.start(priority=1)
+    for half in range(2):
+        rows = slice(half * piece, (half + 1) * piece)
+        angles = freq_ref[...] * pos_ref[half].astype(F32)
+        cos_h = jnp.cos(angles).T
+        sin_h = jnp.sin(angles).T
+        cos_ref[rows] = jnp.concatenate([cos_h, cos_h], axis=1)
+        sin_ref[rows] = jnp.concatenate([-sin_h, sin_h], axis=1)
 
     @pl.loop(0, blocks)
     def _(idx):
         x_copy(idx).wait()
         norm_rows(x_buf, a_buf, gain_ref, pl.multiple_of(idx * rows_blk, rows_blk), rows_blk)
+        a_copy(idx).start()
 
     for copy in wkv:
         copy.wait()
     kv_raw = fdot(a_buf[...], jnp.concatenate([wk_buf[...], wv_buf[...]], axis=1))
-
-    def rope(raw):
-        return raw * cos_t + pltpu.roll(raw, HEAD_DIM // 2, 1) * sin_t
-
-    k_rot = rope(kv_raw[:, :HEAD_DIM])
+    k_rot = rope(kv_raw[:, :HEAD_DIM], cos_ref[...], sin_ref[...])
     v_raw = kv_raw[:, HEAD_DIM:]
     kc_ref[...] = k_rot.astype(BF16)
     vc_ref[...] = v_raw.astype(BF16)
@@ -98,30 +99,16 @@
         rows = slice(half * piece, (half + 1) * piece)
         kv_ref[half] = k_rot[rows].astype(BF16)
         kv_ref[2 + half] = v_raw[rows].T.astype(BF16)
-
-    for copy in wq_copies:
-        copy.wait()
-    for col in range(wq_hbm.shape[1] // COLS):
-        q_raw = fdot(a_buf[...], jnp.concatenate([wq_buf[idx, :, col * COLS:(col + 1) * COLS] for idx in range(chunks)], axis=0))
-        for sub in range(COLS // HEAD_DIM):
-            head = col * (COLS // HEAD_DIM) + sub
-            q_rot = rope(q_raw[:, sub * HEAD_DIM:(sub + 1) * HEAD_DIM])
-            for half in range(2):
-                qt_ref[half, :, head * piece:(head + 1) * piece] = q_rot[half * piece:(half + 1) * piece].T.astype(BF16)
-
-
-def rope_tables(pos_ref, freq_ref):
-    cos_parts, sin_parts = [], []
-    for half in range(2):
-        angles = freq_ref[...] * pos_ref[half].astype(F32)
-        cos_parts.append(jnp.cos(angles).T)
-        sin_parts.append(jnp.sin(angles).T)
-    cos_h = jnp.concatenate(cos_parts, axis=0)
-    sin_h = jnp.concatenate(sin_parts, axis=0)
-    return jnp.concatenate([cos_h, cos_h], axis=1), jnp.concatenate([-sin_h, sin_h], axis=1)
-
-
-def gather_shards(side, kv_ref, all_ref, send_sem, recv_sem, on_start, on_group):
+    for idx in range(blocks):
+        a_copy(idx).wait()
+
+
+def rope(raw, cos_t, sin_t):
+    half = HEAD_DIM // 2
+    return raw * cos_t + jnp.concatenate([raw[:, half:], raw[:, :half]], axis=1) * sin_t
+
+
+def torus_place(side):
     me = lax.axis_index('cp')
     core = lax.rem(me, 2)
     chip = me // 2
@@ -136,7 +123,12 @@
     def other(first, second):
         return owner(first, second, 1 - core)
 
-    sibling = me + 1 - 2 * core
+    return me, owner, other
+
+
+def gather_shards(place, kv_ref, all_ref, send_sem, recv_sem, on_start, on_group):
+    me, owner, other = place
+    sibling = other(0, 0)
     targets = {'a+': owner(1, 0), 'a-': owner(-1, 0), 'b+': owner(0, 1), 'b-': owner(0, -1), 's': sibling}
     barrier = pltpu.get_barrier_semaphore()
     for target in targets.values():
@@ -164,6 +156,26 @@
         minus = send(shard, 'b-')
         from_sibling.append(send(shard, 's'))
         return plus, minus
+
+    def relay(first, row):
+        row[0].wait_recv()
+        shard = owner(first, -1)
+        half_k = send(shard, 'b+', 0)
+        from_sibling.append(send(shard, 's'))
+        row[1].wait_recv()
+        shard = owner(first, 1)
+        half_v = send(shard, 'b-', 1)
+        from_sibling.append(send(shard, 's'))
+        return half_k, half_v
+
+    def close(first, halves):
+        halves[0].wait_recv()
+        halves[1].wait_recv()
+        from_sibling.append(send(owner(first, 2), 's'))
+
+    def arrived(*nums):
+        for num in nums:
+            from_sibling[num].wait_recv()
 
     own_right = send(me, 'a+')
     own_left = send(me, 'a-')
@@ -178,30 +190,9 @@
     shard = owner(1, 0)
     far_v = send(shard, 'a-', 1)
     row_right = spread(shard)
-
-    def relay(first, row):
-        row[0].wait_recv()
-        shard = owner(first, -1)
-        half_k = send(shard, 'b+', 0)
-        from_sibling.append(send(shard, 's'))
-        row[1].wait_recv()
-        shard = owner(first, 1)
-        half_v = send(shard, 'b-', 1)
-        from_sibling.append(send(shard, 's'))
-        return half_k, half_v
-
-    def close(first, halves):
-        halves[0].wait_recv()
-        halves[1].wait_recv()
-        from_sibling.append(send(owner(first, 2), 's'))
-
-    def arrived(*nums):
-        for num in nums:
-            from_sibling[num].wait_recv()
-
+    far_own = relay(0, row_own)
     arrived(0)
     on_group(me, sibling, owner(-1, 0), owner(1, 0))
-    far_own = relay(0, row_own)
     far_k.wait_recv()
     far_v.wait_recv()
     row_far = spread(owner(2, 0))
@@ -233,11 +224,19 @@
 NUM_COPIES = 36
 
 
-def attend_kernel(cp_size, side, kv_ref, qt_ref, pos_ref, out_ref, all_ref, max_ref, sum_ref, acc_ref, score_ref, send_sem, recv_sem):
-    me = lax.axis_index('cp')
-    piece = kv_ref.shape[1]
+def attend_kernel(cp_size, side, kv_ref, pos_ref, cos_ref, sin_ref, a_hbm, wq_hbm, out_ref, a_buf, wq_buf, qt_ref, all_ref, max_ref, sum_ref, acc_ref, score_ref, a_sem, wq_sem, send_sem, recv_sem):
+    place = torus_place(side)
+    me = place[0]
+    count = a_buf.shape[0]
+    piece = count // 2
     width = qt_ref.shape[2]
     tiles = width // LANES
+    chunks, chunk_rows = wq_buf.shape[:2]
+    loads = [pltpu.make_async_copy(a_hbm, a_buf, a_sem)]
+    loads += [pltpu.make_async_copy(wq_hbm.at[pl.ds(idx * chunk_rows, chunk_rows)], wq_buf.at[idx], wq_sem.at[idx]) for idx in range(chunks)]
+    for copy in loads:
+        copy.start()
+
     bases = (me * piece, (2 * cp_size - 1 - me) * piece)
     lane_tok = lax.broadcasted_iota(jnp.int32, (1, piece), 1)
 
@@ -249,11 +248,22 @@
     tok = jnp.concatenate([lane_tok] * (LANES // piece), axis=1)
     key_row = lax.broadcasted_iota(jnp.int32, (piece, LANES), 0)
 
-    def diagonal():
+    def queries_and_diagonal():
+        for copy in loads:
+            copy.wait()
+        for col in range(wq_buf.shape[2] // COLS):
+            q_raw = fdot(a_buf[...], jnp.concatenate([wq_buf[idx, :, col * COLS:(col + 1) * COLS] for idx in range(chunks)], axis=0))
+            for sub in range(COLS // HEAD_DIM):
+                head = col * (COLS // HEAD_DIM) + sub
+                q_rot = rope(q_raw[:, sub * HEAD_DIM:(sub + 1) * HEAD_DIM], cos_ref[...], sin_ref[...])
+                for half in range(2):
+                    qt_ref[half, :, head * piece:(head + 1) * piece] = q_rot[half * piece:(half + 1) * piece].T.astype(BF16)
         for half in range(2):
             visible = (key_row <= tok) & (key_row + bases[half] >= first_key[half])
-            for tile in range(tiles):
-                cols = slice(tile * LANES, (tile + 1) * LANES)
+
+            @pl.loop(0, tiles)
+            def _(tile):
+                cols = pl.ds(pl.multiple_of(tile * LANES, LANES), LANES)
                 scores = fdot(kv_ref[half], qt_ref[half, :, cols])
                 scores = jnp.where(visible, scores, NEG_BIG)
                 top = jnp.max(scores, axis=0, keepdims=True)
@@ -262,46 +272,48 @@
                 sum_ref[half, :, cols] = jnp.sum(prob, axis=0, keepdims=True)
                 acc_ref[half, :, cols] = fdot(kv_ref[2 + half], prob.astype(BF16))
 
-    def block(half, part, owners, key_base):
-        keys = jnp.concatenate([all_ref[own, part] for own in owners], axis=0)
-        vals = jnp.concatenate([all_ref[own, 2 + part] for own in owners], axis=1)
-        hidden = [key_row < first_key[half] - base for base in key_base]
-        tops, scales = [], []
-        for tile in range(tiles):
-            cols = slice(tile * LANES, (tile + 1) * LANES)
-            raw = fdot(keys, qt_ref[half, :, cols])
-            peak = None
-            for sub in range(OWNERS):
-                rows = slice(sub * piece, (sub + 1) * piece)
-                score = jnp.where(hidden[sub], NEG_BIG, raw[rows])
-                score_ref[rows, cols] = score
-                best = jnp.max(score, axis=0, keepdims=True)
-                peak = best if peak is None else jnp.maximum(peak, best)
-            old_top = max_ref[half, :, cols]
-            top = jnp.maximum(old_top, peak)
-            max_ref[half, :, cols] = top
-            tops.append(top)
-            scales.append(jnp.exp2((old_top - top) * SCORE_LOG2))
-        for tile in range(tiles):
-            cols = slice(tile * LANES, (tile + 1) * LANES)
-            prob = jnp.exp2((score_ref[:, cols] - tops[tile]) * SCORE_LOG2)
-            sum_ref[half, :, cols] = sum_ref[half, :, cols] * scales[tile] + jnp.sum(prob, axis=0, keepdims=True)
-            acc_ref[half, :, cols] = acc_ref[half, :, cols] * scales[tile] + fdot(vals, prob.astype(BF16))
-
-    def low_group(*owners):
-        block(1, 0, owners, [own * piece for own in owners])
-
-    gather_shards(side, kv_ref, all_ref, send_sem, recv_sem, diagonal, low_group)
-
-    @pl.loop(0, (me + OWNERS - 1) // OWNERS)
-    def _(idx):
-        owners = [idx * OWNERS + sub for sub in range(OWNERS)]
-        block(0, 0, owners, [jnp.where(own < me, own * piece, -2 * piece) for own in owners])
-
-    @pl.loop((me + 1) // OWNERS, cp_size // OWNERS)
-    def _(idx):
-        owners = [idx * OWNERS + sub for sub in range(OWNERS)]
-        block(1, 1, owners, [jnp.where(own > me, (2 * cp_size - 1 - own) * piece, -2 * piece) for own in owners])
+    def low_tile(owners, cols):
+        keys = jnp.concatenate([all_ref[own, 0] for own in owners], axis=0)
+        vals = jnp.concatenate([all_ref[own, 2] for own in owners], axis=1)
+        raw = fdot(keys, qt_ref[1, :, cols])
+        peak = None
+        for sub, own in enumerate(owners):
+            rows = slice(sub * piece, (sub + 1) * piece)
+            score = jnp.where(key_row < first_key[1] - own * piece, NEG_BIG, raw[rows])
+            score_ref[rows] = score
+            best = jnp.max(score, axis=0, keepdims=True)
+            peak = best if peak is None else jnp.maximum(peak, best)
+        old_top = max_ref[1, :, cols]
+        top = jnp.maximum(old_top, peak)
+        scale = jnp.exp2((old_top - top) * SCORE_LOG2)
+        prob = jnp.exp2((score_ref[...] - top) * SCORE_LOG2)
+        max_ref[1, :, cols] = top
+        sum_ref[1, :, cols] = sum_ref[1, :, cols] * scale + jnp.sum(prob, axis=0, keepdims=True)
+        acc_ref[1, :, cols] = acc_ref[1, :, cols] * scale + fdot(vals, prob.astype(BF16))
+
+    def side_tile(own, cols):
+        half = (own - me + cp_size) // cp_size
+        base = (own + half * (2 * cp_size - 1 - 2 * own)) * piece
+        hidden = key_row < jnp.where(half == 0, first_key[0], first_key[1]) - base
+        score = jnp.where(hidden, NEG_BIG, fdot(all_ref[own, half], qt_ref[half, :, cols]))
+        old_top = max_ref[half, :, cols]
+        top = jnp.maximum(old_top, jnp.max(score, axis=0, keepdims=True))
+        prob = jnp.exp2((score - top) * SCORE_LOG2)
+        scale = jnp.exp2((old_top - top) * SCORE_LOG2)
+        max_ref[half, :, cols] = top
+        sum_ref[half, :, cols] = sum_ref[half, :, cols] * scale + jnp.sum(prob, axis=0, keepdims=True)
+        acc_ref[half, :, cols] = acc_ref[half, :, cols] * scale + fdot(all_ref[own, 2 + half], prob.astype(BF16))
+
+    def on_group(*owners):
+        @pl.loop(0, tiles)
+        def _(tile):
+            cols = pl.ds(pl.multiple_of(tile * LANES, LANES), LANES)
+            low_tile(owners, cols)
+            for own in owners:
+                if own is not me:
+                    side_tile(own, cols)
+
+    gather_shards(place, kv_ref, all_ref, send_sem, recv_sem, queries_and_diagonal, on_group)
 
     for half in range(2):
         for head in range(width // piece):
@@ -452,24 +464,28 @@
         ff = w_gate.shape[1]
         pos3 = pos_loc.reshape(2, 1, piece)
         freqs = jnp.asarray(rope_freqs()).reshape(HEAD_DIM // 2, 1)
-        q_t, kv, k_rows, v_rows = pl.pallas_call(
+        chunks = depth // SLOT_ROWS
+        blocks = count // 32
+        table = jax.ShapeDtypeStruct((count, HEAD_DIM), F32)
+        cache = jax.ShapeDtypeStruct((count, HEAD_DIM), BF16)
+        a_rows, cos_t, sin_t, kv, k_rows, v_rows = pl.pallas_call(
             project_kernel,
-            out_shape=(jax.ShapeDtypeStruct((2, HEAD_DIM, width), BF16), jax.ShapeDtypeStruct((4, piece, HEAD_DIM), BF16), jax.ShapeDtypeStruct((count, HEAD_DIM), BF16), jax.ShapeDtypeStruct((count, HEAD_DIM), BF16)),
-            in_specs=[hbm, vmem, vmem, vmem, hbm, hbm, hbm],
-            out_specs=(vmem, vmem, vmem, vmem),
-            scratch_shapes=[pltpu.VMEM((count, depth), BF16), pltpu.VMEM((count, depth), BF16), pltpu.VMEM((depth, HEAD_DIM), BF16), pltpu.VMEM((depth, HEAD_DIM), BF16), pltpu.VMEM((depth // SLOT_ROWS, SLOT_ROWS, w_q.shape[1]), BF16), dma((count // 32,)), dma((2,)), dma((depth // SLOT_ROWS,))],
+            out_shape=(jax.ShapeDtypeStruct((count, depth), BF16), table, table, jax.ShapeDtypeStruct((4, piece, HEAD_DIM), BF16), cache, cache),
+            in_specs=[hbm, vmem, vmem, vmem, hbm, hbm],
+            out_specs=(hbm, vmem, vmem, vmem, vmem, vmem),
+            scratch_shapes=[pltpu.VMEM((count, depth), BF16), pltpu.VMEM((count, depth), BF16), pltpu.VMEM((depth, HEAD_DIM), BF16), pltpu.VMEM((depth, HEAD_DIM), BF16), dma((blocks,)), dma((2,)), dma((blocks,))],
             compiler_params=pltpu.CompilerParams(vmem_limit_bytes=limit),
             name='project',
-        )(rows, attn_gain, pos3, freqs, w_q, w_k, w_v)
+        )(rows, attn_gain, pos3, freqs, w_k, w_v)
         attn_rows = pl.pallas_call(
             functools.partial(attend_kernel, cp_size, side),
             out_shape=jax.ShapeDtypeStruct((count, w_q.shape[1]), BF16),
-            in_specs=[vmem, vmem, vmem],
+            in_specs=[vmem, vmem, vmem, vmem, hbm, hbm],
             out_specs=vmem,
-            scratch_shapes=[pltpu.VMEM((cp_size, 4, piece, HEAD_DIM), BF16), pltpu.VMEM((2, 1, width), F32), pltpu.VMEM((2, 1, width), F32), pltpu.VMEM((2, HEAD_DIM, width), F32), pltpu.VMEM((OWNERS * piece, width), F32), dma((NUM_COPIES,)), dma((NUM_COPIES,))],
+            scratch_shapes=[pltpu.VMEM((count, depth), BF16), pltpu.VMEM((chunks, SLOT_ROWS, w_q.shape[1]), BF16), pltpu.VMEM((2, HEAD_DIM, width), BF16), pltpu.VMEM((cp_size, 4, piece, HEAD_DIM), BF16), pltpu.VMEM((2, 1, width), F32), pltpu.VMEM((2, 1, width), F32), pltpu.VMEM((2, HEAD_DIM, width), F32), pltpu.VMEM((OWNERS * piece, LANES), F32), dma(()), dma((chunks,)), dma((NUM_COPIES,)), dma((NUM_COPIES,))],
             compiler_params=pltpu.CompilerParams(vmem_limit_bytes=limit, collective_id=0, has_side_effects=True),
             name='attend',
-        )(kv, q_t, pos3)
+        )(kv, pos3, cos_t, sin_t, a_rows, w_q)
         z_rows = pl.pallas_call(
             finish_kernel,
             out_shape=jax.ShapeDtypeStruct((count, depth), BF16),

time: 124 us -> 128 us (1.032)
  Pallas kernels: 123 us -> 127 us
    pallas_call x1, Pallas kernels: 36.6 us -> 47.5 us  [device_fn(): pl.pallas_call(functools.partial(attend_kernel, cp_size, side), out_shape...]
    pallas_call x1, Pallas kernels: 14.9 us -> 8.11 us  [device_fn(): pl.pallas_call(project_kernel, out_shape=(jax.ShapeDtypeStruct((count, de...]
where the time goes in v4:
time: 128 us
  Pallas kernels  127 us (99%)
    pallas_call x1, Pallas kernels, device_fn(): pl.pallas_call(finish_kernel, out_shape=jax.ShapeDtypeStruct((count, dept...  71.7 us
    pallas_call x1, Pallas kernels, device_fn(): pl.pallas_call(functools.partial(attend_kernel, cp_size, side), out_shape...  47.5 us
    pallas_call x1, Pallas kernels, device_fn(): pl.pallas_call(project_kernel, out_shape=(jax.ShapeDtypeStruct((count, de...  8.11 us

profile of v4, /device:TPU:97, one launch (start us, length us, event | category | flops | bytes accessed | tf_op | source)
XLA Modules:
  0.0 128.1 jit_solution(14949074743854970859)
XLA Ops:
  0.6 8.1 %project.1 = (bf16[256,8192]{1,0:T(8,128)(2,1)}, f32[256,128]{1,0:T(8,128)}, f32[256,128]{1,0:T(8,128)}, bf16[4,128,128]{2,1,0:T(8,128)(2,1)}, bf16[256,128]{1,0:T(8,128)(2,1)}, /*index=5*/bf16[256,128]{1,0:T(8,128)(2,1)}) custom-call(bf16[256,8192]{1,0:T(8,128)(2,1)} %bitcast.5, bf16[8192]{0:T(1024)(128)(2,1)} %gain_ref.2, s32[2,1,128]{2,1,0:T(1,128)} %bitcast.8, ...), custom_call_target="tpu_custom_call" | custom-call | tf_op jit(solution)/shard_map/project/pallas_call | solution.py:471
  8.7 47.5 %attend.1.attn_ref = bf16[256,1024]{1,0:T(8,128)(2,1)} custom-call(bf16[4,128,128]{2,1,0:T(8,128)(2,1)} %get-tuple-element.9.kv_ref, s32[2,1,128]{2,1,0:T(1,128)} %bitcast.9, f32[256,128]{1,0:T(8,128)} %get-tuple-element.10.cos_ref, f32[256,128]{1,0:T(8,128)} %get-tuple-element.11.sin_ref, bf16[256,8192]{1,0:T(8,128)(2,1)} %get-tuple-element.12.a_hbm, ...), custom_call_target="tpu_custom_call" | custom-call | tf_op jit(solution)/shard_map/attend/pallas_call | solution.py:480
  56.2 71.7 %finish.1 = bf16[256,8192]{1,0:T(8,128)(2,1)} custom-call(bf16[256,8192]{1,0:T(8,128)(2,1)} %bitcast.6, bf16[256,1024]{1,0:T(8,128)(2,1)} %attend.1.attn_ref, bf16[8192]{0:T(1024)(128)(2,1)} %gain_ref.3, bf16[1024,8192]{1,0:T(8,128)(2,1)} %wo_hbm.1, bf16[8192,3584]{1,0:T(8,128)(2,1)} %wg_hbm.1, bf16[8192,3584]{1,0:T(8,128)(2,1)} %wu_hbm.1, ...), custom_call_target="tpu_custom_call" | custom-call | tf_op jit(solution)/shard_map/finish/pallas_call | solution.py:489

commit v5 on v4

--- a/solution.py
+++ b/solution.py
@@ -20,11 +20,11 @@
 SCORE_LOG2 = HEAD_DIM ** -0.5 * math.log2(math.e)
 MESH = pl.DeviceIdType.MESH
 COLS = 512
-SLOTS = 8
+SLOTS = 6
 SLOT_ROWS = 1024
 SLOT_COLS = 2048
 OWNERS = 4
-LANES = 512
+LANES = 256
 F32 = jnp.float32
 BF16 = jnp.bfloat16
 
@@ -55,7 +55,7 @@
         dst_ref[rows, col:col + 512] = (part * inv_rms * gain).astype(BF16)
 
 
-def project_kernel(x_hbm, gain_ref, pos_ref, freq_ref, wk_hbm, wv_hbm, a_hbm, cos_ref, sin_ref, kv_ref, kc_ref, vc_ref, x_buf, a_buf, wk_buf, wv_buf, x_sem, wkv_sem, a_sem):
+def project_kernel(x_hbm, gain_ref, pos_ref, freq_ref, wk_hbm, wv_hbm, a_hbm, cos_ref, sin_ref, kv_ref, pos_out, kc_ref, vc_ref, x_buf, a_buf, wk_buf, wv_buf, x_sem, wkv_sem, a_sem):
     count = x_buf.shape[0]
     piece = count // 2
     blocks = x_sem.shape[0]
@@ -74,6 +74,7 @@
     wkv = [pltpu.make_async_copy(wk_hbm, wk_buf, wkv_sem.at[0]), pltpu.make_async_copy(wv_hbm, wv_buf, wkv_sem.at[1])]
     for copy in wkv:
         copy.start(priority=1)
+    pos_out[...] = pos_ref[...]
     for half in range(2):
         rows = slice(half * piece, (half + 1) * piece)
         angles = freq_ref[...] * pos_ref[half].astype(F32)
@@ -181,7 +182,6 @@
     own_left = send(me, 'a-')
     row_own = spread(me)
     all_ref[me] = kv_ref[...]
-    on_start()
     own_right.wait_recv()
     shard = owner(-1, 0)
     far_k = send(shard, 'a+', 0)
@@ -191,26 +191,28 @@
     far_v = send(shard, 'a-', 1)
     row_right = spread(shard)
     far_own = relay(0, row_own)
-    arrived(0)
-    on_group(me, sibling, owner(-1, 0), owner(1, 0))
+    on_start(0)
     far_k.wait_recv()
     far_v.wait_recv()
     row_far = spread(owner(2, 0))
+    on_start(1)
+    far_left = relay(-1, row_left)
+    far_right = relay(1, row_right)
+    arrived(0)
+    on_group(me, sibling, owner(-1, 0), owner(1, 0))
+    close(0, far_own)
+    far_far = relay(2, row_far)
     arrived(1, 2)
     on_group(owner(0, -1), owner(0, 1), other(-1, 0), other(1, 0))
-    far_left = relay(-1, row_left)
-    far_right = relay(1, row_right)
+    close(-1, far_left)
+    close(1, far_right)
     arrived(3, 4)
     on_group(owner(2, 0), owner(-1, -1), other(0, -1), other(0, 1))
-    close(0, far_own)
-    far_far = relay(2, row_far)
+    close(2, far_far)
     arrived(5)
     on_group(owner(-1, 1), owner(1, -1), owner(1, 1), other(2, 0))
-    close(-1, far_left)
-    close(1, far_right)
     arrived(6, 7)
     on_group(owner(0, 2), owner(2, -1), other(-1, -1), other(-1, 1))
-    close(2, far_far)
     arrived(8, 9)
     on_group(owner(2, 1), owner(-1, 2), other(1, -1), other(1, 1))
     arrived(10, 11)
@@ -224,7 +226,7 @@
 NUM_COPIES = 36
 
 
-def attend_kernel(cp_size, side, kv_ref, pos_ref, cos_ref, sin_ref, a_hbm, wq_hbm, out_ref, a_buf, wq_buf, qt_ref, all_ref, max_ref, sum_ref, acc_ref, score_ref, a_sem, wq_sem, send_sem, recv_sem):
+def attend_kernel(cp_size, side, kv_ref, pos_ref, cos_ref, sin_ref, a_hbm, wq_hbm, wo_hbm, out_ref, wo_ref, a_buf, wq_buf, qt_ref, all_ref, max_ref, sum_ref, acc_ref, score_ref, a_sem, wq_sem, wo_sem, send_sem, recv_sem):
     place = torus_place(side)
     me = place[0]
     count = a_buf.shape[0]
@@ -234,7 +236,8 @@
     chunks, chunk_rows = wq_buf.shape[:2]
     loads = [pltpu.make_async_copy(a_hbm, a_buf, a_sem)]
     loads += [pltpu.make_async_copy(wq_hbm.at[pl.ds(idx * chunk_rows, chunk_rows)], wq_buf.at[idx], wq_sem.at[idx]) for idx in range(chunks)]
-    for copy in loads:
+    wo_copy = pltpu.make_async_copy(wo_hbm, wo_ref, wo_sem)
+    for copy in loads + [wo_copy]:
         copy.start()
 
     bases = (me * piece, (2 * cp_size - 1 - me) * piece)
@@ -248,93 +251,96 @@
     tok = jnp.concatenate([lane_tok] * (LANES // piece), axis=1)
     key_row = lax.broadcasted_iota(jnp.int32, (piece, LANES), 0)
 
-    def queries_and_diagonal():
-        for copy in loads:
-            copy.wait()
-        for col in range(wq_buf.shape[2] // COLS):
+    n_blocks = wq_buf.shape[2] // COLS
+
+    def queries(part):
+        if part == 0:
+            for copy in loads:
+                copy.wait()
+        for col in range(part * n_blocks // 2, (part + 1) * n_blocks // 2):
             q_raw = fdot(a_buf[...], jnp.concatenate([wq_buf[idx, :, col * COLS:(col + 1) * COLS] for idx in range(chunks)], axis=0))
             for sub in range(COLS // HEAD_DIM):
                 head = col * (COLS // HEAD_DIM) + sub
                 q_rot = rope(q_raw[:, sub * HEAD_DIM:(sub + 1) * HEAD_DIM], cos_ref[...], sin_ref[...])
                 for half in range(2):
                     qt_ref[half, :, head * piece:(head + 1) * piece] = q_rot[half * piece:(half + 1) * piece].T.astype(BF16)
-        for half in range(2):
-            visible = (key_row <= tok) & (key_row + bases[half] >= first_key[half])
-
-            @pl.loop(0, tiles)
-            def _(tile):
-                cols = pl.ds(pl.multiple_of(tile * LANES, LANES), LANES)
-                scores = fdot(kv_ref[half], qt_ref[half, :, cols])
-                scores = jnp.where(visible, scores, NEG_BIG)
-                top = jnp.max(scores, axis=0, keepdims=True)
-                prob = jnp.exp2((scores - top) * SCORE_LOG2)
-                max_ref[half, :, cols] = top
-                sum_ref[half, :, cols] = jnp.sum(prob, axis=0, keepdims=True)
-                acc_ref[half, :, cols] = fdot(kv_ref[2 + half], prob.astype(BF16))
-
-    def low_tile(owners, cols):
-        keys = jnp.concatenate([all_ref[own, 0] for own in owners], axis=0)
-        vals = jnp.concatenate([all_ref[own, 2] for own in owners], axis=1)
-        raw = fdot(keys, qt_ref[1, :, cols])
-        peak = None
-        for sub, own in enumerate(owners):
-            rows = slice(sub * piece, (sub + 1) * piece)
-            score = jnp.where(key_row < first_key[1] - own * piece, NEG_BIG, raw[rows])
-            score_ref[rows] = score
-            best = jnp.max(score, axis=0, keepdims=True)
-            peak = best if peak is None else jnp.maximum(peak, best)
-        old_top = max_ref[1, :, cols]
-        top = jnp.maximum(old_top, peak)
-        scale = jnp.exp2((old_top - top) * SCORE_LOG2)
-        prob = jnp.exp2((score_ref[...] - top) * SCORE_LOG2)
-        max_ref[1, :, cols] = top
-        sum_ref[1, :, cols] = sum_ref[1, :, cols] * scale + jnp.sum(prob, axis=0, keepdims=True)
-        acc_ref[1, :, cols] = acc_ref[1, :, cols] * scale + fdot(vals, prob.astype(BF16))
-
-    def side_tile(own, cols):
-        half = (own - me + cp_size) // cp_size
-        base = (own + half * (2 * cp_size - 1 - 2 * own)) * piece
-        hidden = key_row < jnp.where(half == 0, first_key[0], first_key[1]) - base
-        score = jnp.where(hidden, NEG_BIG, fdot(all_ref[own, half], qt_ref[half, :, cols]))
-        old_top = max_ref[half, :, cols]
-        top = jnp.maximum(old_top, jnp.max(score, axis=0, keepdims=True))
-        prob = jnp.exp2((score - top) * SCORE_LOG2)
-        scale = jnp.exp2((old_top - top) * SCORE_LOG2)
-        max_ref[half, :, cols] = top
-        sum_ref[half, :, cols] = sum_ref[half, :, cols] * scale + jnp.sum(prob, axis=0, keepdims=True)
-        acc_ref[half, :, cols] = acc_ref[half, :, cols] * scale + fdot(all_ref[own, 2 + half], prob.astype(BF16))
-
-    def on_group(*owners):
-        @pl.loop(0, tiles)
-        def _(tile):
-            cols = pl.ds(pl.multiple_of(tile * LANES, LANES), LANES)
-            low_tile(owners, cols)
-            for own in owners:
-                if own is not me:
-                    side_tile(own, cols)
-
-    gather_shards(place, kv_ref, all_ref, send_sem, recv_sem, queries_and_diagonal, on_group)
+        if part == 1:
+            for half in range(2):
+                visible = (key_row <= tok) & (key_row + bases[half] >= first_key[half])
+                for tile in range(tiles):
+                    cols = slice(tile * LANES, (tile + 1) * LANES)
+                    scores = fdot(kv_ref[half], qt_ref[half, :, cols])
+                    scores = jnp.where(visible, scores, NEG_BIG)
+                    top = jnp.max(scores, axis=0, keepdims=True)
+                    prob = jnp.exp2((scores - top) * SCORE_LOG2)
+                    max_ref[half, :, cols] = top
+                    sum_ref[half, :, cols] = jnp.sum(prob, axis=0, keepdims=True)
+                    acc_ref[half, :, cols] = fdot(kv_ref[2 + half], prob.astype(BF16))
+
+    def block(half, part, owners, key_base):
+        keys = jnp.concatenate([all_ref[own, part] for own in owners], axis=0)
+        vals = jnp.concatenate([all_ref[own, 2 + part] for own in owners], axis=1)
+        hidden = [key_row < first_key[half] - base for base in key_base]
+        tops, scales = [], []
+        for tile in range(tiles):
+            cols = slice(tile * LANES, (tile + 1) * LANES)
+            raw = fdot(keys, qt_ref[half, :, cols])
+            peak = None
+            for sub in range(OWNERS):
+                rows = slice(sub * piece, (sub + 1) * piece)
+                score = jnp.where(hidden[sub], NEG_BIG, raw[rows])
+                score_ref[rows, cols] = score
+                best = jnp.max(score, axis=0, keepdims=True)
+                peak = best if peak is None else jnp.maximum(peak, best)
+            old_top = max_ref[half, :, cols]
+            top = jnp.maximum(old_top, peak)
+            max_ref[half, :, cols] = top
+            tops.append(top)
+            scales.append(jnp.exp2((old_top - top) * SCORE_LOG2))
+        for tile in range(tiles):
+            cols = slice(tile * LANES, (tile + 1) * LANES)
+            prob = jnp.exp2((score_ref[:, cols] - tops[tile]) * SCORE_LOG2)
+            sum_ref[half, :, cols] = sum_ref[half, :, cols] * scales[tile] + jnp.sum(prob, axis=0, keepdims=True)
+            acc_ref[half, :, cols] = acc_ref[half, :, cols] * scales[tile] + fdot(vals, prob.astype(BF16))
+
+    def low_group(*owners):
+        block(1, 0, owners, [own * piece for own in owners])
+
+    gather_shards(place, kv_ref, all_ref, send_sem, recv_sem, queries, low_group)
+
+    @pl.loop(0, (me + OWNERS - 1) // OWNERS)
+    def _(idx):
+        owners = [idx * OWNERS + sub for sub in range(OWNERS)]
+        block(0, 0, owners, [jnp.where(own < me, own * piece, -2 * piece) for own in owners])
+
+    @pl.loop((me + 1) // OWNERS, cp_size // OWNERS)
+    def _(idx):
+        owners = [idx * OWNERS + sub for sub in range(OWNERS)]
+        block(1, 1, owners, [jnp.where(own > me, (2 * cp_size - 1 - own) * piece, -2 * piece) for own in owners])
 
     for half in range(2):
         for head in range(width // piece):
             cols = slice(head * piece, (head + 1) * piece)
             done = acc_ref[half, :, cols] / sum_ref[half, :, cols]
             out_ref[half * piece:(half + 1) * piece, head * HEAD_DIM:(head + 1) * HEAD_DIM] = done.T.astype(BF16)
-
-
-def finish_kernel(x_hbm, attn_ref, gain_ref, wo_hbm, wg_hbm, wu_hbm, wd_hbm, z_hbm, h_buf, b_buf, m_buf, acc_ref, z_buf, slots, x_sem, slot_sem, z_sem):
+    wo_copy.wait()
+
+
+def finish_kernel(x_hbm, attn_ref, gain_ref, wo_ref, wg_hbm, wu_hbm, wd_hbm, z_hbm, h_buf, b_buf, m_buf, acc_ref, z_buf, slots, x_sem, slot_sem, z_sem):
     count, depth = h_buf.shape
     ff = wg_hbm.shape[1]
     ff_half = ff // 2
-    group = 4
+    group = 2
     n_wo = depth // SLOT_COLS
     k_steps = depth // (SLOT_ROWS * group)
     n_ff = 4 * k_steps
+    dn_cols = SLOT_COLS // 2
     dn_rows = [min(SLOT_ROWS, ff - row) for row in range(0, ff, SLOT_ROWS)]
-    n_dn = depth // SLOT_COLS
-    ff_from = n_wo
+    dn_slots = [dn_rows[idx:idx + 2] for idx in range(0, len(dn_rows), 2)]
+    n_dn = depth // dn_cols
+    ff_from = 0
     dn_from = ff_from + n_ff * group
-    total = dn_from + n_dn * len(dn_rows)
+    total = dn_from + n_dn * len(dn_slots)
 
     def cols_of(idx, size):
         return pl.ds(pl.multiple_of(idx * size, size), size)
@@ -348,10 +354,6 @@
         slot = lax.rem(num, SLOTS)
         sem = slot_sem.at[slot]
         dst = slots.at[slot]
-
-        @pl.when(num < ff_from)
-        def _():
-            halves(wo_hbm.at[:, cols_of(num, SLOT_COLS)], dst, SLOT_ROWS, sem)
 
         rel = num - ff_from
         step = rel // group
@@ -369,11 +371,12 @@
             halves(wu_hbm.at[row, cols_of(half, ff_half)], dst.at[:, pl.ds(0, ff_half)], SLOT_ROWS, sem)
 
         rel = num - dn_from
-        for idx, rows in enumerate(dn_rows):
-            @pl.when((num >= dn_from) & (num < total) & (lax.rem(rel, len(dn_rows)) == idx))
+        for idx, pair in enumerate(dn_slots):
+            @pl.when((num >= dn_from) & (num < total) & (lax.rem(rel, len(dn_slots)) == idx))
             def _():
-                src = wd_hbm.at[pl.ds(idx * SLOT_ROWS, rows), cols_of(rel // len(dn_rows), SLOT_COLS)]
-                halves(src, dst.at[pl.ds(0, rows)], rows, sem)
+                for side, rows in enumerate(pair):
+                    src = wd_hbm.at[pl.ds((2 * idx + side) * SLOT_ROWS, rows), cols_of(rel // len(dn_slots), dn_cols)]
+                    pltpu.make_async_copy(src, dst.at[pl.ds(0, rows), pl.ds(side * dn_cols, dn_cols)], sem).start(priority=side)
 
     def take(num, rows, cols):
         slot = lax.rem(num, SLOTS)
@@ -389,12 +392,10 @@
 
     @pl.loop(0, n_wo)
     def _(num):
-        slot = take(num, SLOT_ROWS, SLOT_COLS)
         for sub in range(0, SLOT_COLS, COLS):
             cols = pl.ds(pl.multiple_of(num * SLOT_COLS + sub, COLS), COLS)
-            out = fdot(attn_ref[...], slot[:, sub:sub + COLS])
+            out = fdot(attn_ref[...], wo_ref[:, cols])
             h_buf[:, cols] = (h_buf[:, cols].astype(F32) + out).astype(BF16)
-        issue(num + SLOTS)
 
     @pl.loop(0, count // 32)
     def _(idx):
@@ -425,27 +426,37 @@
 
     def z_copy(blk):
         slot = lax.rem(blk, 2)
-        return pltpu.make_async_copy(z_buf.at[slot], z_hbm.at[:, cols_of(blk, SLOT_COLS)], z_sem.at[slot])
+        return pltpu.make_async_copy(z_buf.at[slot], z_hbm.at[:, cols_of(blk, dn_cols)], z_sem.at[slot])
 
     @pl.loop(0, n_dn)
     def _(blk):
-        num = dn_from + blk * len(dn_rows)
-        parts = [take(num + idx, rows, SLOT_COLS) for idx, rows in enumerate(dn_rows)]
+        num = dn_from + blk * len(dn_slots)
+        parts = []
+        for idx, pair in enumerate(dn_slots):
+            slot = lax.rem(num + idx, SLOTS)
+            for side, rows in enumerate(pair):
+                part = slots.at[slot, pl.ds(0, rows), pl.ds(side * dn_cols, dn_cols)]
+                pltpu.make_async_copy(part, part, slot_sem.at[slot]).wait()
+                parts.append(part)
 
         @pl.when(blk >= 2)
         def _():
             z_copy(blk - 2).wait()
 
-        for sub in range(0, SLOT_COLS, COLS):
-            cols = pl.ds(pl.multiple_of(blk * SLOT_COLS + sub, COLS), COLS)
-            out = fdot(m_buf[...], jnp.concatenate([part[:rows, sub:sub + COLS] for part, rows in zip(parts, dn_rows)], axis=0))
+        for sub in range(0, dn_cols, COLS):
+            cols = pl.ds(pl.multiple_of(blk * dn_cols + sub, COLS), COLS)
+            out = fdot(m_buf[...], jnp.concatenate([part[:, sub:sub + COLS] for part in parts], axis=0))
             z_buf[lax.rem(blk, 2), :, sub:sub + COLS] = (h_buf[:, cols].astype(F32) + out).astype(BF16)
         z_copy(blk).start()
-        for idx in range(len(dn_rows)):
+        for idx in range(len(dn_slots)):
             issue(num + idx + SLOTS)
 
     for blk in range(max(0, n_dn - 2), n_dn):
         z_copy(blk).wait()
+
+
+def in_vmem(array):
+    return pltpu.with_memory_space_constraint(array, pltpu.VMEM)
 
 
 def solution(mesh):
@@ -468,33 +479,33 @@
         blocks = count // 32
         table = jax.ShapeDtypeStruct((count, HEAD_DIM), F32)
         cache = jax.ShapeDtypeStruct((count, HEAD_DIM), BF16)
-        a_rows, cos_t, sin_t, kv, k_rows, v_rows = pl.pallas_call(
+        a_rows, cos_t, sin_t, kv, pos_v, k_rows, v_rows = pl.pallas_call(
             project_kernel,
-            out_shape=(jax.ShapeDtypeStruct((count, depth), BF16), table, table, jax.ShapeDtypeStruct((4, piece, HEAD_DIM), BF16), cache, cache),
+            out_shape=(jax.ShapeDtypeStruct((count, depth), BF16), table, table, jax.ShapeDtypeStruct((4, piece, HEAD_DIM), BF16), jax.ShapeDtypeStruct((2, 1, piece), jnp.int32), cache, cache),
             in_specs=[hbm, vmem, vmem, vmem, hbm, hbm],
-            out_specs=(hbm, vmem, vmem, vmem, vmem, vmem),
+            out_specs=(hbm, vmem, vmem, vmem, vmem, vmem, vmem),
             scratch_shapes=[pltpu.VMEM((count, depth), BF16), pltpu.VMEM((count, depth), BF16), pltpu.VMEM((depth, HEAD_DIM), BF16), pltpu.VMEM((depth, HEAD_DIM), BF16), dma((blocks,)), dma((2,)), dma((blocks,))],
-            compiler_params=pltpu.CompilerParams(vmem_limit_bytes=limit),
+            compiler_params=pltpu.CompilerParams(vmem_limit_bytes=24 * 1024 * 1024),
             name='project',
         )(rows, attn_gain, pos3, freqs, w_k, w_v)
-        attn_rows = pl.pallas_call(
+        attn_rows, wo_near = pl.pallas_call(
             functools.partial(attend_kernel, cp_size, side),
-            out_shape=jax.ShapeDtypeStruct((count, w_q.shape[1]), BF16),
-            in_specs=[vmem, vmem, vmem, vmem, hbm, hbm],
-            out_specs=vmem,
-            scratch_shapes=[pltpu.VMEM((count, depth), BF16), pltpu.VMEM((chunks, SLOT_ROWS, w_q.shape[1]), BF16), pltpu.VMEM((2, HEAD_DIM, width), BF16), pltpu.VMEM((cp_size, 4, piece, HEAD_DIM), BF16), pltpu.VMEM((2, 1, width), F32), pltpu.VMEM((2, 1, width), F32), pltpu.VMEM((2, HEAD_DIM, width), F32), pltpu.VMEM((OWNERS * piece, LANES), F32), dma(()), dma((chunks,)), dma((NUM_COPIES,)), dma((NUM_COPIES,))],
-            compiler_params=pltpu.CompilerParams(vmem_limit_bytes=limit, collective_id=0, has_side_effects=True),
+            out_shape=(jax.ShapeDtypeStruct((count, w_q.shape[1]), BF16), jax.ShapeDtypeStruct(w_o.shape, BF16)),
+            in_specs=[vmem, vmem, vmem, vmem, hbm, hbm, hbm],
+            out_specs=(vmem, vmem),
+            scratch_shapes=[pltpu.VMEM((count, depth), BF16), pltpu.VMEM((chunks, SLOT_ROWS, w_q.shape[1]), BF16), pltpu.VMEM((2, HEAD_DIM, width), BF16), pltpu.VMEM((cp_size, 4, piece, HEAD_DIM), BF16), pltpu.VMEM((2, 1, width), F32), pltpu.VMEM((2, 1, width), F32), pltpu.VMEM((2, HEAD_DIM, width), F32), pltpu.VMEM((OWNERS * piece, width), F32), dma(()), dma((chunks,)), dma(()), dma((NUM_COPIES,)), dma((NUM_COPIES,))],
+            compiler_params=pltpu.CompilerParams(vmem_limit_bytes=36 * 1024 * 1024, collective_id=0, has_side_effects=True),
             name='attend',
-        )(kv, pos3, cos_t, sin_t, a_rows, w_q)
+        )(in_vmem(kv), in_vmem(pos_v), in_vmem(cos_t), in_vmem(sin_t), pltpu.with_memory_space_constraint(a_rows, pltpu.HBM), pltpu.with_memory_space_constraint(w_q, pltpu.HBM), pltpu.with_memory_space_constraint(w_o, pltpu.HBM))
         z_rows = pl.pallas_call(
             finish_kernel,
             out_shape=jax.ShapeDtypeStruct((count, depth), BF16),
-            in_specs=[hbm, vmem, vmem, hbm, hbm, hbm, hbm],
+            in_specs=[hbm, vmem, vmem, vmem, hbm, hbm, hbm],
             out_specs=hbm,
-            scratch_shapes=[pltpu.VMEM((count, depth), BF16), pltpu.VMEM((count, depth), BF16), pltpu.VMEM((count, ff), BF16), pltpu.VMEM((2, count, ff // 2), F32), pltpu.VMEM((2, count, SLOT_COLS), BF16), pltpu.VMEM((SLOTS, SLOT_ROWS, SLOT_COLS), BF16), dma(()), dma((SLOTS,)), dma((2,))],
-            compiler_params=pltpu.CompilerParams(vmem_limit_bytes=limit),
+            scratch_shapes=[pltpu.VMEM((count, depth), BF16), pltpu.VMEM((count, depth), BF16), pltpu.VMEM((count, ff), BF16), pltpu.VMEM((2, count, ff // 2), F32), pltpu.VMEM((2, count, SLOT_COLS // 2), BF16), pltpu.VMEM((SLOTS, SLOT_ROWS, SLOT_COLS), BF16), dma(()), dma((SLOTS,)), dma((2,))],
+            compiler_params=pltpu.CompilerParams(vmem_limit_bytes=42 * 1024 * 1024),
             name='finish',
-        )(rows, attn_rows, mlp_gain, w_o, w_gate, w_up, w_down)
+        )(rows, in_vmem(attn_rows), mlp_gain, in_vmem(wo_near), w_gate, w_up, w_down)
         return z_rows[None], k_rows[:, None, :], v_rows[:, None, :]
 
     seq_spec = P(('dp', 'cp'))

time: 128 us -> 120 us (0.938)
  Pallas kernels: 127 us -> 109 us
  local copies, waits for them, and re-layouts: 0 us -> 9.52 us
    pallas_call x1, Pallas kernels: 47.5 us -> 36 us  [device_fn(): pl.pallas_call(functools.partial(attend_kernel, cp_size, side), out_shape...]
    unnamed x0 -> x14, local copies, waits for them, and re-layouts: none -> 9.52 us
    pallas_call x1, Pallas kernels: 71.7 us -> 66.9 us  [device_fn(): pl.pallas_call(finish_kernel, out_shape=jax.ShapeDtypeStruct((count, dept...]
    pallas_call x1, Pallas kernels: 8.11 us -> 5.96 us  [device_fn(): pl.pallas_call(project_kernel, out_shape=(jax.ShapeDtypeStruct((count, de...]
where the time goes in v5:
time: 120 us; the launch traced here: 119 us
  Pallas kernels  109 us (91%)
  local copies, waits for them, and re-layouts  9.52 us (8%)
    pallas_call x1, Pallas kernels, device_fn(): pl.pallas_call(finish_kernel, out_shape=jax.ShapeDtypeStruct((count, dept...  66.9 us
    pallas_call x1, Pallas kernels, device_fn(): pl.pallas_call(functools.partial(attend_kernel, cp_size, side), out_shape...  36 us
    unnamed x14, local copies, waits for them, and re-layouts  9.52 us
    pallas_call x1, Pallas kernels, device_fn(): pl.pallas_call(project_kernel, out_shape=(jax.ShapeDtypeStruct((count, de...  5.96 us

profile of v5, /device:TPU:97, one launch (start us, length us, event | category | flops | bytes accessed | tf_op | source)
XLA Modules:
  0.0 119.3 jit_solution(12134384134636249551)
XLA Ops:
  0.6 0.0 copy-start
  0.6 2.2 %copy-done = bf16[1,256,8192]{2,1,0:T(8,128)(2,1)S(1)} copy-done((bf16[1,256,8192]{2,1,0:T(8,128)(2,1)S(1)}, bf16[1,256,8192]{2,1,0:T(8,128)(2,1)}, u32[]{:S(2)}) %copy-start) | copy-done | bytes 4194328
  2.8 0.0 copy-start.2
  2.8 1.6 %copy-done.2 = bf16[8192,128]{1,0:T(8,128)(2,1)S(1)} copy-done((bf16[8192,128]{1,0:T(8,128)(2,1)S(1)}, bf16[8192,128]{1,0:T(8,128)(2,1)}, u32[]{:S(2)}) %copy-start.2) | copy-done | bytes 2097176
  4.4 0.0 copy-start.3
  4.4 1.6 %copy-done.3 = bf16[8192,128]{1,0:T(8,128)(2,1)S(1)} copy-done((bf16[8192,128]{1,0:T(8,128)(2,1)S(1)}, bf16[8192,128]{1,0:T(8,128)(2,1)}, u32[]{:S(2)}) %copy-start.3) | copy-done | bytes 2097176
  6.0 0.0 copy-start.4
  6.0 0.8 copy-done.4
  6.8 0.0 copy-start.5
  6.8 0.7 copy-done.5
  7.5 0.0 copy-start.6
  7.5 0.7 copy-done.6
  8.2 6.0 %project.1 = (bf16[256,8192]{1,0:T(8,128)(2,1)S(1)}, f32[256,128]{1,0:T(8,128)S(1)}, f32[256,128]{1,0:T(8,128)S(1)}, bf16[4,128,128]{2,1,0:T(8,128)(2,1)S(1)}, s...) custom-call(bf16[256,8192]{1,0:T(8,128)(2,1)S(1)} %bitcast.6, ...), custom_call_target="tpu_custom_call" | custom-call | tf_op jit(solution)/shard_map/project/pallas_call | solution.py:482
  14.1 0.0 copy-start.1
  14.1 2.0 %copy-done.1 = bf16[256,8192]{1,0:T(8,128)(2,1)} copy-done((bf16[256,8192]{1,0:T(8,128)(2,1)}, bf16[256,8192]{1,0:T(8,128)(2,1)S(1)}, u32[]{:S(2)}) %copy-start.1) | copy-done | bytes 4194328
  16.1 36.0 %attend.1 = (bf16[256,1024]{1,0:T(8,128)(2,1)S(1)}, bf16[1024,8192]{1,0:T(8,128)(2,1)S(1)}) custom-call(bf16[4,128,128]{2,1,0:T(8,128)(2,1)S(1)} %get-tuple-element.12.kv_ref, s32[2,1,128]{2,1,0:T(1,128)S(1)} %get-tuple-element.13.pos_ref, f32[256,128]{1,0:T(8,128)S(1)} %get-tuple-element.14.cos_ref, f32[256,128]{1,0:T(8,128)S(1)} %get-tuple-element.15.sin_ref, ...), custom_call_target="tpu_custom_call" | custom-call | tf_op jit(solution)/shard_map/attend/pallas_call | solution.py:491
  52.2 66.9 %finish.1 = bf16[256,8192]{1,0:T(8,128)(2,1)} custom-call(bf16[256,8192]{1,0:T(8,128)(2,1)} %bitcast.5, bf16[256,1024]{1,0:T(8,128)(2,1)S(1)} %get-tuple-element.17.attn_ref, bf16[8192]{0:T(1024)(128)(2,1)} %gain_ref.3, bf16[1024,8192]{1,0:T(8,128)(2,1)S(1)} %get-tuple-element.18.wo_ref, bf16[8192,3584]{1,0:T(8,128)(2,1)} %wg_hbm.1, ...), custom_call_target="tpu_custom_call" | custom-call | tf_op jit(solution)/shard_map/finish/pallas_call | solution.py:500
Async XLA Ops:
  0.6 2.2 %copy-start = (bf16[1,256,8192]{2,1,0:T(8,128)(2,1)S(1)}, bf16[1,256,8192]{2,1,0:T(8,128)(2,1)}, u32[]{:S(2)}) copy-start(bf16[1,256,8192]{2,1,0:T(8,128)(2,1)} %param.13) | copy-start | bytes 12582916
  2.8 1.6 %copy-start.2 = (bf16[8192,128]{1,0:T(8,128)(2,1)S(1)}, bf16[8192,128]{1,0:T(8,128)(2,1)}, u32[]{:S(2)}) copy-start(bf16[8192,128]{1,0:T(8,128)(2,1)} %wk_hbm.1) | copy-start | bytes 6291460
  4.4 1.6 %copy-start.3 = (bf16[8192,128]{1,0:T(8,128)(2,1)S(1)}, bf16[8192,128]{1,0:T(8,128)(2,1)}, u32[]{:S(2)}) copy-start(bf16[8192,128]{1,0:T(8,128)(2,1)} %wv_hbm.1) | copy-start | bytes 6291460
  6.0 0.8 copy-start.4
  6.8 0.7 copy-start.5
  7.5 0.7 copy-start.6
  14.1 2.0 %copy-start.1 = (bf16[256,8192]{1,0:T(8,128)(2,1)}, bf16[256,8192]{1,0:T(8,128)(2,1)S(1)}, u32[]{:S(2)}) copy-start(bf16[256,8192]{1,0:T(8,128)(2,1)S(1)} %get-tuple-element.16.a_hbm) | copy-start | bytes 12582916

commit v6 on v5

--- a/solution.py
+++ b/solution.py
@@ -55,7 +55,7 @@
         dst_ref[rows, col:col + 512] = (part * inv_rms * gain).astype(BF16)
 
 
-def project_kernel(x_hbm, gain_ref, pos_ref, freq_ref, wk_hbm, wv_hbm, a_hbm, cos_ref, sin_ref, kv_ref, pos_out, kc_ref, vc_ref, x_buf, a_buf, wk_buf, wv_buf, x_sem, wkv_sem, a_sem):
+def project_kernel(x_hbm, gain_ref, pos_ref, freq_ref, wk_hbm, wv_hbm, a_buf, cos_ref, sin_ref, kv_ref, pos_out, kc_ref, vc_ref, x_buf, wk_buf, wv_buf, x_sem, wkv_sem):
     count = x_buf.shape[0]
     piece = count // 2
     blocks = x_sem.shape[0]
@@ -64,10 +64,6 @@
     def x_copy(idx):
         rows = pl.ds(idx * rows_blk, rows_blk)
         return pltpu.make_async_copy(x_hbm.at[rows], x_buf.at[rows], x_sem.at[idx])
-
-    def a_copy(idx):
-        rows = pl.ds(idx * rows_blk, rows_blk)
-        return pltpu.make_async_copy(a_buf.at[rows], a_hbm.at[rows], a_sem.at[idx])
 
     for idx in range(blocks):
         x_copy(idx).start()
@@ -87,7 +83,6 @@
     def _(idx):
         x_copy(idx).wait()
         norm_rows(x_buf, a_buf, gain_ref, pl.multiple_of(idx * rows_blk, rows_blk), rows_blk)
-        a_copy(idx).start()
 
     for copy in wkv:
         copy.wait()
@@ -100,8 +95,6 @@
         rows = slice(half * piece, (half + 1) * piece)
         kv_ref[half] = k_rot[rows].astype(BF16)
         kv_ref[2 + half] = v_raw[rows].T.astype(BF16)
-    for idx in range(blocks):
-        a_copy(idx).wait()
 
 
 def rope(raw, cos_t, sin_t):
@@ -198,9 +191,9 @@
     on_start(1)
     far_left = relay(-1, row_left)
     far_right = relay(1, row_right)
+    close(0, far_own)
     arrived(0)
     on_group(me, sibling, owner(-1, 0), owner(1, 0))
-    close(0, far_own)
     far_far = relay(2, row_far)
     arrived(1, 2)
     on_group(owner(0, -1), owner(0, 1), other(-1, 0), other(1, 0))
@@ -226,7 +219,7 @@
 NUM_COPIES = 36
 
 
-def attend_kernel(cp_size, side, kv_ref, pos_ref, cos_ref, sin_ref, a_hbm, wq_hbm, wo_hbm, out_ref, wo_ref, a_buf, wq_buf, qt_ref, all_ref, max_ref, sum_ref, acc_ref, score_ref, a_sem, wq_sem, wo_sem, send_sem, recv_sem):
+def attend_kernel(cp_size, side, kv_ref, pos_ref, cos_ref, sin_ref, a_buf, wq_hbm, wo_hbm, out_ref, wo_ref, wq_buf, qt_ref, all_ref, max_ref, sum_ref, acc_ref, score_ref, wq_sem, wo_sem, send_sem, recv_sem):
     place = torus_place(side)
     me = place[0]
     count = a_buf.shape[0]
@@ -234,8 +227,7 @@
     width = qt_ref.shape[2]
     tiles = width // LANES
     chunks, chunk_rows = wq_buf.shape[:2]
-    loads = [pltpu.make_async_copy(a_hbm, a_buf, a_sem)]
-    loads += [pltpu.make_async_copy(wq_hbm.at[pl.ds(idx * chunk_rows, chunk_rows)], wq_buf.at[idx], wq_sem.at[idx]) for idx in range(chunks)]
+    loads = [pltpu.make_async_copy(wq_hbm.at[pl.ds(idx * chunk_rows, chunk_rows)], wq_buf.at[idx], wq_sem.at[idx]) for idx in range(chunks)]
     wo_copy = pltpu.make_async_copy(wo_hbm, wo_ref, wo_sem)
     for copy in loads + [wo_copy]:
         copy.start()
@@ -277,10 +269,15 @@
                     sum_ref[half, :, cols] = jnp.sum(prob, axis=0, keepdims=True)
                     acc_ref[half, :, cols] = fdot(kv_ref[2 + half], prob.astype(BF16))
 
-    def block(half, part, owners, key_base):
+    def block(half, part, owners):
+        start = jnp.where(half == 0, first_key[0], first_key[1])
+        hidden = []
+        for own in owners:
+            low_base = jnp.where((half == 1) | (own < me), own * piece, -2 * piece)
+            high_base = jnp.where(own > me, (2 * cp_size - 1 - own) * piece, -2 * piece)
+            hidden.append(key_row < start - jnp.where(part == 0, low_base, high_base))
         keys = jnp.concatenate([all_ref[own, part] for own in owners], axis=0)
         vals = jnp.concatenate([all_ref[own, 2 + part] for own in owners], axis=1)
-        hidden = [key_row < first_key[half] - base for base in key_base]
         tops, scales = [], []
         for tile in range(tiles):
             cols = slice(tile * LANES, (tile + 1) * LANES)
@@ -303,20 +300,12 @@
             sum_ref[half, :, cols] = sum_ref[half, :, cols] * scales[tile] + jnp.sum(prob, axis=0, keepdims=True)
             acc_ref[half, :, cols] = acc_ref[half, :, cols] * scales[tile] + fdot(vals, prob.astype(BF16))
 
-    def low_group(*owners):
-        block(1, 0, owners, [own * piece for own in owners])
-
-    gather_shards(place, kv_ref, all_ref, send_sem, recv_sem, queries, low_group)
-
-    @pl.loop(0, (me + OWNERS - 1) // OWNERS)
-    def _(idx):
-        owners = [idx * OWNERS + sub for sub in range(OWNERS)]
-        block(0, 0, owners, [jnp.where(own < me, own * piece, -2 * piece) for own in owners])
-
-    @pl.loop((me + 1) // OWNERS, cp_size // OWNERS)
-    def _(idx):
-        owners = [idx * OWNERS + sub for sub in range(OWNERS)]
-        block(1, 1, owners, [jnp.where(own > me, (2 * cp_size - 1 - own) * piece, -2 * piece) for own in owners])
+    def on_group(*owners):
+        @pl.loop(0, 3)
+        def _(which):
+            block((which + 1) // 2, which // 2, owners)
+
+    gather_shards(place, kv_ref, all_ref, send_sem, recv_sem, queries, on_group)
 
     for half in range(2):
         for head in range(width // piece):
@@ -453,6 +442,10 @@
 
     for blk in range(max(0, n_dn - 2), n_dn):
         z_copy(blk).wait()
+
+
+def in_hbm(array):
+    return pltpu.with_memory_space_constraint(array, pltpu.HBM)
 
 
 def in_vmem(array):
@@ -483,20 +476,20 @@
             project_kernel,
             out_shape=(jax.ShapeDtypeStruct((count, depth), BF16), table, table, jax.ShapeDtypeStruct((4, piece, HEAD_DIM), BF16), jax.ShapeDtypeStruct((2, 1, piece), jnp.int32), cache, cache),
             in_specs=[hbm, vmem, vmem, vmem, hbm, hbm],
-            out_specs=(hbm, vmem, vmem, vmem, vmem, vmem, vmem),
-            scratch_shapes=[pltpu.VMEM((count, depth), BF16), pltpu.VMEM((count, depth), BF16), pltpu.VMEM((depth, HEAD_DIM), BF16), pltpu.VMEM((depth, HEAD_DIM), BF16), dma((blocks,)), dma((2,)), dma((blocks,))],
+            out_specs=(vmem,) * 7,
+            scratch_shapes=[pltpu.VMEM((count, depth), BF16), pltpu.VMEM((depth, HEAD_DIM), BF16), pltpu.VMEM((depth, HEAD_DIM), BF16), dma((blocks,)), dma((2,))],
             compiler_params=pltpu.CompilerParams(vmem_limit_bytes=24 * 1024 * 1024),
             name='project',
-        )(rows, attn_gain, pos3, freqs, w_k, w_v)
+        )(in_hbm(rows), in_hbm(attn_gain), in_hbm(pos3), in_hbm(freqs), in_hbm(w_k), in_hbm(w_v))
         attn_rows, wo_near = pl.pallas_call(
             functools.partial(attend_kernel, cp_size, side),
             out_shape=(jax.ShapeDtypeStruct((count, w_q.shape[1]), BF16), jax.ShapeDtypeStruct(w_o.shape, BF16)),
-            in_specs=[vmem, vmem, vmem, vmem, hbm, hbm, hbm],
+            in_specs=[vmem, vmem, vmem, vmem, vmem, hbm, hbm],
             out_specs=(vmem, vmem),
-            scratch_shapes=[pltpu.VMEM((count, depth), BF16), pltpu.VMEM((chunks, SLOT_ROWS, w_q.shape[1]), BF16), pltpu.VMEM((2, HEAD_DIM, width), BF16), pltpu.VMEM((cp_size, 4, piece, HEAD_DIM), BF16), pltpu.VMEM((2, 1, width), F32), pltpu.VMEM((2, 1, width), F32), pltpu.VMEM((2, HEAD_DIM, width), F32), pltpu.VMEM((OWNERS * piece, width), F32), dma(()), dma((chunks,)), dma(()), dma((NUM_COPIES,)), dma((NUM_COPIES,))],
-            compiler_params=pltpu.CompilerParams(vmem_limit_bytes=36 * 1024 * 1024, collective_id=0, has_side_effects=True),
+            scratch_shapes=[pltpu.VMEM((chunks, SLOT_ROWS, w_q.shape[1]), BF16), pltpu.VMEM((2, HEAD_DIM, width), BF16), pltpu.VMEM((cp_size, 4, piece, HEAD_DIM), BF16), pltpu.VMEM((2, 1, width), F32), pltpu.VMEM((2, 1, width), F32), pltpu.VMEM((2, HEAD_DIM, width), F32), pltpu.VMEM((OWNERS * piece, width), F32), dma((chunks,)), dma(()), dma((NUM_COPIES,)), dma((NUM_COPIES,))],
+            compiler_params=pltpu.CompilerParams(vmem_limit_bytes=28 * 1024 * 1024, collective_id=0, has_side_effects=True),
             name='attend',
-        )(in_vmem(kv), in_vmem(pos_v), in_vmem(cos_t), in_vmem(sin_t), pltpu.with_memory_space_constraint(a_rows, pltpu.HBM), pltpu.with_memory_space_constraint(w_q, pltpu.HBM), pltpu.with_memory_space_constraint(w_o, pltpu.HBM))
+        )(in_vmem(kv), in_vmem(pos_v), in_vmem(cos_t), in_vmem(sin_t), in_vmem(a_rows), in_hbm(w_q), in_hbm(w_o))
         z_rows = pl.pallas_call(
             finish_kernel,
             out_shape=jax.ShapeDtypeStruct((count, depth), BF16),
@@ -505,7 +498,7 @@
             scratch_shapes=[pltpu.VMEM((count, depth), BF16), pltpu.VMEM((count, depth), BF16), pltpu.VMEM((count, ff), BF16), pltpu.VMEM((2, count, ff // 2), F32), pltpu.VMEM((2, count, SLOT_COLS // 2), BF16), pltpu.VMEM((SLOTS, SLOT_ROWS, SLOT_COLS), BF16), dma(()), dma((SLOTS,)), dma((2,))],
             compiler_params=pltpu.CompilerParams(vmem_limit_bytes=42 * 1024 * 1024),
             name='finish',
-        )(rows, in_vmem(attn_rows), mlp_gain, in_vmem(wo_near), w_gate, w_up, w_down)
+        )(in_hbm(rows), in_vmem(attn_rows), in_hbm(mlp_gain), in_vmem(wo_near), w_gate, w_up, w_down)
         return z_rows[None], k_rows[:, None, :], v_rows[:, None, :]
 
     seq_spec = P(('dp', 'cp'))

time: 120 us -> 116 us (0.967)
  local copies, waits for them, and re-layouts: 9.52 us -> 0 us
  Pallas kernels: 109 us -> 115 us
    unnamed x14 -> x0, local copies, waits for them, and re-layouts: 9.52 us -> none
    pallas_call x1, Pallas kernels: 36 us -> 41.8 us  [device_fn(): pl.pallas_call(functools.partial(attend_kernel, cp_size, side), out_shape...]
where the time goes in v6:
time: 116 us
  Pallas kernels  115 us (99%)
    pallas_call x1, Pallas kernels, device_fn(): pl.pallas_call(finish_kernel, out_shape=jax.ShapeDtypeStruct((count, dept...  66.9 us
    pallas_call x1, Pallas kernels, device_fn(): pl.pallas_call(functools.partial(attend_kernel, cp_size, side), out_shape...  41.8 us
    pallas_call x1, Pallas kernels, device_fn(): pl.pallas_call(project_kernel, out_shape=(jax.ShapeDtypeStruct((count, de...  6.37 us

profile of v6, /device:TPU:97, one launch (start us, length us, event | category | flops | bytes accessed | tf_op | source)
XLA Modules:
  0.0 115.9 jit_solution(6311718041311323991)
XLA Ops:
  0.6 6.4 %project.1 = (bf16[256,8192]{1,0:T(8,128)(2,1)S(1)}, f32[256,128]{1,0:T(8,128)S(1)}, f32[256,128]{1,0:T(8,128)S(1)}, bf16[4,128,128]{2,1,0:T(8,128)(2,1)S(1)}, s...) custom-call(bf16[256,8192]{1,0:T(8,128)(2,1)} %bitcast.5, bf16[8192]{0:T(1024)(128)(2,1)} %gain_ref.2, ...), custom_call_target="tpu_custom_call" | custom-call | tf_op jit(solution)/shard_map/project/pallas_call | solution.py:475
  7.0 41.8 %attend.1 = (bf16[256,1024]{1,0:T(8,128)(2,1)S(1)}, bf16[1024,8192]{1,0:T(8,128)(2,1)S(1)}) custom-call(bf16[4,128,128]{2,1,0:T(8,128)(2,1)S(1)} %get-tuple-element.12.kv_ref, s32[2,1,128]{2,1,0:T(1,128)S(1)} %get-tuple-element.13.pos_ref, f32[256,128]{1,0:T(8,128)S(1)} %get-tuple-element.14.cos_ref, f32[256,128]{1,0:T(8,128)S(1)} %get-tuple-element.15.sin_ref, ...), custom_call_target="tpu_custom_call" | custom-call | tf_op jit(solution)/shard_map/attend/pallas_call | solution.py:484
  48.8 66.9 %finish.1 = bf16[256,8192]{1,0:T(8,128)(2,1)} custom-call(bf16[256,8192]{1,0:T(8,128)(2,1)} %bitcast.6, bf16[256,1024]{1,0:T(8,128)(2,1)S(1)} %get-tuple-element.17.attn_ref, bf16[8192]{0:T(1024)(128)(2,1)} %gain_ref.3, bf16[1024,8192]{1,0:T(8,128)(2,1)S(1)} %get-tuple-element.18.wo_ref, bf16[8192,3584]{1,0:T(8,128)(2,1)} %wg_hbm.1, ...), custom_call_target="tpu_custom_call" | custom-call | tf_op jit(solution)/shard_map/finish/pallas_call | solution.py:493

commit v7 on v6

--- a/solution.py
+++ b/solution.py
@@ -191,9 +191,9 @@
     on_start(1)
     far_left = relay(-1, row_left)
     far_right = relay(1, row_right)
-    close(0, far_own)
     arrived(0)
     on_group(me, sibling, owner(-1, 0), owner(1, 0))
+    close(0, far_own)
     far_far = relay(2, row_far)
     arrived(1, 2)
     on_group(owner(0, -1), owner(0, 1), other(-1, 0), other(1, 0))
@@ -229,7 +229,7 @@
     chunks, chunk_rows = wq_buf.shape[:2]
     loads = [pltpu.make_async_copy(wq_hbm.at[pl.ds(idx * chunk_rows, chunk_rows)], wq_buf.at[idx], wq_sem.at[idx]) for idx in range(chunks)]
     wo_copy = pltpu.make_async_copy(wo_hbm, wo_ref, wo_sem)
-    for copy in loads + [wo_copy]:
+    for copy in loads:
         copy.start()
 
     bases = (me * piece, (2 * cp_size - 1 - me) * piece)
@@ -249,6 +249,7 @@
         if part == 0:
             for copy in loads:
                 copy.wait()
+            wo_copy.start()
         for col in range(part * n_blocks // 2, (part + 1) * n_blocks // 2):
             q_raw = fdot(a_buf[...], jnp.concatenate([wq_buf[idx, :, col * COLS:(col + 1) * COLS] for idx in range(chunks)], axis=0))
             for sub in range(COLS // HEAD_DIM):
@@ -269,15 +270,10 @@
                     sum_ref[half, :, cols] = jnp.sum(prob, axis=0, keepdims=True)
                     acc_ref[half, :, cols] = fdot(kv_ref[2 + half], prob.astype(BF16))
 
-    def block(half, part, owners):
-        start = jnp.where(half == 0, first_key[0], first_key[1])
-        hidden = []
-        for own in owners:
-            low_base = jnp.where((half == 1) | (own < me), own * piece, -2 * piece)
-            high_base = jnp.where(own > me, (2 * cp_size - 1 - own) * piece, -2 * piece)
-            hidden.append(key_row < start - jnp.where(part == 0, low_base, high_base))
+    def block(half, part, owners, key_base):
         keys = jnp.concatenate([all_ref[own, part] for own in owners], axis=0)
         vals = jnp.concatenate([all_ref[own, 2 + part] for own in owners], axis=1)
+        hidden = [key_row < first_key[half] - base for base in key_base]
         tops, scales = [], []
         for tile in range(tiles):
             cols = slice(tile * LANES, (tile + 1) * LANES)
@@ -300,12 +296,20 @@
             sum_ref[half, :, cols] = sum_ref[half, :, cols] * scales[tile] + jnp.sum(prob, axis=0, keepdims=True)
             acc_ref[half, :, cols] = acc_ref[half, :, cols] * scales[tile] + fdot(vals, prob.astype(BF16))
 
-    def on_group(*owners):
-        @pl.loop(0, 3)
-        def _(which):
-            block((which + 1) // 2, which // 2, owners)
-
-    gather_shards(place, kv_ref, all_ref, send_sem, recv_sem, queries, on_group)
+    def low_group(*owners):
+        block(1, 0, owners, [own * piece for own in owners])
+
+    gather_shards(place, kv_ref, all_ref, send_sem, recv_sem, queries, low_group)
+
+    @pl.loop(0, (me + OWNERS - 1) // OWNERS)
+    def _(idx):
+        owners = [idx * OWNERS + sub for sub in range(OWNERS)]
+        block(0, 0, owners, [jnp.where(own < me, own * piece, -2 * piece) for own in owners])
+
+    @pl.loop((me + 1) // OWNERS, cp_size // OWNERS)
+    def _(idx):
+        owners = [idx * OWNERS + sub for sub in range(OWNERS)]
+        block(1, 1, owners, [jnp.where(own > me, (2 * cp_size - 1 - own) * piece, -2 * piece) for own in owners])
 
     for half in range(2):
         for head in range(width // piece):

time: 116 us -> 111 us (0.957)
  Pallas kernels: 115 us -> 109 us
    pallas_call x1, Pallas kernels: 41.8 us -> 36.1 us  [device_fn(): pl.pallas_call(functools.partial(attend_kernel, cp_size, side), out_shape...]
where the time goes in v7:
time: 111 us; the launch traced here: 110 us
  Pallas kernels  109 us (98%)
    pallas_call x1, Pallas kernels, device_fn(): pl.pallas_call(finish_kernel, out_shape=jax.ShapeDtypeStruct((count, dept...  66.9 us
    pallas_call x1, Pallas kernels, device_fn(): pl.pallas_call(functools.partial(attend_kernel, cp_size, side), out_shape...  36.1 us
    pallas_call x1, Pallas kernels, device_fn(): pl.pallas_call(project_kernel, out_shape=(jax.ShapeDtypeStruct((count, de...  6.37 us

profile of v7, /device:TPU:97, one launch (start us, length us, event | category | flops | bytes accessed | tf_op | source)
XLA Modules:
  0.0 110.2 jit_solution(15707987557687611342)
XLA Ops:
  0.6 6.4 %project.1 = (bf16[256,8192]{1,0:T(8,128)(2,1)S(1)}, f32[256,128]{1,0:T(8,128)S(1)}, f32[256,128]{1,0:T(8,128)S(1)}, bf16[4,128,128]{2,1,0:T(8,128)(2,1)S(1)}, s...) custom-call(bf16[256,8192]{1,0:T(8,128)(2,1)} %bitcast.5, bf16[8192]{0:T(1024)(128)(2,1)} %gain_ref.2, ...), custom_call_target="tpu_custom_call" | custom-call | tf_op jit(solution)/shard_map/project/pallas_call | solution.py:479
  7.0 36.1 %attend.1 = (bf16[256,1024]{1,0:T(8,128)(2,1)S(1)}, bf16[1024,8192]{1,0:T(8,128)(2,1)S(1)}) custom-call(bf16[4,128,128]{2,1,0:T(8,128)(2,1)S(1)} %get-tuple-element.12.kv_ref, s32[2,1,128]{2,1,0:T(1,128)S(1)} %get-tuple-element.13.pos_ref, f32[256,128]{1,0:T(8,128)S(1)} %get-tuple-element.14.cos_ref, f32[256,128]{1,0:T(8,128)S(1)} %get-tuple-element.15.sin_ref, ...), custom_call_target="tpu_custom_call" | custom-call | tf_op jit(solution)/shard_map/attend/pallas_call | solution.py:488
  43.1 66.9 %finish.1 = bf16[256,8192]{1,0:T(8,128)(2,1)} custom-call(bf16[256,8192]{1,0:T(8,128)(2,1)} %bitcast.6, bf16[256,1024]{1,0:T(8,128)(2,1)S(1)} %get-tuple-element.17.attn_ref, bf16[8192]{0:T(1024)(128)(2,1)} %gain_ref.3, bf16[1024,8192]{1,0:T(8,128)(2,1)S(1)} %get-tuple-element.18.wo_ref, bf16[8192,3584]{1,0:T(8,128)(2,1)} %wg_hbm.1, ...), custom_call_target="tpu_custom_call" | custom-call | tf_op jit(solution)/shard_map/finish/pallas_call | solution.py:497
